TPU v7x, 32 devices: a whole 2x2x4 slice. The times are simulated.
32 devices in a mesh: aux: 16 (over z, x, core), pair: 2 (over y).
Axes of the slice: x: 2, y: 2, z: 4, core: 2. Of those that a mesh axis runs over, the one named last changes fastest.
Arguments:
- three_center: bfloat16 [128, 64, 1024], P('aux', 'pair'), may hold values from -6 to 6
- tile_live: int32 [16, 64], P('aux', 'pair'), may hold values from 0 to 1
- pair_atoms: int32 [64], replicated, may hold values from 0 to 63, each once
- green_occ: bfloat16 [256, 256], replicated, may hold values from -0.375 to 0.375
- green_vir: bfloat16 [256, 256], replicated, may hold values from -0.375 to 0.375
- screened: bfloat16 [128, 40], P('aux'), may hold values from -1 to 1
Outputs:
- polarizability: float32 [128, 40], P('aux', 'pair')
- self_energy: float32 [64, 1024], P('pair')
Inputs may be any that keep to these rules, and one draw needn't show every extreme that they name: `pair_atoms`: a permutation of the 64 atom pairs.
All inputs are finite; a program needn't handle non-finite values.
Results may differ from a plain program's by a relative error of at most 0.0043.
Values may be sent and summed in bfloat16 or wider, within the bound.
No kernel may reach another device: no remote copies, remote signals or barrier semaphores. Data moves between devices by JAX's collectives and lax.ppermute only.
A program may use at most 64 MiB of HBM per device.

v0:
```python
import math

import jax
import jax.numpy as jnp
from jax import lax
from jax.sharding import PartitionSpec as P

OA = 32
NAT = 8
REACH = 2


def shifted(value, axis, steps):
    count = lax.axis_size(axis)
    initial, last = (max(0, -steps), min(count, count - steps))
    return lax.ppermute(value, axis, [(source, source + steps) for source in range(initial, last)])


def tiles_to_matrix(tile_data, inverse):
    tile_rows = tile_data.shape[0]
    ordered = jnp.take(tile_data, inverse, axis=1)
    reshaped = ordered.reshape(tile_rows, NAT, NAT, OA, OA)
    return jnp.transpose(reshaped, (0, 1, 3, 2, 4)).reshape(tile_rows, NAT * OA, NAT * OA)


def matrix_to_tiles(matrix, pair_atoms):
    tile_rows = matrix.shape[0]
    reshaped = matrix.reshape(tile_rows, NAT, OA, NAT, OA)
    ordered = jnp.transpose(reshaped, (0, 1, 3, 2, 4)).reshape(tile_rows, NAT * NAT, OA * OA)
    return jnp.take(ordered, pair_atoms, axis=1)


def neighbor_window(masked):
    pieces = []
    for offset in range(-REACH, REACH + 1):
        if offset == 0:
            pieces.append(masked)
        else:
            pieces.append(shifted(masked, "aux", -offset))
    return jnp.concatenate(pieces, axis=0)


def row_groups(orbital_form, group_fn):
    row_count = orbital_form.shape[0]
    group_size = math.gcd(row_count, 8)
    grouped = orbital_form.reshape(row_count // group_size, group_size, NAT * OA, NAT * OA)
    result = lax.map(group_fn, grouped)
    return result.reshape((row_count,) + result.shape[2:])


def own_products(orbital_form, green_occ, green_vir, own_first, own_second):
    vir_cols = jnp.take(green_vir.reshape(NAT * OA, NAT, OA), own_second, axis=1)

    def group_fn(row_group):
        left_half = jnp.einsum(
            "lu,plm->pum", green_occ, row_group, preferred_element_type=jnp.float32
        ).astype(jnp.bfloat16)
        picked = jnp.take(
            left_half.reshape(row_group.shape[0], NAT, OA, NAT * OA), own_first, axis=1
        )
        return jnp.einsum(
            "pkum,mkv->pkuv", picked, vir_cols, preferred_element_type=jnp.float32
        ).astype(jnp.bfloat16)

    products = row_groups(orbital_form, group_fn)
    return products.reshape(products.shape[0], products.shape[1], OA * OA)


def energy_rows(mixed_tiles, occ_rows, orbital_form, tile_first):
    tile_rows, tile_count = (mixed_tiles.shape[0], mixed_tiles.shape[1])
    mixed_tiles = mixed_tiles.reshape(tile_rows, tile_count, OA, OA)
    scaled_rows = jnp.einsum(
        "qkml,kls->qkms", mixed_tiles, occ_rows, preferred_element_type=jnp.float32
    ).astype(jnp.bfloat16)
    term_sums = jnp.einsum(
        "qkms,qsn->kmn", scaled_rows, orbital_form, preferred_element_type=jnp.float32
    )
    atom_onehot = (tile_first[:, None] == jnp.arange(NAT, dtype=jnp.int32)[None, :]).astype(
        jnp.float32
    )
    return jnp.einsum("ka,kmn->amn", atom_onehot, term_sums, precision=lax.Precision.HIGHEST)


def per_device(three_center, tile_live, pair_atoms, green_occ, green_vir, screened):
    row_count, own_count = (three_center.shape[0], three_center.shape[1])
    masked = three_center * tile_live[0].astype(jnp.bfloat16)[:, None]
    inverse = jnp.argsort(pair_atoms)
    first_atom = pair_atoms // NAT
    second_atom = pair_atoms % NAT
    own_start = lax.axis_index("pair") * own_count
    own_first = lax.dynamic_slice_in_dim(first_atom, own_start, own_count)
    own_second = lax.dynamic_slice_in_dim(second_atom, own_start, own_count)
    occ_rows = green_occ.reshape(NAT, OA, NAT * OA)
    window = neighbor_window(masked)
    flat_window = window.reshape(window.shape[0], own_count * OA * OA)
    mixed_tiles = jnp.dot(screened, flat_window, preferred_element_type=jnp.float32).astype(
        jnp.bfloat16
    )
    mixed_tiles = mixed_tiles.reshape(row_count, own_count, OA * OA)
    gathered = lax.all_gather(masked, "pair", axis=1, tiled=True)
    orbital_form = tiles_to_matrix(gathered, inverse)
    products = own_products(orbital_form, green_occ, green_vir, own_first, own_second)
    by_atom = energy_rows(
        mixed_tiles, jnp.take(occ_rows, own_second, axis=0), orbital_form, own_first
    )
    chi_part = lax.dot_general(
        products.reshape(row_count, own_count * OA * OA),
        flat_window,
        (((1,), (1,)), ((), ())),
        preferred_element_type=jnp.float32,
    ) * (1.0 / (OA * NAT))
    polarizability = lax.psum_scatter(chi_part, "pair", scatter_dimension=1, tiled=True)
    aux_total = row_count * lax.axis_size("aux")
    sigma_scale = 1.0 / math.sqrt(aux_total * NAT * OA * NAT)
    partial_value = (
        matrix_to_tiles(by_atom.reshape(1, NAT * OA, NAT * OA), pair_atoms)[0] * -sigma_scale
    )
    columns = lax.psum_scatter(partial_value, "aux", scatter_dimension=1, tiled=True)
    owned_tiles = lax.psum_scatter(columns, "pair", scatter_dimension=0, tiled=True)
    self_energy = lax.all_gather(owned_tiles, "aux", axis=1, tiled=True)
    return (polarizability, self_energy)


def solution(mesh):
    placed = (P("aux", "pair", None), P("aux", "pair"), P(), P(), P(), P("aux", None))
    return jax.shard_map(
        per_device,
        mesh=mesh,
        in_specs=placed,
        out_specs=(P("aux", "pair"), P("pair", None)),
        check_vma=False,
    )
```

profile of v0, /device:TPU:0, one launch (start us, length us, event | category | flops | bytes accessed | tf_op | source)
XLA Modules:
  0.0 193.0 jit_solution(12782846579390709109)
XLA Ops:
  7.2 0.0 copy-start
  7.2 0.0 all-gather.3.cloned.1.call-start
  7.2 0.7 convert_bitcast_fusion.1
  7.9 2.2 %copy_multiply_fusion = bf16[8,32,1024]{2,0,1:T(8,128)(2,1)} fusion(bf16[8,32,1024]{2,1,0:T(8,128)(2,1)} %param.6, bf16[32]{0:T(256)(128)(2,1)S(1)} %convert_bitcast_fusion.1), kind=kLoop, calls=%fused_computation.26 | loop fusion | flops 262144 | bytes 1048640 | tf_op jit(solution)/shard_map/mul | solution.py:86
  10.1 0.0 all-gather.3.cloned.1.call-update
  10.1 0.0 reduce-scatter.8.cloned.1.call-start
  10.2 4.9 %collective-permute-start = (bf16[8,32,1024]{2,0,1:T(8,128)(2,1)}, bf16[8,32,1024]{2,0,1:T(8,128)(2,1)S(1)}, u32[]{:S(2)}, u32[]{:S(2)}) collective-permute-start(bf16[8,32,1024]{2,0,1:T(8,128)(2,1)} %copy_multiply_fusion), channel_id=1, source_target_pairs={{0,4},{2,6},{4,8},{6,10},{8,12},{10,14},{12,16},{14,18},{16,20},{1... | collective-permute-start | bytes 1572872 | tf_op jit(solution)/shard_map/ppermute | solution.py:16
  15.1 1.5 collective-permute-start.1
  16.6 1.3 collective-permute-start.2
  17.9 1.3 collective-permute-start.3
  19.2 2.7 %sort.17 = (s32[64]{0:T(128)}, s32[64]{0:T(128)S(1)}) sort(s32[64]{0:T(128)} %param.8, s32[64]{0:T(128)S(1)} %iota.8), dimensions={0}, to_apply=%region_0.0 | sort | flops 384 | bytes 1024 | tf_op jit(solution)/shard_map/jit(argsort)/sort | solution.py:87
  21.9 0.7 compare_select_fusion.3
  22.5 0.1 compare_and_fusion.2
  22.7 0.1 compare_and_fusion.3
  22.7 0.7 compare_and_fusion
  23.4 0.1 broadcast_in_dim.73
  23.5 1.0 copy.28
  24.5 0.0 copy-start.6
  24.5 0.6 gather_fusion
  25.1 0.0 copy-start.3
  25.1 1.4 gather_fusion.3
  26.5 0.6 dynamic-slice
  27.7 16.8 %collective-permute-done = bf16[8,32,1024]{2,0,1:T(8,128)(2,1)S(1)} collective-permute-done((bf16[8,32,1024]{2,0,1:T(8,128)(2,1)}, bf16[8,32,1024]{2,0,1:T(8,128)(2,1)S(1)}, u32[]{:S(2)}, u32[]{:S(2)}) %collective-permute-start) | collective-permute-done | bytes 524320 | tf_op jit(solution)/shard_map/ppermute | solution.py:16
  44.5 0.0 collective-permute-done.1
  44.6 0.3 constant_dynamic-update-slice_fusion.2
  44.9 0.0 collective-permute-done.2
  45.0 0.0 collective-permute-done.3
  45.0 0.0 copy-start.5
  45.0 0.3 copy.47
  45.4 0.0 copy-start.1
  45.4 1.5 copy-done.1
  46.9 0.5 fusion
  47.4 3.1 %reshape_reshape.7 = bf16[8,32,32,32]{3,2,1,0:T(8,128)(2,1)} reshape(bf16[8,32768]{1,0:T(8,128)(2,1)S(1)} %fusion) | data formatting | bytes 1048576 | tf_op jit(solution)/shard_map/reshape;reshape | solution.py:71
  50.5 1.8 gather_fusion.1
  52.3 4.6 %gather.27 = bf16[8,8,8,32,32]{4,3,0,2,1:T(8,128)(2,1)} reshape(bf16[8,64,1024]{2,0,1:T(8,128)(2,1)S(1)} %bitcast.83) | data formatting | bytes 2097152 | tf_op jit(solution)/shard_map/jit(_take)/gather | solution.py:21
  56.9 2.6 %select_bitcast_fusion = bf16[8,8,32,8,32]{4,2,0,3,1:T(8,128)(2,1)S(1)} fusion(bf16[8,8,8,32,32]{4,3,0,2,1:T(8,128)(2,1)} %gather.27, pred[8,8]{1,0:T(8,128)(4,1)S(1)} %broadcast_in_dim.73), kind=kLoop, calls=%fused_computation.13 | loop fusion | flops 524288 | bytes 2097216 | tf_op jit(solution)/shard_map/transpose | solution.py:23
  59.5 6.8 %copy.30 = bf16[8,8,32,8,32]{4,3,2,1,0:T(8,128)(2,1)} copy(bf16[8,8,32,8,32]{4,2,0,3,1:T(8,128)(2,1)S(1)} %select_bitcast_fusion) | data formatting | bytes 2097152 | tf_op jit(solution)/shard_map/transpose | solution.py:23
  66.3 5.3 %squeeze.7 = bf16[8,256,256]{2,1,0:T(8,128)(2,1)S(1)} reshape(bf16[8,8,32,8,32]{4,3,2,1,0:T(8,128)(2,1)} %copy.30) | data formatting | bytes 2097152 | tf_op jit(solution)/shard_map/while/body/jit(dynamic_index_in_dim)/squeeze | solution.py:47
  71.6 6.2 %reshape.122 = bf16[8,256,256,1]{2,1,0,3:T(8,128)(2,1)} reshape(bf16[8,8,32,8,32]{4,3,2,1,0:T(8,128)(2,1)} %copy.30) | data formatting | bytes 2097152 | tf_op jit(solution)/shard_map/while/body/jit(dynamic_index_in_dim)/squeeze | solution.py:47
  77.9 0.5 convolution_convert_fusion.1
  78.4 4.2 %fusion.15 = f32[32,32,256]{2,1,0:T(8,128)S(1)} fusion(bf16[8,256,256,1]{2,1,0,3:T(8,128)(2,1)} %reshape.122, bf16[8,32,32,32]{3,2,1,0:T(8,128)(2,1)} %reshape_reshape.7, bf16[32,32,256]{2,1,0:T(8,128)(2,1)S(1)} %copy-done.4, pred[32]{0:T(512)(128)(4,1)S(1)} %get-tuple-element.16), kind=kOutput, calls=%fused_computation.20 | convolution fusion | flops 1210318848 | bytes 3145760 | tf_op jit(solution)/shard_map/qkms,qsn->kmn/dot_general | solution.py:75
  82.6 1.0 fusion.20
  83.7 0.3 reshape_reshape.8
  83.9 1.6 copy.36
  85.5 1.7 reshape.100
  87.2 0.7 gather_fusion.4
  87.9 0.1 select_multiply_fusion
  88.0 1.0 copy.45
  89.0 0.0 reduce-scatter.8.cloned.1.call-update
  89.1 0.0 reduce-scatter.6.cloned.1.call-start
  89.1 2.8 %gather_fusion.2 = bf16[32,8,32,256]{3,2,1,0:T(8,128)(2,1)} fusion(bf16[8,8,32,256]{3,2,1,0:T(8,128)(2,1)S(1)} %bitcast.80, s32[1024]{0:T(1024)S(1)} %get-tuple-element.30), kind=kCustom, calls=%fused_computation.2 | custom fusion | bytes 8388736 | tf_op jit(solution)/shard_map/while/body/eval_jaxpr/jit(_take)/gather | solution.py:58
  91.9 7.1 %convert_bitcast_fusion = bf16[8,32,32,32]{2,3,0,1:T(8,128)(2,1)} fusion(bf16[32,8,32,256]{3,2,1,0:T(8,128)(2,1)} %gather_fusion.2, pred[32]{0:T(512)(128)(4,1)S(1)} %get-tuple-element.24, bf16[32,256,32]{1,2,0:T(8,128)(2,1)S(1)} %gather_fusion, pred[32]{0:T(512)(128)(4,1)S(1)} %get-tuple-element.16), kind=kOutput, calls=%fused_computation.18 | convolution fusion | flops 136839168 | bytes 5242944 | tf_op jit(solution)/shard_map/while/body/eval_jaxpr/pkum,mkv->pkuv/dot_general | solution.py:61
  99.0 4.2 %copy.32 = bf16[8,32,32,32]{3,2,1,0:T(8,128)(2,1)} copy(bf16[8,32,32,32]{2,3,0,1:T(8,128)(2,1)} %convert_bitcast_fusion) | data formatting | bytes 1048576 | tf_op jit(solution)/shard_map/while/body/eval_jaxpr/convert_element_type | solution.py:63
  103.2 3.8 %reshape_reshape_reshape.3 = bf16[8,32768]{1,0:T(8,128)(2,1)S(1)} reshape(bf16[8,32,32,32]{3,2,1,0:T(8,128)(2,1)} %copy.32) | data formatting | bytes 1048576 | tf_op jit(solution)/shard_map/reshape;reshape;reshape | solution.py:107
  107.1 0.8 convolution_multiply_fusion
  107.9 4.9 %all-reduce = f32[8,40]{1,0:T(8,128)S(1)} all-reduce(f32[8,40]{1,0:T(8,128)S(1)} %convolution_multiply_fusion), channel_id=2, replica_groups=mesh['aux'=16,'pair'=2] {'pair'}, use_global_device_ids=true, to_apply=%region_1.2.clone | all-reduce | flops 320 | bytes 2560
  112.8 38.7 %reduce-scatter.8.cloned.1.call-done = f32[64,64]{1,0:T(8,128)} async-done(((f32[1024,64]{1,0:T(8,128)}), f32[64,64]{1,0:T(8,128)}) %reduce-scatter.8.cloned.1.call-update) | async-done | bytes 16400
  151.5 1.5 copy.46
  152.9 0.0 reduce-scatter.6.cloned.1.call-update
  153.0 0.7 constant_dynamic-slice_fusion
  153.6 9.7 %reduce-scatter.6.cloned.1.call-done = f32[32,64]{1,0:T(8,128)} async-done(((f32[64,64]{1,0:T(8,128)}), f32[32,64]{1,0:T(8,128)}) %reduce-scatter.6.cloned.1.call-update) | async-done | bytes 8208 | tf_op jit(solution)/shard_map/reduce_scatter | solution.py:119
  163.3 22.3 %all-gather = f32[16,64,32]{1,2,0:T(8,128)S(1)} all-gather(f32[1,64,32]{1,2,0:T(8,128)} %bitcast.89), channel_id=1, replica_groups=mesh['aux'=16,'pair'=2] {'aux'}, dimensions={0}, use_global_device_ids=true | all-gather | bytes 139264 | tf_op jit(solution)/shard_map/all_gather | solution.py:120
  185.5 0.2 copy.37
  185.7 0.8 reshape.118
  (20 shorter events, 0.2 us)
Async XLA Ops:
  7.2 18.0 %copy-start = (bf16[256,256]{1,0:T(8,128)(2,1)S(1)}, bf16[256,256]{1,0:T(8,128)(2,1)}, u32[]{:S(2)}) copy-start(bf16[256,256]{1,0:T(8,128)(2,1)} %param.9) | copy-start | bytes 393220
  7.2 43.3 %all-gather.3.cloned.1.call-start = ((), (), s32[]{:S(2)}) async-start(), calls=%async_computation.2 | async-start | bytes 1572864 | tf_op jit(solution)/shard_map/all_gather | solution.py:100
  10.1 141.4 %reduce-scatter.8.cloned.1.call-start = ((), (), s32[]{:S(2)}) async-start(), calls=%async_computation.4 | async-start | bytes 557056
  10.2 34.3 %collective-permute-start = (bf16[8,32,1024]{2,0,1:T(8,128)(2,1)}, bf16[8,32,1024]{2,0,1:T(8,128)(2,1)S(1)}, u32[]{:S(2)}, u32[]{:S(2)}) collective-permute-start(bf16[8,32,1024]{2,0,1:T(8,128)(2,1)} %copy_multiply_fusion), channel_id=1, source_target_pairs={{0,4},{2,6},{4,8},{6,10},{8,12},{10,14},{12,16},{14,18},{16,20},{1... | collective-permute-start | bytes 1572872 | tf_op jit(solution)/shard_map/ppermute | solution.py:16
  15.1 29.5 %collective-permute-start.1 = (bf16[8,32,1024]{2,0,1:T(8,128)(2,1)}, bf16[8,32,1024]{2,0,1:T(8,128)(2,1)S(1)}, u32[]{:S(2)}, u32[]{:S(2)}) collective-permute-start(bf16[8,32,1024]{2,0,1:T(8,128)(2,1)} %copy_multiply_fusion), channel_id=1, source_target_pairs={{0,2},{2,4},{4,6},{6,8},{8,10},{10,12},{12,14},{14,16},{16,18},{18... | collective-permute-start | bytes 1572872 | tf_op jit(solution)/shard_map/ppermute | solution.py:16
  16.6 28.4 %collective-permute-start.2 = (bf16[8,32,1024]{2,0,1:T(8,128)(2,1)}, bf16[8,32,1024]{2,0,1:T(8,128)(2,1)S(1)}, u32[]{:S(2)}, u32[]{:S(2)}) collective-permute-start(bf16[8,32,1024]{2,0,1:T(8,128)(2,1)} %copy_multiply_fusion), channel_id=1, source_target_pairs={{2,0},{4,2},{6,4},{8,6},{10,8},{12,10},{14,12},{16,14},{18,16},{20... | collective-permute-start | bytes 1572872 | tf_op jit(solution)/shard_map/ppermute | solution.py:16
  17.9 27.1 %collective-permute-start.3 = (bf16[8,32,1024]{2,0,1:T(8,128)(2,1)}, bf16[8,32,1024]{2,0,1:T(8,128)(2,1)S(1)}, u32[]{:S(2)}, u32[]{:S(2)}) collective-permute-start(bf16[8,32,1024]{2,0,1:T(8,128)(2,1)} %copy_multiply_fusion), channel_id=1, source_target_pairs={{4,0},{6,2},{8,4},{10,6},{12,8},{14,10},{16,12},{18,14},{20,16},{2... | collective-permute-start | bytes 1572872 | tf_op jit(solution)/shard_map/ppermute | solution.py:16
  24.5 2.0 %copy-start.6 = (u32[32]{0:T(128)S(1)}, u32[32]{0:T(128)}, u32[]{:S(2)}) copy-start(u32[32]{0:T(128)} %constant.122) | copy-start | bytes 388
  25.1 19.5 %copy-start.3 = (bf16[8,32,1024]{2,1,0:T(8,128)(2,1)S(1)}, bf16[8,32,1024]{2,1,0:T(8,128)(2,1)}, u32[]{:S(2)}) copy-start(bf16[8,32,1024]{2,1,0:T(8,128)(2,1)} %param.6) | copy-start | bytes 1572868
  45.0 1.9 copy-start.5
  45.4 1.5 copy-start.1
  71.6 6.7 %copy-start.4 = (bf16[32,32,256]{2,1,0:T(8,128)(2,1)S(1)}, bf16[32,32,256]{2,1,0:T(8,128)(2,1)}, u32[]{:S(2)}) copy-start(bf16[32,32,256]{2,1,0:T(8,128)(2,1)} %gather_fusion.3) | copy-start | bytes 1572868
  89.1 74.2 %reduce-scatter.6.cloned.1.call-start = ((), (), s32[]{:S(2)}) async-start(), calls=%async_computation.3 | async-start | bytes 49152 | tf_op jit(solution)/shard_map/reduce_scatter | solution.py:119
  99.0 8.1 %copy-start.2 = (bf16[32,5,8,1024]{3,2,0,1:T(8,128)(2,1)S(1)}, bf16[32,5,8,1024]{3,2,0,1:T(8,128)(2,1)}, u32[]{:S(2)}) copy-start(bf16[32,5,8,1024]{3,2,0,1:T(8,128)(2,1)} %copy-done.1) | copy-start | bytes 7864324
Sparse Core Ops, SparseCore 0:
  10.2 23.9 all-gather.2
  89.2 62.2 reduce-scatter.7
  154.2 8.9 reduce-scatter.5
where the time goes:
time: 194 us; the launch traced here: 193 us
  waiting for transfers between devices  65.2 us (34%)
  local copies, waits for them, and re-layouts  52.6 us (27%)
  blocking collectives  27.2 us (14%)
  between operations  14.7 us (8%)
  matrix products  14.1 us (7%)
  other arithmetic  10.1 us (5%)
  starting transfers between devices  9.1 us (5%)
    unnamed x4, waiting for transfers between devices  38.7 us
    all_gather x1, blocking collectives, per_device(): self_energy = lax.all_gather(owned_tiles, 'aux', axis=1, tiled=True)  22.3 us
    ppermute x4, waiting for transfers between devices, shifted(): lax.ppermute(value, axis, [(source, source + steps) for source in range(i...  16.8 us
    squeeze x2, local copies, waits for them, and re-layouts, row_groups(): result = lax.map(group_fn, grouped)  11.6 us
    reduce_scatter x1, waiting for transfers between devices, per_device(): lax.psum_scatter(columns, 'pair', scatter_dimension=0, tiled=True)  9.66 us
    ppermute x4, starting transfers between devices, shifted(): lax.ppermute(value, axis, [(source, source + steps) for source in range(i...  8.98 us
    unnamed x23, local copies, waits for them, and re-layouts  7.21 us
    dot_general x1, matrix products, group_fn(): jnp.einsum('pkum,mkv->pkuv', picked, vir_cols, preferred_element_type=jnp...  7.14 us
  transfers between devices with their start and end apart: 7, of which 3 were waited for; matrix products, arithmetic and copies ran while one was open for 16% of the time, Pallas kernels for 0%

commit v1 on v0

v1 whole, which is shorter than its diff:
```python
import math

import jax
import jax.numpy as jnp
from jax import lax
from jax.experimental import pallas as pl
from jax.experimental.pallas import tpu as pltpu
from jax.sharding import PartitionSpec as P

OA = 32
NAT = 8
REACH = 2
BLK = 8
NORB = OA * NAT
PAIR = OA * OA
LANE = 128
RQ = LANE // OA
NQ = OA // RQ
LIVE_AT = 64
BF = jnp.bfloat16
F4 = jnp.float32


def iota(shape, dim):
    return lax.broadcasted_iota(jnp.int32, shape, dim)


def mm(a, b):
    return lax.dot_general(a, b, (((1,), (0,)), ((), ())), preferred_element_type=F4)


def mm_nt(a, b):
    return lax.dot_general(a, b, (((1,), (1,)), ((), ())), preferred_element_type=F4)


def mm_tn(a, b):
    return lax.dot_general(a, b, (((0,), (0,)), ((), ())), preferred_element_type=F4)


def onehot(cond):
    return cond.astype(F4).astype(BF)


def div(x, n):
    if n & (n - 1) == 0:
        return lax.shift_right_logical(x, jnp.full_like(x, n.bit_length() - 1))
    return x // n


def mod(x, n):
    if n & (n - 1) == 0:
        return x & (n - 1)
    return x % n


def mm_split(a, b):
    count = a.shape[0]
    high = a.astype(BF)
    rest = a - high.astype(F4)
    middle = rest.astype(BF)
    low = (rest - middle.astype(F4)).astype(BF)
    out = mm(jnp.concatenate([high.astype(F4), middle.astype(F4), low.astype(F4)], axis=0).astype(BF), b)
    return out[:count] + out[count : 2 * count] + out[2 * count :]


def pick_rows(count):
    return -(-count // LANE) * BLK


def slot_onehot(pair_row):
    count = pair_row.shape[1]
    slot = iota((NAT * NAT, count), 0)
    second = mod(div(slot, NAT), 2) * RQ + div(slot, 2 * NAT)
    return mod(slot, NAT) * NAT + second == pair_row


def to_matrix(tiles, swap):
    rows = [
        jnp.concatenate(
            [tiles[i * 2 * NAT : (i + 1) * 2 * NAT, q * LANE : (q + 1) * LANE] for i in range(RQ)],
            axis=1,
        )
        for q in range(NQ)
    ]
    mixed = mm(jnp.concatenate(rows, axis=0), swap)
    out = [
        jnp.concatenate(
            [
                mixed[(q * 2 + g) * NAT : (q * 2 + g + 1) * NAT, i * LANE : (i + 1) * LANE]
                for g in range(2)
            ],
            axis=1,
        )
        for i in range(RQ)
        for q in range(NQ)
    ]
    return jnp.concatenate(out, axis=0).astype(BF)


def from_matrix(matrix, swap):
    rows = [
        jnp.concatenate(
            [
                matrix[(i * NQ + q) * NAT : (i * NQ + q + 1) * NAT, g * LANE : (g + 1) * LANE]
                for i in range(RQ)
            ],
            axis=1,
        )
        for q in range(NQ)
        for g in range(2)
    ]
    mixed = mm(jnp.concatenate(rows, axis=0).astype(BF), swap).astype(BF)
    out = [
        jnp.concatenate(
            [
                mixed[q * 2 * NAT : (q + 1) * 2 * NAT, i * LANE : (i + 1) * LANE]
                for q in range(NQ)
            ],
            axis=1,
        )
        for i in range(RQ)
    ]
    return jnp.concatenate(out, axis=0)


def tables_kernel(occ_ref, vir_ref, swap_ref, both_ref, both_t_ref, cols_ref, vir_t_ref):
    size = RQ * LANE
    row = iota((size, size), 0)
    col = iota((size, size), 1)
    swapped = mod(div(row, OA), RQ) * LANE + div(row, LANE) * OA + mod(row, OA)
    swap_ref[...] = onehot(swapped == col)
    row = iota((NORB, NORB), 0)
    col = iota((NORB, NORB), 1)
    natural = mod(row, NAT) * OA + mod(div(row, NAT), NQ) * RQ + div(row, NAT * NQ)
    order = onehot(natural == col)
    occ = occ_ref[...]
    cols = mm_nt(occ, order).astype(BF)
    both = mm(order, cols)
    cols_ref[...] = cols
    both_ref[...] = both.astype(BF)
    both_t_ref[...] = both.T.astype(BF)
    vir_t_ref[...] = vir_ref[...].astype(F4).T.astype(BF)


def own_kernel(count, *refs):
    pairs_ref, metas = refs[0], refs[1 : 1 + count]
    pieces = refs[1 + count : 1 + 2 * count]
    swap_ref, both_ref, both_t_ref, cols_ref, vir_ref, vir_t_ref = refs[1 + 2 * count : 7 + 2 * count]
    matrix_ref, right_ref, z_ref, y_ref = refs[7 + 2 * count :]
    own_count = pieces[0].shape[1]
    swap = swap_ref[...]
    tiles = None
    for s in range(count):
        live = metas[s][0:1, LIVE_AT : LIVE_AT + own_count].astype(F4)
        select = (slot_onehot(pairs_ref[s : s + 1, :]).astype(F4) * live).astype(BF)
        part = mm(select, pieces[s][0])
        tiles = part if tiles is None else tiles + part
    own_select = onehot(slot_onehot(pairs_ref[0:1, :]))
    matrix = to_matrix(tiles.astype(BF), swap)
    matrix_ref[0] = matrix
    right_ref[0] = mm(matrix, cols_ref[...]).astype(BF)
    left = mm(both_t_ref[...], matrix).astype(BF)
    z_tiles = from_matrix(mm(left, vir_ref[...]), swap)
    z_ref[0] = mm_tn(own_select, z_tiles).astype(BF)
    left = mm(both_ref[...], matrix).astype(BF)
    y_tiles = from_matrix(mm(left, vir_t_ref[...]), swap)
    y_ref[0] = mm_tn(own_select, y_tiles).astype(BF)


def window_kernel(lanes, sigma_scale, chi_scale, place_ref, *refs):
    (pairs_ref, meta0, meta1, meta2, tile0, tile1a, tile1b, tile2) = refs[:8]
    (z_ref, y_ref, matrix_ref, right_ref, swap_ref, cols_ref, keep_ref, send_ref) = refs[8:]
    pair_count, own_count = pairs_ref.shape
    rows = BLK * own_count
    block, pair_at = place_ref[0], place_ref[1]
    row = iota((rows, rows), 0)
    col = iota((rows, rows), 1)
    same = (mod(row, own_count) == mod(col, own_count)).astype(F4)
    spread_row, spread_col = iota((LANE, rows), 0), iota((LANE, rows), 1)
    spread = onehot(spread_row == LIVE_AT + mod(spread_col, own_count))
    metas = [m[...] for m in (meta0, meta1, meta2)]
    masks = [same * mm(m, spread)[0:1, :] for m in metas]
    tiles = [tile0[...], tile1a[...] + tile1b[...], tile2[...]]
    expand = onehot(div(iota((rows, BLK), 0), own_count) == iota((rows, BLK), 1))
    own_weights = mm(expand, metas[0]).astype(BF)
    mixed = jnp.zeros((rows, PAIR), F4)
    for t in range(REACH + 1):
        pick = onehot(spread_row == (REACH + t) * BLK + div(spread_col, own_count))
        mixed = mixed + mm((mm(own_weights, pick) * masks[t]).astype(BF), tiles[t])
    other = jnp.zeros((rows, PAIR), F4)
    unspread = onehot(iota((BLK, rows), 0) == div(iota((BLK, rows), 1), own_count))
    for t in range(1, REACH + 1):
        pick = onehot(
            iota((rows, LANE), 1) == (REACH - t) * BLK + div(iota((rows, LANE), 0), own_count)
        )
        weights = mm(mm_nt(pick, metas[t]).astype(BF), unspread)
        other = other + mm((weights * masks[t]).astype(BF), tiles[t])
    mixed = mixed.astype(BF)
    other = other.astype(BF)
    swap = swap_ref[...]
    own_select = onehot(slot_onehot(pairs_ref[0:1, :]))
    total = jnp.zeros((NORB, NORB), F4)
    for r in range(BLK):
        at = slice(r * own_count, (r + 1) * own_count)
        value = to_matrix(mm(own_select, mixed[at]).astype(BF), swap)
        scaled = mm(value, cols_ref[...]).astype(BF)
        total = total + mm(scaled, matrix_ref[r])
        value = to_matrix(mm(own_select, other[at]).astype(BF), swap)
        total = total + mm(right_ref[r], value)
    total = total * -sigma_scale
    high = total.astype(BF).astype(F4)
    parts = [from_matrix(high, swap), from_matrix(total - high, swap)]
    parity = block & 1
    half = own_count // 2
    for s in range(pair_count):
        select = onehot(slot_onehot(pairs_ref[s : s + 1, :]))
        owned = mm_tn(select, parts[0]) + mm_tn(select, parts[1])
        first, second = owned[:half], owned[half:]
        keep = jnp.where(parity == 0, first, second)
        send = jnp.where(parity == 0, second, first)
        for q in range(NQ):
            keep_ref[s, q * half : (q + 1) * half, :] = keep[:, q * LANE : (q + 1) * LANE]
            send_ref[s, q * half : (q + 1) * half, :] = send[:, q * LANE : (q + 1) * LANE]

    chi = jnp.zeros((BLK, LANE), F4)
    for t in range(-REACH, REACH + 1):
        w = abs(t)
        if t < 0:
            cross = mm_nt(tiles[w], y_ref[...])
        else:
            cross = mm_nt(z_ref[...], tiles[w])
        cross = cross * masks[w]
        sums = jnp.concatenate(
            [
                jnp.sum(cross[p * own_count : (p + 1) * own_count], axis=0, keepdims=True)
                for p in range(BLK)
            ],
            axis=0,
        )
        pick = onehot(
            iota((rows, LANE), 1) == (REACH + t) * BLK + div(iota((rows, LANE), 0), own_count)
        )
        chi = chi + mm_split(sums, pick)
    chi = chi * chi_scale
    share = (2 * REACH + 1) * BLK // pair_count
    column = iota((LANE, 1), 0)
    target = block + jnp.maximum(REACH - div(column, BLK), 0)
    at_pair = jnp.zeros((LANE, 1), jnp.int32)
    for s in range(1, pair_count):
        at_pair = at_pair + (column >= s * share).astype(jnp.int32)
    place = mod(at_pair - pair_at + pair_count, pair_count) + (
        ((target ^ block) & 1) * pair_count
    )
    spot = place * lanes + div(target, 2) * share + column - at_pair * share
    spread = onehot(iota((LANE, 2 * pair_count * lanes), 1) == spot)
    placed = mm_split(chi, spread)
    for s in range(pair_count):
        for i in range(lanes // LANE):
            at = slice(NQ * half + i * BLK, NQ * half + (i + 1) * BLK)
            begin = s * lanes + i * LANE
            keep_ref[s, at, :] = placed[:, begin : begin + LANE]
            begin += pair_count * lanes
            send_ref[s, at, :] = placed[:, begin : begin + LANE]


def last_kernel(place_ref, own_ref, other_ref, chi_ref, energy_ref):
    half = energy_ref.shape[0] // 2
    share = chi_ref.shape[1]
    parity = place_ref[0] & 1
    own, other = own_ref[...], other_ref[...]
    first = jnp.where(parity == 0, own, other)
    second = jnp.where(parity == 0, other, own)
    for q in range(NQ):
        at = slice(q * LANE, (q + 1) * LANE)
        energy_ref[:half, at] = first[q * half : (q + 1) * half]
        energy_ref[half:, at] = second[q * half : (q + 1) * half]
    start = (place_ref[0] >> 1) * share
    total = None
    for i in range((own.shape[0] - NQ * half) // BLK):
        chi = own[NQ * half + i * BLK : NQ * half + (i + 1) * BLK]
        pick = onehot(iota((LANE, LANE), 0) + i * LANE == start + iota((LANE, LANE), 1))
        part = mm_split(chi, pick)
        total = part if total is None else total + part
    chi_ref[...] = total[:, :share]


def call(body, outs, *args, grid=None, in_specs=None, out_specs=None, flops=10**8):
    extra = {}
    if grid is not None:
        extra = dict(grid=grid, in_specs=in_specs, out_specs=out_specs)
    else:
        full = pl.BlockSpec(memory_space=pltpu.VMEM)
        extra = dict(
            in_specs=[
                pl.BlockSpec(memory_space=pltpu.SMEM) if a.ndim == 1 else full for a in args
            ],
            out_specs=jax.tree.map(lambda o: full, outs),
        )
    return pl.pallas_call(
        body,
        out_shape=outs,
        cost_estimate=pl.CostEstimate(flops=flops, bytes_accessed=10**6, transcendentals=0),
        **extra,
    )(*args)


def per_device(three_center, tile_live, pair_atoms, green_occ, green_vir, screened):
    block_rows, own_count = three_center.shape[:2]
    aux_count, pair_count = lax.axis_size("aux"), lax.axis_size("pair")
    block, pair_at = lax.axis_index("aux"), lax.axis_index("pair")
    rows = block_rows * own_count
    window = screened.shape[1]
    shape = jax.ShapeDtypeStruct

    def shifted(value, steps, parity=None):
        return lax.ppermute(
            value,
            "aux",
            [
                (s, s + steps)
                for s in range(aux_count)
                if 0 <= s + steps < aux_count and parity in (None, s % 2)
            ],
        )

    def turned(value, steps):
        return lax.ppermute(
            value, "pair", [(s, (s - steps) % pair_count) for s in range(pair_count)]
        )

    def flipped(value, mask):
        return lax.ppermute(value, "aux", [(s, s ^ mask) for s in range(aux_count)])

    live = jnp.broadcast_to(tile_live.astype(BF), (block_rows, own_count))
    meta = jnp.concatenate(
        [
            screened,
            jnp.zeros((block_rows, LIVE_AT - window), BF),
            live,
            jnp.zeros((block_rows, LANE - LIVE_AT - own_count), BF),
        ],
        axis=1,
    )
    far = shifted(three_center, -2)
    pieces = [three_center] + [turned(three_center, s) for s in range(1, pair_count)]
    near_even = shifted(three_center, -1, 1)
    metas = [meta] + [turned(meta, s) for s in range(1, pair_count)]
    meta_near, meta_far = shifted(meta, -1), shifted(meta, -2)
    near_odd = shifted(far, 1, 0)
    pairs = lax.dynamic_slice_in_dim(
        jnp.concatenate([pair_atoms, pair_atoms]), pair_at * own_count, pair_count * own_count
    ).reshape(pair_count, own_count)
    place = jnp.stack([block, pair_at]).astype(jnp.int32)

    square = shape((NORB, NORB), BF)
    swap, both, both_t, cols, vir_t = call(
        tables_kernel,
        [shape((RQ * LANE, RQ * LANE), BF), square, square, square, square],
        green_occ,
        green_vir,
    )

    def whole(value):
        return pl.BlockSpec(value.shape, lambda p: (0,) * value.ndim)

    def one(a, b):
        return pl.BlockSpec((1, a, b), lambda p: (p, 0, 0))

    fixed = [swap, both, both_t, cols, green_vir, vir_t]
    matrix, right, z, y = call(
        lambda *refs: own_kernel(pair_count, *refs),
        [
            shape((block_rows, NORB, NORB), BF),
            shape((block_rows, NORB, NORB), BF),
            shape((block_rows, own_count, PAIR), BF),
            shape((block_rows, own_count, PAIR), BF),
        ],
        pairs,
        *metas,
        *pieces,
        *fixed,
        grid=(block_rows,),
        in_specs=[whole(pairs)]
        + [whole(m) for m in metas]
        + [one(own_count, PAIR) for _ in pieces]
        + [whole(f) for f in fixed],
        out_specs=[one(NORB, NORB), one(NORB, NORB), one(own_count, PAIR), one(own_count, PAIR)],
    )

    lanes = -(-(aux_count // 2) * (window // pair_count) // LANE) * LANE
    message = shape((pair_count, own_count // 2 * NQ + lanes // LANE * BLK, LANE), F4)
    aux_total = block_rows * aux_count
    keep, send = call(
        lambda *refs: window_kernel(
            lanes, 1.0 / math.sqrt(aux_total * NAT * OA * NAT), 1.0 / (OA * NAT), *refs
        ),
        [message, message],
        place,
        pairs,
        meta,
        meta_near,
        meta_far,
        three_center.reshape(rows, PAIR),
        near_even.reshape(rows, PAIR),
        near_odd.reshape(rows, PAIR),
        far.reshape(rows, PAIR),
        z.reshape(rows, PAIR),
        y.reshape(rows, PAIR),
        matrix,
        right,
        swap,
        cols,
    )
    total = keep + flipped(send, 1)
    owned = total[0]
    for s in range(1, pair_count):
        owned = owned + turned(total[s], -s)
    mask = 2
    while mask < aux_count:
        owned = owned + flipped(owned, mask)
        mask *= 2
    polarizability, self_energy = call(
        last_kernel,
        [
            shape((block_rows, window // pair_count), F4),
            shape((own_count, PAIR), F4),
        ],
        place,
        owned,
        flipped(owned, 1),
    )
    return polarizability, self_energy


def solution(mesh):
    placed = (P("aux", "pair", None), P("aux", "pair"), P(), P(), P(), P("aux", None))
    return jax.shard_map(
        per_device,
        mesh=mesh,
        in_specs=placed,
        out_specs=(P("aux", "pair"), P("pair", None)),
        check_vma=False,
    )
```

time: 194 us -> 87.5 us (0.45)
  local copies, waits for them, and re-layouts: 52.6 us -> 4.61 us
  waiting for transfers between devices: 65.2 us -> 25.1 us
  Pallas kernels: 0 us -> 31.7 us
  blocking collectives: 27.2 us -> 0 us
  matrix products: 14.1 us -> 0 us
  between operations: 14.7 us -> 0.82 us
  starting transfers between devices: 9.1 us -> 22.7 us
  other arithmetic: 10.1 us -> 2.29 us
    unnamed x4 -> x0, waiting for transfers between devices: 38.7 us -> none
    pallas_call x0 -> x4, Pallas kernels: none -> 31.7 us  [call(): pl.pallas_call(body, out_shape=outs, cost_estimate=pl.CostEstimate(flops=...]
    all_gather x1 -> x0, blocking collectives: 22.3 us -> none  [per_device(): self_energy = lax.all_gather(owned_tiles, 'aux', axis=1, tiled=True)]
    dot_general x6 -> x0, matrix products: 14.1 us -> none  [the longest x1 7.14 us: group_fn(): jnp.einsum('pkum,mkv->pkuv', picked, vir_cols, preferred_element_type=jnp...]
    ppermute x4 -> x13, starting transfers between devices: 8.98 us -> 22.7 us  [the longest x5 11 us: flipped(): return lax.ppermute(value, 'aux', [(s, s ^ mask) for s in range(aux_count)])]
    gather x6 -> x0, local copies, waits for them, and re-layouts: 11.8 us -> none  [the longest x2 6.39 us: tiles_to_matrix(): ordered = jnp.take(tile_data, inverse, axis=1)]
    squeeze x2 -> x1, local copies, waits for them, and re-layouts: 11.6 us -> 0.01 us  [per_device(): owned = owned + turned(total[s], -s)]
    reduce_scatter x1 -> x0, waiting for transfers between devices: 9.66 us -> none  [per_device(): lax.psum_scatter(columns, 'pair', scatter_dimension=0, tiled=True)]
  transfers between devices with their start and end apart: 7 -> 13, of which waited for: 3 -> 7; matrix products, arithmetic and copies ran while one was open for 16% -> 3% of each run, Pallas kernels for 0% -> 20%
where the time goes in v1:
time: 87.5 us; the launch traced here: 87.2 us
  Pallas kernels  31.7 us (36%)
  waiting for transfers between devices  25.1 us (29%)
  starting transfers between devices  22.7 us (26%)
  local copies, waits for them, and re-layouts  4.61 us (5%)
  other arithmetic  2.29 us (3%)
    pallas_call x4, Pallas kernels, call(): pl.pallas_call(body, out_shape=outs, cost_estimate=pl.CostEstimate(flops=...  31.7 us
    ppermute x5, waiting for transfers between devices, shifted(): lax.ppermute(value, 'aux', [(s, s + steps) for s in range(aux_count) if 0...  11.4 us
    ppermute x5, starting transfers between devices, flipped(): return lax.ppermute(value, 'aux', [(s, s ^ mask) for s in range(aux_count)])  11 us
    ppermute x5, waiting for transfers between devices, flipped(): return lax.ppermute(value, 'aux', [(s, s ^ mask) for s in range(aux_count)])  9.47 us
    ppermute x5, starting transfers between devices, shifted(): lax.ppermute(value, 'aux', [(s, s + steps) for s in range(aux_count) if 0...  6.45 us
    ppermute x3, starting transfers between devices, turned(): lax.ppermute(value, 'pair', [(s, (s - steps) % pair_count) for s in range...  5.22 us
    ppermute x3, waiting for transfers between devices, turned(): lax.ppermute(value, 'pair', [(s, (s - steps) % pair_count) for s in range...  4.28 us
    unnamed x24, local copies, waits for them, and re-layouts  3.63 us
  transfers between devices with their start and end apart: 13, of which 7 were waited for; matrix products, arithmetic and copies ran while one was open for 3% of the time, Pallas kernels for 20%

profile of v1, /device:TPU:0, one launch (start us, length us, event | category | flops | bytes accessed | tf_op | source)
XLA Modules:
  0.0 87.2 jit_solution(14348551413849912820)
XLA Ops:
  0.6 1.3 %collective-permute-start.3 = (bf16[8,32,1024]{2,1,0:T(8,128)(2,1)}, bf16[8,32,1024]{2,1,0:T(8,128)(2,1)S(1)}, u32[]{:S(2)}, u32[]{:S(2)}) collective-permute-start(bf16[8,32,1024]{2,1,0:T(8,128)(2,1)} %refs_3_.1), channel_id=1, source_target_pairs={{4,0},{6,2},{8,4},{10,6},{12,8},{14,10},{16,12},{18,14},{20,16},{2... | collective-permute-start | bytes 1572872 | tf_op jit(solution)/shard_map/ppermute | solution.py:316
  1.9 3.1 %collective-permute-start.6 = (bf16[8,32,1024]{2,1,0:T(8,128)(2,1)}, bf16[8,32,1024]{2,1,0:T(8,128)(2,1)S(1)}, u32[]{:S(2)}, u32[]{:S(2)}) collective-permute-start(bf16[8,32,1024]{2,1,0:T(8,128)(2,1)} %refs_3_.1), channel_id=1, source_target_pairs={{0,1},{1,0},{2,3},{3,2},{4,5},{5,4},{6,7},{7,6},{8,9},{9,8},{10,11... | collective-permute-start | bytes 1572872 | tf_op jit(solution)/shard_map/ppermute | solution.py:327
  5.0 1.3 %collective-permute-start.2 = (bf16[8,32,1024]{2,1,0:T(8,128)(2,1)}, bf16[8,32,1024]{2,1,0:T(8,128)(2,1)S(1)}, u32[]{:S(2)}, u32[]{:S(2)}) collective-permute-start(bf16[8,32,1024]{2,1,0:T(8,128)(2,1)} %refs_3_.1), channel_id=1, source_target_pairs={{2,0},{6,4},{10,8},{14,12},{18,16},{22,20},{26,24},{30,28},{3,1},{... | collective-permute-start | bytes 1572872 | tf_op jit(solution)/shard_map/ppermute | solution.py:316
  6.3 11.4 %collective-permute-done.3 = bf16[8,32,1024]{2,1,0:T(8,128)(2,1)S(1)} collective-permute-done((bf16[8,32,1024]{2,1,0:T(8,128)(2,1)}, bf16[8,32,1024]{2,1,0:T(8,128)(2,1)S(1)}, u32[]{:S(2)}, u32[]{:S(2)}) %collective-permute-start.3) | collective-permute-done | bytes 524320 | tf_op jit(solution)/shard_map/ppermute | solution.py:316
  17.6 0.0 copy-start.1
  17.6 1.3 %collective-permute-start.4 = (bf16[8,32,1024]{2,1,0:T(8,128)(2,1)S(1)}, bf16[8,32,1024]{2,1,0:T(8,128)(2,1)S(1)}, u32[]{:S(2)}, u32[]{:S(2)}) collective-permute-start(bf16[8,32,1024]{2,1,0:T(8,128)(2,1)S(1)} %collective-permute-done.3), channel_id=1, source_target_pairs={{0,2},{4,6},{8,10},{12,14},{16,18},{20,22},{24,26},{28,30},{1,3},{... | collective-permute-start | bytes 1572872 | tf_op jit(solution)/shard_map/ppermute | solution.py:316
  19.0 0.7 convert_bitcast_fusion
  19.6 0.1 pad.1.clone
  19.7 0.1 pad.2.clone
  19.8 0.0 copy-start.8
  19.8 0.1 pad.3.clone
  19.9 0.6 copy-done.8
  20.5 0.0 copy-start.5
  20.5 1.8 %collective-permute-start.5 = (bf16[8,128]{1,0:T(8,128)(2,1)S(1)}, bf16[8,128]{1,0:T(8,128)(2,1)S(1)}, u32[]{:S(2)}, u32[]{:S(2)}) collective-permute-start(bf16[8,128]{1,0:T(8,128)(2,1)S(1)} %maximum_maximum_fusion.refs_1_.refs_2_), channel_id=1, source_target_pairs={{0,1},{1,0},{2,3},{3,2},{4,5},{5,4},{6,7},{7,6},{8,9},{9,8},{10,11... | collective-permute-start | bytes 6152 | tf_op jit(solution)/shard_map/ppermute | solution.py:327
  22.3 1.3 %collective-permute-start = (bf16[8,128]{1,0:T(8,128)(2,1)S(1)}, bf16[8,128]{1,0:T(8,128)(2,1)S(1)}, u32[]{:S(2)}, u32[]{:S(2)}) collective-permute-start(bf16[8,128]{1,0:T(8,128)(2,1)S(1)} %maximum_maximum_fusion.refs_1_.refs_2_), channel_id=1, source_target_pairs={{2,0},{4,2},{6,4},{8,6},{10,8},{12,10},{14,12},{16,14},{18,16},{20... | collective-permute-start | bytes 6152 | tf_op jit(solution)/shard_map/ppermute | solution.py:316
  23.6 0.0 copy-start.11
  23.6 0.6 copy-done.11
  24.2 0.1 pad_add_fusion.1
  24.3 0.6 pad_add_fusion.refs_0_.place_ref
  24.9 2.5 %shard_map.77 = (bf16[512,512]{1,0:T(8,128)(2,1)}, bf16[256,256]{1,0:T(8,128)(2,1)}, bf16[256,256]{1,0:T(8,128)(2,1)}, bf16[256,256]{1,0:T(8,128)(2,1)}, bf16[256,256]{1,0:T(8,128)(2,1)}) custom-call(bf16[256,256]{1,0:T(8,128)(2,1)} %occ_ref.1, bf16[256,256]{1,0:T(8,128)(2,1)} %refs_9_.1), custom_call_target="tpu_custom_call" | custom-call | flops 100000000 | bytes 1000000 | tf_op jit(solution)/shard_map/pallas_call | solution.py:299
  27.4 0.1 dynamic_slice.3
  27.5 0.7 reshape.25.refs_0_.refs_1_
  28.1 0.0 collective-permute-done.5.refs_2_
  28.1 0.0 copy-done.5
  28.1 0.0 copy-start.9
  28.1 1.3 %collective-permute-start.1 = (bf16[8,128]{1,0:T(8,128)(2,1)S(1)}, bf16[8,128]{1,0:T(8,128)(2,1)S(1)}, u32[]{:S(2)}, u32[]{:S(2)}) collective-permute-start(bf16[8,128]{1,0:T(8,128)(2,1)S(1)} %maximum_maximum_fusion.refs_1_.refs_2_), channel_id=1, source_target_pairs={{4,0},{6,2},{8,4},{10,6},{12,8},{14,10},{16,12},{18,14},{20,16},{2... | collective-permute-start | bytes 6152 | tf_op jit(solution)/shard_map/ppermute | solution.py:316
  29.4 0.0 collective-permute-done.6.refs_4_
  29.4 0.0 copy-start
  29.4 0.0 copy-done.9
  29.5 0.8 copy-done
  30.2 14.7 %shard_map.78 = (bf16[8,256,256]{2,1,0:T(8,128)(2,1)}, bf16[8,256,256]{2,1,0:T(8,128)(2,1)}, bf16[8,32,1024]{2,1,0:T(8,128)(2,1)}, bf16[8,32,1024]{2,1,0:T(8,128)(2,1)}) custom-call(s32[2,32]{1,0:T(2,128)} %reshape.25.refs_0_.refs_1_, bf16[8,128]{1,0:T(8,128)(2,1)} %copy-done.5, bf16[8,128]{1,0:T(8,128)(2,1)} %copy-done.9, bf16[8,32,1024]{2,1,0:T(8,128)(2,1)} %refs_3_.1, ...), custom_call_target="tpu_custom_call" | custom-call | flops 100000000 | bytes 1000000 | tf_op jit(solution)/shard_map/pallas_call | solution.py:299
  44.9 0.0 collective-permute-done.refs_3_
  44.9 0.0 copy-start.6
  44.9 0.0 collective-permute-done.1.refs_4_
  44.9 0.0 copy-start.7
  44.9 0.0 collective-permute-done.2
  44.9 0.0 copy-start.2
  45.0 0.0 collective-permute-done.4
  45.0 0.0 copy-start.3
  45.0 0.5 copy-done.6
  45.5 0.0 copy-done.7
  45.5 0.0 copy-done.1
  45.5 0.2 copy-done.2
  45.7 0.2 copy-done.3
  45.9 12.9 %shard_map.79 = (f32[2,144,128]{2,1,0:T(8,128)}, f32[2,144,128]{2,1,0:T(8,128)}) custom-call(s32[2]{0:T(128)} %pad_add_fusion.refs_0_.place_ref, s32[2,32]{1,0:T(2,128)} %reshape.25.refs_0_.refs_1_, bf16[8,128]{1,0:T(8,128)(2,1)} %copy-done.5, bf16[8,128]{1,0:T(8,128)(2,1)} %copy-done.6, bf16[8,128]{1,0:T(8,128)(2,1)} %copy-done.7, ...), custom_call_target="tpu_custom_call" | custom-call | flops 100000000 | bytes 1000000 | tf_op jit(solution)/shard_map/pallas_call | solution.py:299
  58.8 1.0 %collective-permute-start.7 = (f32[2,144,128]{2,1,0:T(8,128)}, f32[2,144,128]{2,1,0:T(8,128)S(1)}, u32[]{:S(2)}, u32[]{:S(2)}) collective-permute-start(f32[2,144,128]{2,1,0:T(8,128)} %get-tuple-element.23), channel_id=1, source_target_pairs={{0,2},{2,0},{4,6},{6,4},{8,10},{10,8},{12,14},{14,12},{16,18},{18,... | collective-permute-start | bytes 442376 | tf_op jit(solution)/shard_map/ppermute | solution.py:332
  59.8 1.2 %collective-permute-done.7 = f32[2,144,128]{2,1,0:T(8,128)S(1)} collective-permute-done((f32[2,144,128]{2,1,0:T(8,128)}, f32[2,144,128]{2,1,0:T(8,128)S(1)}, u32[]{:S(2)}, u32[]{:S(2)}) %collective-permute-start.7) | collective-permute-done | bytes 147488 | tf_op jit(solution)/shard_map/ppermute | solution.py:332
  61.0 0.9 %add.19 = f32[2,144,128]{2,1,0:T(8,128)S(1)} add(f32[2,144,128]{2,1,0:T(8,128)} %get-tuple-element.22, f32[2,144,128]{2,1,0:T(8,128)S(1)} %collective-permute-done.7) | non-fusion elementwise | flops 36864 | bytes 442368 | tf_op jit(solution)/shard_map/add | solution.py:414
  62.0 0.3 collective-permute-start.8
  62.3 4.3 %collective-permute-done.8 = f32[144,128]{1,0:T(8,128)S(1)} collective-permute-done((f32[144,128]{1,0:T(8,128)S(1)}, f32[144,128]{1,0:T(8,128)S(1)}, u32[]{:S(2)}, u32[]{:S(2)}) %collective-permute-start.8) | collective-permute-done | bytes 73760 | tf_op jit(solution)/shard_map/ppermute | solution.py:327
  66.6 3.2 %collective-permute-start.9 = (f32[144,128]{1,0:T(8,128)S(1)}, f32[144,128]{1,0:T(8,128)S(1)}, u32[]{:S(2)}, u32[]{:S(2)}) collective-permute-start(f32[144,128]{1,0:T(8,128)S(1)} %fusion), channel_id=1, source_target_pairs={{0,4},{2,6},{4,0},{6,2},{8,12},{10,14},{12,8},{14,10},{16,20},{18,... | collective-permute-start | bytes 221192 | tf_op jit(solution)/shard_map/ppermute | solution.py:332
  69.8 2.3 %collective-permute-done.9 = f32[144,128]{1,0:T(8,128)S(1)} collective-permute-done((f32[144,128]{1,0:T(8,128)S(1)}, f32[144,128]{1,0:T(8,128)S(1)}, u32[]{:S(2)}, u32[]{:S(2)}) %collective-permute-start.9) | collective-permute-done | bytes 73760 | tf_op jit(solution)/shard_map/ppermute | solution.py:332
  72.1 3.3 %collective-permute-start.10 = (f32[144,128]{1,0:T(8,128)S(1)}, f32[144,128]{1,0:T(8,128)S(1)}, u32[]{:S(2)}, u32[]{:S(2)}) collective-permute-start(f32[144,128]{1,0:T(8,128)S(1)} %add.21), channel_id=1, source_target_pairs={{0,8},{2,10},{4,12},{6,14},{8,0},{10,2},{12,4},{14,6},{16,24},{18,... | collective-permute-start | bytes 221192 | tf_op jit(solution)/shard_map/ppermute | solution.py:332
  75.4 2.3 %collective-permute-done.10 = f32[144,128]{1,0:T(8,128)S(1)} collective-permute-done((f32[144,128]{1,0:T(8,128)S(1)}, f32[144,128]{1,0:T(8,128)S(1)}, u32[]{:S(2)}, u32[]{:S(2)}) %collective-permute-start.10) | collective-permute-done | bytes 73760 | tf_op jit(solution)/shard_map/ppermute | solution.py:332
  77.8 3.4 %collective-permute-start.11 = (f32[144,128]{1,0:T(8,128)S(1)}, f32[144,128]{1,0:T(8,128)S(1)}, u32[]{:S(2)}, u32[]{:S(2)}) collective-permute-start(f32[144,128]{1,0:T(8,128)S(1)} %add.22), channel_id=1, source_target_pairs={{0,16},{2,18},{4,20},{6,22},{8,24},{10,26},{12,28},{14,30},{16,0},... | collective-permute-start | bytes 221192 | tf_op jit(solution)/shard_map/ppermute | solution.py:332
  81.2 2.3 %collective-permute-done.11 = f32[144,128]{1,0:T(8,128)S(1)} collective-permute-done((f32[144,128]{1,0:T(8,128)S(1)}, f32[144,128]{1,0:T(8,128)S(1)}, u32[]{:S(2)}, u32[]{:S(2)}) %collective-permute-start.11) | collective-permute-done | bytes 73760 | tf_op jit(solution)/shard_map/ppermute | solution.py:332
  83.5 0.0 copy-start.4
  83.5 0.1 collective-permute-start.12
  83.6 1.3 %collective-permute-done.12.other_ref = f32[144,128]{1,0:T(8,128)S(1)} collective-permute-done((f32[144,128]{1,0:T(8,128)S(1)}, f32[144,128]{1,0:T(8,128)S(1)}, u32[]{:S(2)}, u32[]{:S(2)}) %collective-permute-start.12) | collective-permute-done | bytes 73760 | tf_op jit(solution)/shard_map/ppermute | solution.py:332
  84.9 0.0 copy-done.4
  84.9 0.0 copy-start.10
  84.9 0.6 copy-done.10
  85.5 1.7 %shard_map.80 = (f32[8,20]{1,0:T(8,128)}, f32[32,1024]{1,0:T(8,128)}) custom-call(s32[2]{0:T(128)} %pad_add_fusion.refs_0_.place_ref, f32[144,128]{1,0:T(8,128)} %copy-done.4, f32[144,128]{1,0:T(8,128)} %copy-done.10), custom_call_target="tpu_custom_call" | custom-call | flops 100000000 | bytes 1000000 | tf_op jit(solution)/shard_map/pallas_call | solution.py:299
  (8 shorter events, 0.1 us)
Async XLA Ops:
  0.6 17.0 %collective-permute-start.3 = (bf16[8,32,1024]{2,1,0:T(8,128)(2,1)}, bf16[8,32,1024]{2,1,0:T(8,128)(2,1)S(1)}, u32[]{:S(2)}, u32[]{:S(2)}) collective-permute-start(bf16[8,32,1024]{2,1,0:T(8,128)(2,1)} %refs_3_.1), channel_id=1, source_target_pairs={{4,0},{6,2},{8,4},{10,6},{12,8},{14,10},{16,12},{18,14},{20,16},{2... | collective-permute-start | bytes 1572872 | tf_op jit(solution)/shard_map/ppermute | solution.py:316
  1.9 27.5 %collective-permute-start.6 = (bf16[8,32,1024]{2,1,0:T(8,128)(2,1)}, bf16[8,32,1024]{2,1,0:T(8,128)(2,1)S(1)}, u32[]{:S(2)}, u32[]{:S(2)}) collective-permute-start(bf16[8,32,1024]{2,1,0:T(8,128)(2,1)} %refs_3_.1), channel_id=1, source_target_pairs={{0,1},{1,0},{2,3},{3,2},{4,5},{5,4},{6,7},{7,6},{8,9},{9,8},{10,11... | collective-permute-start | bytes 1572872 | tf_op jit(solution)/shard_map/ppermute | solution.py:327
  5.0 39.9 %collective-permute-start.2 = (bf16[8,32,1024]{2,1,0:T(8,128)(2,1)}, bf16[8,32,1024]{2,1,0:T(8,128)(2,1)S(1)}, u32[]{:S(2)}, u32[]{:S(2)}) collective-permute-start(bf16[8,32,1024]{2,1,0:T(8,128)(2,1)} %refs_3_.1), channel_id=1, source_target_pairs={{2,0},{6,4},{10,8},{14,12},{18,16},{22,20},{26,24},{30,28},{3,1},{... | collective-permute-start | bytes 1572872 | tf_op jit(solution)/shard_map/ppermute | solution.py:316
  17.6 27.9 %copy-start.1 = (bf16[8,32,1024]{2,1,0:T(8,128)(2,1)}, bf16[8,32,1024]{2,1,0:T(8,128)(2,1)S(1)}, u32[]{:S(2)}) copy-start(bf16[8,32,1024]{2,1,0:T(8,128)(2,1)S(1)} %collective-permute-done.3) | copy-start | bytes 1572868
  17.6 27.3 %collective-permute-start.4 = (bf16[8,32,1024]{2,1,0:T(8,128)(2,1)S(1)}, bf16[8,32,1024]{2,1,0:T(8,128)(2,1)S(1)}, u32[]{:S(2)}, u32[]{:S(2)}) collective-permute-start(bf16[8,32,1024]{2,1,0:T(8,128)(2,1)S(1)} %collective-permute-done.3), channel_id=1, source_target_pairs={{0,2},{4,6},{8,10},{12,14},{16,18},{20,22},{24,26},{28,30},{1,3},{... | collective-permute-start | bytes 1572872 | tf_op jit(solution)/shard_map/ppermute | solution.py:316
  19.8 0.7 copy-start.8
  20.5 7.7 %copy-start.5 = (bf16[8,128]{1,0:T(8,128)(2,1)}, bf16[8,128]{1,0:T(8,128)(2,1)S(1)}, u32[]{:S(2)}) copy-start(bf16[8,128]{1,0:T(8,128)(2,1)S(1)} %maximum_maximum_fusion.refs_1_.refs_2_) | copy-start | bytes 6148
  20.5 7.7 %collective-permute-start.5 = (bf16[8,128]{1,0:T(8,128)(2,1)S(1)}, bf16[8,128]{1,0:T(8,128)(2,1)S(1)}, u32[]{:S(2)}, u32[]{:S(2)}) collective-permute-start(bf16[8,128]{1,0:T(8,128)(2,1)S(1)} %maximum_maximum_fusion.refs_1_.refs_2_), channel_id=1, source_target_pairs={{0,1},{1,0},{2,3},{3,2},{4,5},{5,4},{6,7},{7,6},{8,9},{9,8},{10,11... | collective-permute-start | bytes 6152 | tf_op jit(solution)/shard_map/ppermute | solution.py:327
  22.3 22.6 %collective-permute-start = (bf16[8,128]{1,0:T(8,128)(2,1)S(1)}, bf16[8,128]{1,0:T(8,128)(2,1)S(1)}, u32[]{:S(2)}, u32[]{:S(2)}) collective-permute-start(bf16[8,128]{1,0:T(8,128)(2,1)S(1)} %maximum_maximum_fusion.refs_1_.refs_2_), channel_id=1, source_target_pairs={{2,0},{4,2},{6,4},{8,6},{10,8},{12,10},{14,12},{16,14},{18,16},{20... | collective-permute-start | bytes 6152 | tf_op jit(solution)/shard_map/ppermute | solution.py:316
  23.6 0.7 copy-start.11
  28.1 1.3 %copy-start.9 = (bf16[8,128]{1,0:T(8,128)(2,1)}, bf16[8,128]{1,0:T(8,128)(2,1)S(1)}, u32[]{:S(2)}) copy-start(bf16[8,128]{1,0:T(8,128)(2,1)S(1)} %collective-permute-done.5.refs_2_) | copy-start | bytes 6148
  28.1 16.8 %collective-permute-start.1 = (bf16[8,128]{1,0:T(8,128)(2,1)S(1)}, bf16[8,128]{1,0:T(8,128)(2,1)S(1)}, u32[]{:S(2)}, u32[]{:S(2)}) collective-permute-start(bf16[8,128]{1,0:T(8,128)(2,1)S(1)} %maximum_maximum_fusion.refs_1_.refs_2_), channel_id=1, source_target_pairs={{4,0},{6,2},{8,4},{10,6},{12,8},{14,10},{16,12},{18,14},{20,16},{2... | collective-permute-start | bytes 6152 | tf_op jit(solution)/shard_map/ppermute | solution.py:316
  29.4 0.8 copy-start
  44.9 0.6 copy-start.6
  44.9 0.6 copy-start.7
  44.9 0.8 copy-start.2
  45.0 1.0 %copy-start.3 = (bf16[8,32,1024]{2,1,0:T(8,128)(2,1)}, bf16[8,32,1024]{2,1,0:T(8,128)(2,1)S(1)}, u32[]{:S(2)}) copy-start(bf16[8,32,1024]{2,1,0:T(8,128)(2,1)S(1)} %collective-permute-done.4) | copy-start | bytes 1572868
  58.8 2.2 %collective-permute-start.7 = (f32[2,144,128]{2,1,0:T(8,128)}, f32[2,144,128]{2,1,0:T(8,128)S(1)}, u32[]{:S(2)}, u32[]{:S(2)}) collective-permute-start(f32[2,144,128]{2,1,0:T(8,128)} %get-tuple-element.23), channel_id=1, source_target_pairs={{0,2},{2,0},{4,6},{6,4},{8,10},{10,8},{12,14},{14,12},{16,18},{18,... | collective-permute-start | bytes 442376 | tf_op jit(solution)/shard_map/ppermute | solution.py:332
  62.0 4.6 %collective-permute-start.8 = (f32[144,128]{1,0:T(8,128)S(1)}, f32[144,128]{1,0:T(8,128)S(1)}, u32[]{:S(2)}, u32[]{:S(2)}) collective-permute-start(f32[144,128]{1,0:T(8,128)S(1)} %slice_bitcast_fusion), channel_id=1, source_target_pairs={{0,1},{1,0},{2,3},{3,2},{4,5},{5,4},{6,7},{7,6},{8,9},{9,8},{10,11... | collective-permute-start | bytes 221192 | tf_op jit(solution)/shard_map/ppermute | solution.py:327
  66.6 5.5 %collective-permute-start.9 = (f32[144,128]{1,0:T(8,128)S(1)}, f32[144,128]{1,0:T(8,128)S(1)}, u32[]{:S(2)}, u32[]{:S(2)}) collective-permute-start(f32[144,128]{1,0:T(8,128)S(1)} %fusion), channel_id=1, source_target_pairs={{0,4},{2,6},{4,0},{6,2},{8,12},{10,14},{12,8},{14,10},{16,20},{18,... | collective-permute-start | bytes 221192 | tf_op jit(solution)/shard_map/ppermute | solution.py:332
  72.1 5.6 %collective-permute-start.10 = (f32[144,128]{1,0:T(8,128)S(1)}, f32[144,128]{1,0:T(8,128)S(1)}, u32[]{:S(2)}, u32[]{:S(2)}) collective-permute-start(f32[144,128]{1,0:T(8,128)S(1)} %add.21), channel_id=1, source_target_pairs={{0,8},{2,10},{4,12},{6,14},{8,0},{10,2},{12,4},{14,6},{16,24},{18,... | collective-permute-start | bytes 221192 | tf_op jit(solution)/shard_map/ppermute | solution.py:332
  77.8 5.8 %collective-permute-start.11 = (f32[144,128]{1,0:T(8,128)S(1)}, f32[144,128]{1,0:T(8,128)S(1)}, u32[]{:S(2)}, u32[]{:S(2)}) collective-permute-start(f32[144,128]{1,0:T(8,128)S(1)} %add.22), channel_id=1, source_target_pairs={{0,16},{2,18},{4,20},{6,22},{8,24},{10,26},{12,28},{14,30},{16,0},... | collective-permute-start | bytes 221192 | tf_op jit(solution)/shard_map/ppermute | solution.py:332
  83.5 1.3 %copy-start.4 = (f32[144,128]{1,0:T(8,128)}, f32[144,128]{1,0:T(8,128)S(1)}, u32[]{:S(2)}) copy-start(f32[144,128]{1,0:T(8,128)S(1)} %add.23.own_ref) | copy-start | bytes 221188
  83.5 1.3 %collective-permute-start.12 = (f32[144,128]{1,0:T(8,128)S(1)}, f32[144,128]{1,0:T(8,128)S(1)}, u32[]{:S(2)}, u32[]{:S(2)}) collective-permute-start(f32[144,128]{1,0:T(8,128)S(1)} %add.23.own_ref), channel_id=1, source_target_pairs={{0,2},{2,0},{4,6},{6,4},{8,10},{10,8},{12,14},{14,12},{16,18},{18,... | collective-permute-start | bytes 221192 | tf_op jit(solution)/shard_map/ppermute | solution.py:332
  84.9 0.6 copy-start.10

commit v2 on v1

--- a/solution.py
+++ b/solution.py
@@ -6,6 +6,7 @@
 from jax.experimental import pallas as pl
 from jax.experimental.pallas import tpu as pltpu
 from jax.sharding import PartitionSpec as P
+
 
 OA = 32
 NAT = 8
@@ -17,6 +18,7 @@
 RQ = LANE // OA
 NQ = OA // RQ
 LIVE_AT = 64
+CHUNKS = (4, 4)
 BF = jnp.bfloat16
 F4 = jnp.float32
 
@@ -63,10 +65,6 @@
     return out[:count] + out[count : 2 * count] + out[2 * count :]
 
 
-def pick_rows(count):
-    return -(-count // LANE) * BLK
-
-
 def slot_onehot(pair_row):
     count = pair_row.shape[1]
     slot = iota((NAT * NAT, count), 0)
@@ -74,56 +72,83 @@
     return mod(slot, NAT) * NAT + second == pair_row
 
 
+def pair_row(pairs_ref, place_ref, step):
+    at = mod(place_ref[1] + step, pairs_ref.shape[0])
+    return pairs_ref[pl.ds(at, 1), :]
+
+
 def to_matrix(tiles, swap):
     rows = [
         jnp.concatenate(
-            [tiles[i * 2 * NAT : (i + 1) * 2 * NAT, q * LANE : (q + 1) * LANE] for i in range(RQ)],
+            [t[i * 2 * NAT : (i + 1) * 2 * NAT, q * LANE : (q + 1) * LANE] for i in range(RQ)],
             axis=1,
         )
+        for t in tiles
         for q in range(NQ)
     ]
     mixed = mm(jnp.concatenate(rows, axis=0), swap)
-    out = [
-        jnp.concatenate(
-            [
-                mixed[(q * 2 + g) * NAT : (q * 2 + g + 1) * NAT, i * LANE : (i + 1) * LANE]
-                for g in range(2)
-            ],
-            axis=1,
-        )
-        for i in range(RQ)
-        for q in range(NQ)
-    ]
-    return jnp.concatenate(out, axis=0).astype(BF)
-
-
-def from_matrix(matrix, swap):
+    out = []
+    for n in range(len(tiles)):
+        part = mixed[n * 2 * NQ * NAT : (n + 1) * 2 * NQ * NAT]
+        blocks = [
+            jnp.concatenate(
+                [
+                    part[(q * 2 + g) * NAT : (q * 2 + g + 1) * NAT, i * LANE : (i + 1) * LANE]
+                    for g in range(2)
+                ],
+                axis=1,
+            )
+            for i in range(RQ)
+            for q in range(NQ)
+        ]
+        out.append(jnp.concatenate(blocks, axis=0).astype(BF))
+    return out
+
+
+def from_matrix(matrices, swap):
     rows = [
         jnp.concatenate(
             [
-                matrix[(i * NQ + q) * NAT : (i * NQ + q + 1) * NAT, g * LANE : (g + 1) * LANE]
+                m[(i * NQ + q) * NAT : (i * NQ + q + 1) * NAT, g * LANE : (g + 1) * LANE]
                 for i in range(RQ)
             ],
             axis=1,
         )
+        for m in matrices
         for q in range(NQ)
         for g in range(2)
     ]
     mixed = mm(jnp.concatenate(rows, axis=0).astype(BF), swap).astype(BF)
-    out = [
-        jnp.concatenate(
-            [
-                mixed[q * 2 * NAT : (q + 1) * 2 * NAT, i * LANE : (i + 1) * LANE]
-                for q in range(NQ)
-            ],
-            axis=1,
-        )
-        for i in range(RQ)
-    ]
-    return jnp.concatenate(out, axis=0)
-
-
-def tables_kernel(occ_ref, vir_ref, swap_ref, both_ref, both_t_ref, cols_ref, vir_t_ref):
+    out = []
+    for n in range(len(matrices)):
+        part = mixed[n * 2 * NQ * NAT : (n + 1) * 2 * NQ * NAT]
+        out.append(
+            jnp.concatenate(
+                [
+                    jnp.concatenate(
+                        [
+                            part[q * 2 * NAT : (q + 1) * 2 * NAT, i * LANE : (i + 1) * LANE]
+                            for q in range(NQ)
+                        ],
+                        axis=1,
+                    )
+                    for i in range(RQ)
+                ],
+                axis=0,
+            )
+        )
+    return out
+
+
+def tables_kernel(
+    occ_ref, vir_ref, screened_ref, live_ref, meta_ref, swap_ref, both_ref, cols_ref, vir_t_ref
+):
+    own_count = live_ref.shape[1]
+    meta_ref[...] = jnp.zeros(meta_ref.shape, BF)
+    meta_ref[:, : screened_ref.shape[1]] = screened_ref[...]
+    meta_ref[:, LIVE_AT : LIVE_AT + own_count] = jnp.broadcast_to(
+        live_ref[...].astype(F4), (BLK, own_count)
+    ).astype(BF)
     size = RQ * LANE
     row = iota((size, size), 0)
     col = iota((size, size), 1)
@@ -137,39 +162,52 @@
     cols = mm_nt(occ, order).astype(BF)
     both = mm(order, cols)
     cols_ref[...] = cols
-    both_ref[...] = both.astype(BF)
-    both_t_ref[...] = both.T.astype(BF)
+    both_ref[:NORB] = both.T.astype(BF)
+    both_ref[NORB:] = both.astype(BF)
     vir_t_ref[...] = vir_ref[...].astype(F4).T.astype(BF)
 
 
-def own_kernel(count, *refs):
-    pairs_ref, metas = refs[0], refs[1 : 1 + count]
-    pieces = refs[1 + count : 1 + 2 * count]
-    swap_ref, both_ref, both_t_ref, cols_ref, vir_ref, vir_t_ref = refs[1 + 2 * count : 7 + 2 * count]
-    matrix_ref, right_ref, z_ref, y_ref = refs[7 + 2 * count :]
-    own_count = pieces[0].shape[1]
+def own_kernel(count, first, place_ref, pairs_ref, *refs):
+    metas, pieces = refs[:count], refs[count : 2 * count]
+    swap_ref, both_ref, cols_ref, vir_ref, vir_t_ref = refs[2 * count : 2 * count + 5]
+    matrix_ref, right_ref, z_ref, y_ref = refs[2 * count + 5 :]
+    group, own_count = matrix_ref.shape[0], pieces[0].shape[1]
     swap = swap_ref[...]
-    tiles = None
+    selects = []
     for s in range(count):
         live = metas[s][0:1, LIVE_AT : LIVE_AT + own_count].astype(F4)
-        select = (slot_onehot(pairs_ref[s : s + 1, :]).astype(F4) * live).astype(BF)
-        part = mm(select, pieces[s][0])
-        tiles = part if tiles is None else tiles + part
-    own_select = onehot(slot_onehot(pairs_ref[0:1, :]))
-    matrix = to_matrix(tiles.astype(BF), swap)
-    matrix_ref[0] = matrix
-    right_ref[0] = mm(matrix, cols_ref[...]).astype(BF)
-    left = mm(both_t_ref[...], matrix).astype(BF)
-    z_tiles = from_matrix(mm(left, vir_ref[...]), swap)
-    z_ref[0] = mm_tn(own_select, z_tiles).astype(BF)
-    left = mm(both_ref[...], matrix).astype(BF)
-    y_tiles = from_matrix(mm(left, vir_t_ref[...]), swap)
-    y_ref[0] = mm_tn(own_select, y_tiles).astype(BF)
+        select = slot_onehot(pair_row(pairs_ref, place_ref, s)).astype(F4)
+        selects.append((select * live).astype(BF))
+    tiles = []
+    for p in range(group):
+        total = mm(selects[0], pieces[0][first + p])
+        for s in range(1, count):
+            total = total + mm(selects[s], pieces[s][first + p])
+        tiles.append(total.astype(BF))
+    own_select = slot_onehot(pair_row(pairs_ref, place_ref, 0)).astype(F4).T.astype(BF)
+    matrices = to_matrix(tiles, swap)
+    right = mm(jnp.concatenate(matrices, axis=0), cols_ref[...]).astype(BF)
+    both = both_ref[...]
+    lefts = [mm(both, m).astype(BF) for m in matrices]
+    z = mm(jnp.concatenate([left[:NORB] for left in lefts], axis=0), vir_ref[...])
+    y = mm(jnp.concatenate([left[NORB:] for left in lefts], axis=0), vir_t_ref[...])
+    for value, ref in ((z, z_ref), (y, y_ref)):
+        parts = from_matrix([value[p * NORB : (p + 1) * NORB] for p in range(group)], swap)
+        for p in range(group):
+            ref[p * own_count : (p + 1) * own_count] = mm(own_select, parts[p]).astype(BF)
+    for p in range(group):
+        matrix_ref[p] = matrices[p]
+        right_ref[p] = right[p * NORB : (p + 1) * NORB]
 
 
 def window_kernel(lanes, sigma_scale, chi_scale, place_ref, *refs):
     (pairs_ref, meta0, meta1, meta2, tile0, tile1a, tile1b, tile2) = refs[:8]
-    (z_ref, y_ref, matrix_ref, right_ref, swap_ref, cols_ref, keep_ref, send_ref) = refs[8:]
+    swap_ref, cols_ref = refs[8:10]
+    own, (keep_ref, send_ref) = refs[10:-2], refs[-2:]
+    matrices = [ref[p] for ref in own[::4] for p in range(ref.shape[0])]
+    rights = [ref[p] for ref in own[1::4] for p in range(ref.shape[0])]
+    z = jnp.concatenate([ref[...] for ref in own[2::4]], axis=0)
+    y = jnp.concatenate([ref[...] for ref in own[3::4]], axis=0)
     pair_count, own_count = pairs_ref.shape
     rows = BLK * own_count
     block, pair_at = place_ref[0], place_ref[1]
@@ -198,22 +236,26 @@
     mixed = mixed.astype(BF)
     other = other.astype(BF)
     swap = swap_ref[...]
-    own_select = onehot(slot_onehot(pairs_ref[0:1, :]))
-    total = jnp.zeros((NORB, NORB), F4)
-    for r in range(BLK):
-        at = slice(r * own_count, (r + 1) * own_count)
-        value = to_matrix(mm(own_select, mixed[at]).astype(BF), swap)
-        scaled = mm(value, cols_ref[...]).astype(BF)
-        total = total + mm(scaled, matrix_ref[r])
-        value = to_matrix(mm(own_select, other[at]).astype(BF), swap)
-        total = total + mm(right_ref[r], value)
+    own_select = onehot(slot_onehot(pair_row(pairs_ref, place_ref, 0)))
+    parts = [
+        mm(own_select, value[r * own_count : (r + 1) * own_count]).astype(BF)
+        for value in (mixed, other)
+        for r in range(BLK)
+    ]
+    values = to_matrix(parts, swap)
+    scaled = mm(jnp.concatenate(values[:BLK], axis=0), cols_ref[...]).astype(BF)
+    lefts = [scaled[r * NORB : (r + 1) * NORB] for r in range(BLK)]
+    total = mm(
+        jnp.concatenate(lefts + rights, axis=1),
+        jnp.concatenate(matrices + values[BLK:], axis=0),
+    )
     total = total * -sigma_scale
     high = total.astype(BF).astype(F4)
-    parts = [from_matrix(high, swap), from_matrix(total - high, swap)]
+    parts = from_matrix([high, total - high], swap)
     parity = block & 1
     half = own_count // 2
     for s in range(pair_count):
-        select = onehot(slot_onehot(pairs_ref[s : s + 1, :]))
+        select = onehot(slot_onehot(pair_row(pairs_ref, place_ref, s)))
         owned = mm_tn(select, parts[0]) + mm_tn(select, parts[1])
         first, second = owned[:half], owned[half:]
         keep = jnp.where(parity == 0, first, second)
@@ -226,9 +268,9 @@
     for t in range(-REACH, REACH + 1):
         w = abs(t)
         if t < 0:
-            cross = mm_nt(tiles[w], y_ref[...])
+            cross = mm_nt(tiles[w], y)
         else:
-            cross = mm_nt(z_ref[...], tiles[w])
+            cross = mm_nt(z, tiles[w])
         cross = cross * masks[w]
         sums = jnp.concatenate(
             [
@@ -284,23 +326,15 @@
     chi_ref[...] = total[:, :share]
 
 
-def call(body, outs, *args, grid=None, in_specs=None, out_specs=None, flops=10**8):
-    extra = {}
-    if grid is not None:
-        extra = dict(grid=grid, in_specs=in_specs, out_specs=out_specs)
-    else:
-        full = pl.BlockSpec(memory_space=pltpu.VMEM)
-        extra = dict(
-            in_specs=[
-                pl.BlockSpec(memory_space=pltpu.SMEM) if a.ndim == 1 else full for a in args
-            ],
-            out_specs=jax.tree.map(lambda o: full, outs),
-        )
+def call(body, outs, *args, flops=10**8):
+    full = pl.BlockSpec(memory_space=pltpu.VMEM)
     return pl.pallas_call(
         body,
         out_shape=outs,
+        in_specs=[pl.BlockSpec(memory_space=pltpu.SMEM) if a.ndim == 1 else full for a in args],
+        out_specs=jax.tree.map(lambda o: full, outs),
         cost_estimate=pl.CostEstimate(flops=flops, bytes_accessed=10**6, transcendentals=0),
-        **extra,
+        compiler_params=pltpu.CompilerParams(vmem_limit_bytes=24 << 20),
     )(*args)
 
 
@@ -331,61 +365,53 @@
     def flipped(value, mask):
         return lax.ppermute(value, "aux", [(s, s ^ mask) for s in range(aux_count)])
 
-    live = jnp.broadcast_to(tile_live.astype(BF), (block_rows, own_count))
-    meta = jnp.concatenate(
-        [
-            screened,
-            jnp.zeros((block_rows, LIVE_AT - window), BF),
-            live,
-            jnp.zeros((block_rows, LANE - LIVE_AT - own_count), BF),
-        ],
-        axis=1,
-    )
     far = shifted(three_center, -2)
+    firsts = [sum(CHUNKS[:c]) for c in range(len(CHUNKS))]
     pieces = [three_center] + [turned(three_center, s) for s in range(1, pair_count)]
     near_even = shifted(three_center, -1, 1)
-    metas = [meta] + [turned(meta, s) for s in range(1, pair_count)]
-    meta_near, meta_far = shifted(meta, -1), shifted(meta, -2)
-    near_odd = shifted(far, 1, 0)
-    pairs = lax.dynamic_slice_in_dim(
-        jnp.concatenate([pair_atoms, pair_atoms]), pair_at * own_count, pair_count * own_count
-    ).reshape(pair_count, own_count)
-    place = jnp.stack([block, pair_at]).astype(jnp.int32)
-
     square = shape((NORB, NORB), BF)
-    swap, both, both_t, cols, vir_t = call(
+    meta, swap, both, cols, vir_t = call(
         tables_kernel,
-        [shape((RQ * LANE, RQ * LANE), BF), square, square, square, square],
+        [
+            shape((block_rows, LANE), BF),
+            shape((RQ * LANE, RQ * LANE), BF),
+            shape((2 * NORB, NORB), BF),
+            square,
+            square,
+        ],
         green_occ,
         green_vir,
-    )
-
-    def whole(value):
-        return pl.BlockSpec(value.shape, lambda p: (0,) * value.ndim)
-
-    def one(a, b):
-        return pl.BlockSpec((1, a, b), lambda p: (p, 0, 0))
-
-    fixed = [swap, both, both_t, cols, green_vir, vir_t]
-    matrix, right, z, y = call(
-        lambda *refs: own_kernel(pair_count, *refs),
-        [
-            shape((block_rows, NORB, NORB), BF),
-            shape((block_rows, NORB, NORB), BF),
-            shape((block_rows, own_count, PAIR), BF),
-            shape((block_rows, own_count, PAIR), BF),
-        ],
-        pairs,
-        *metas,
-        *pieces,
-        *fixed,
-        grid=(block_rows,),
-        in_specs=[whole(pairs)]
-        + [whole(m) for m in metas]
-        + [one(own_count, PAIR) for _ in pieces]
-        + [whole(f) for f in fixed],
-        out_specs=[one(NORB, NORB), one(NORB, NORB), one(own_count, PAIR), one(own_count, PAIR)],
-    )
+        screened,
+        tile_live,
+    )
+    metas = [meta] + [turned(meta, s) for s in range(1, pair_count)]
+    meta_near = shifted(meta, -1)
+    meta_far = shifted(meta, -2)
+    near_odd = shifted(far, 1, 0)
+    pairs = pair_atoms.reshape(pair_count, own_count)
+    place = jnp.stack([block, pair_at]).astype(jnp.int32)
+    own = []
+    for c, first in enumerate(firsts):
+        own.append(
+            call(
+                lambda *refs, first=first: own_kernel(pair_count, first, *refs),
+                [
+                    shape((CHUNKS[c], NORB, NORB), BF),
+                    shape((CHUNKS[c], NORB, NORB), BF),
+                    shape((CHUNKS[c] * own_count, PAIR), BF),
+                    shape((CHUNKS[c] * own_count, PAIR), BF),
+                ],
+                place,
+                pairs,
+                *metas,
+                *pieces,
+                swap,
+                both,
+                cols,
+                green_vir,
+                vir_t,
+            )
+        )
 
     lanes = -(-(aux_count // 2) * (window // pair_count) // LANE) * LANE
     message = shape((pair_count, own_count // 2 * NQ + lanes // LANE * BLK, LANE), F4)
@@ -404,12 +430,9 @@
         near_even.reshape(rows, PAIR),
         near_odd.reshape(rows, PAIR),
         far.reshape(rows, PAIR),
-        z.reshape(rows, PAIR),
-        y.reshape(rows, PAIR),
-        matrix,
-        right,
         swap,
         cols,
+        *[value for values in own for value in values],
     )
     total = keep + flipped(send, 1)
     owned = total[0]

time: 87.5 us -> 69.2 us (0.79)
  Pallas kernels: 31.7 us -> 15.4 us
  other arithmetic: 2.29 us -> 0.13 us
    pallas_call x4 -> x5, Pallas kernels: 31.7 us -> 15.4 us  [call(): pl.pallas_call(body, out_shape=outs, in_specs=[pl.BlockSpec(memory_space=...]
    unnamed x24 -> x16, local copies, waits for them, and re-layouts: 3.63 us -> 4.76 us
    add x1, other arithmetic: 0.93 us -> 0.02 us  [per_device(): total = keep + flipped(send, 1)]
  transfers between devices with their start and end apart: 13 -> 13, of which waited for: 7 -> 7; matrix products, arithmetic and copies ran while one was open for 3% -> 0% of each run, Pallas kernels for 20% -> 10%
where the time goes in v2:
time: 69.2 us; the launch traced here: 68.9 us
  waiting for transfers between devices  24.4 us (35%)
  starting transfers between devices  23.2 us (34%)
  Pallas kernels  15.4 us (22%)
  local copies, waits for them, and re-layouts  4.85 us (7%)
  between operations  0.83 us (1%)
    pallas_call x5, Pallas kernels, call(): pl.pallas_call(body, out_shape=outs, in_specs=[pl.BlockSpec(memory_space=...  15.4 us
    ppermute x5, waiting for transfers between devices, shifted(): lax.ppermute(value, 'aux', [(s, s + steps) for s in range(aux_count) if 0...  11.4 us
    ppermute x5, starting transfers between devices, flipped(): return lax.ppermute(value, 'aux', [(s, s ^ mask) for s in range(aux_count)])  11.1 us
    ppermute x5, waiting for transfers between devices, flipped(): return lax.ppermute(value, 'aux', [(s, s ^ mask) for s in range(aux_count)])  9.26 us
    ppermute x5, starting transfers between devices, shifted(): lax.ppermute(value, 'aux', [(s, s + steps) for s in range(aux_count) if 0...  6.44 us
    ppermute x3, starting transfers between devices, turned(): lax.ppermute(value, 'pair', [(s, (s - steps) % pair_count) for s in range...  5.72 us
    unnamed x16, local copies, waits for them, and re-layouts  4.76 us
    ppermute x3, waiting for transfers between devices, turned(): lax.ppermute(value, 'pair', [(s, (s - steps) % pair_count) for s in range...  3.77 us
  transfers between devices with their start and end apart: 13, of which 7 were waited for; matrix products, arithmetic and copies ran while one was open for 0% of the time, Pallas kernels for 10%

profile of v2, /device:TPU:0, one launch (start us, length us, event | category | flops | bytes accessed | tf_op | source)
XLA Modules:
  0.0 68.9 jit_solution(11682271371873379767)
XLA Ops:
  0.6 1.3 %collective-permute-start.3 = (bf16[8,32,1024]{2,1,0:T(8,128)(2,1)}, bf16[8,32,1024]{2,1,0:T(8,128)(2,1)S(1)}, u32[]{:S(2)}, u32[]{:S(2)}) collective-permute-start(bf16[8,32,1024]{2,1,0:T(8,128)(2,1)} %refs_4_.3), channel_id=1, source_target_pairs={{4,0},{6,2},{8,4},{10,6},{12,8},{14,10},{16,12},{18,14},{20,16},{2... | collective-permute-start | bytes 1572872 | tf_op jit(solution)/shard_map/ppermute | solution.py:350
  1.9 3.1 %collective-permute-start.6 = (bf16[8,32,1024]{2,1,0:T(8,128)(2,1)}, bf16[8,32,1024]{2,1,0:T(8,128)(2,1)S(1)}, u32[]{:S(2)}, u32[]{:S(2)}) collective-permute-start(bf16[8,32,1024]{2,1,0:T(8,128)(2,1)} %refs_4_.3), channel_id=1, source_target_pairs={{0,1},{1,0},{2,3},{3,2},{4,5},{5,4},{6,7},{7,6},{8,9},{9,8},{10,11... | collective-permute-start | bytes 1572872 | tf_op jit(solution)/shard_map/ppermute | solution.py:361
  5.0 1.3 %collective-permute-start.2 = (bf16[8,32,1024]{2,1,0:T(8,128)(2,1)}, bf16[8,32,1024]{2,1,0:T(8,128)(2,1)S(1)}, u32[]{:S(2)}, u32[]{:S(2)}) collective-permute-start(bf16[8,32,1024]{2,1,0:T(8,128)(2,1)} %refs_4_.3), channel_id=1, source_target_pairs={{2,0},{6,4},{10,8},{14,12},{18,16},{22,20},{26,24},{30,28},{3,1},{... | collective-permute-start | bytes 1572872 | tf_op jit(solution)/shard_map/ppermute | solution.py:350
  6.3 11.4 %collective-permute-done.3 = bf16[8,32,1024]{2,1,0:T(8,128)(2,1)S(1)} collective-permute-done((bf16[8,32,1024]{2,1,0:T(8,128)(2,1)}, bf16[8,32,1024]{2,1,0:T(8,128)(2,1)S(1)}, u32[]{:S(2)}, u32[]{:S(2)}) %collective-permute-start.3) | collective-permute-done | bytes 524320 | tf_op jit(solution)/shard_map/ppermute | solution.py:350
  17.6 1.3 %collective-permute-start.4 = (bf16[8,32,1024]{2,1,0:T(8,128)(2,1)S(1)}, bf16[8,32,1024]{2,1,0:T(8,128)(2,1)S(1)}, u32[]{:S(2)}, u32[]{:S(2)}) collective-permute-start(bf16[8,32,1024]{2,1,0:T(8,128)(2,1)S(1)} %collective-permute-done.3), channel_id=1, source_target_pairs={{0,2},{4,6},{8,10},{12,14},{16,18},{20,22},{24,26},{28,30},{1,3},{... | collective-permute-start | bytes 1572872 | tf_op jit(solution)/shard_map/ppermute | solution.py:350
  19.0 0.0 copy-start.2
  19.0 0.9 %copy-done.2 = bf16[256,256]{1,0:T(8,128)(2,1)S(1)} copy-done((bf16[256,256]{1,0:T(8,128)(2,1)S(1)}, bf16[256,256]{1,0:T(8,128)(2,1)}, u32[]{:S(2)}) %copy-start.2) | copy-done | bytes 131096
  19.9 0.0 copy-start.4
  19.9 0.9 %copy-done.4 = bf16[256,256]{1,0:T(8,128)(2,1)S(1)} copy-done((bf16[256,256]{1,0:T(8,128)(2,1)S(1)}, bf16[256,256]{1,0:T(8,128)(2,1)}, u32[]{:S(2)}) %copy-start.4) | copy-done | bytes 131096
  20.8 0.0 copy-start.5
  20.8 0.7 copy-done.5
  21.4 0.0 copy-start.6
  21.4 0.7 copy-done.6
  22.1 0.0 copy-start.3
  22.1 0.8 %shard_map.77 = (bf16[8,128]{1,0:T(8,128)(2,1)S(1)}, bf16[512,512]{1,0:T(8,128)(2,1)S(1)}, bf16[512,256]{1,0:T(8,128)(2,1)S(1)}, bf16[256,256]{1,0:T(8,128)(2,1)S(1)}, bf16[256,256]{1,0:T(8,128)(2,1)S(1)}) custom-call(bf16[256,256]{1,0:T(8,128)(2,1)S(1)} %copy-done.4, bf16[256,256]{1,0:T(8,128)(2,1)S(1)} %copy-done.2, bf16[8,40]{1,0:T(8,128)(2,1)S(1)} %copy-done.5, ...), custom_call_target="tpu_custom_call" | custom-call | flops 100000000 | bytes 1000000 | tf_op jit(solution)/shard_map/pallas_call | solution.py:331
  22.9 1.8 %collective-permute-start.5 = (bf16[8,128]{1,0:T(8,128)(2,1)S(1)}, bf16[8,128]{1,0:T(8,128)(2,1)S(1)}, u32[]{:S(2)}, u32[]{:S(2)}) collective-permute-start(bf16[8,128]{1,0:T(8,128)(2,1)S(1)} %get-tuple-element.17.refs_2_), channel_id=1, source_target_pairs={{0,1},{1,0},{2,3},{3,2},{4,5},{5,4},{6,7},{7,6},{8,9},{9,8},{10,11... | collective-permute-start | bytes 6152 | tf_op jit(solution)/shard_map/ppermute | solution.py:361
  24.7 1.3 %collective-permute-start = (bf16[8,128]{1,0:T(8,128)(2,1)S(1)}, bf16[8,128]{1,0:T(8,128)(2,1)S(1)}, u32[]{:S(2)}, u32[]{:S(2)}) collective-permute-start(bf16[8,128]{1,0:T(8,128)(2,1)S(1)} %get-tuple-element.17.refs_2_), channel_id=1, source_target_pairs={{2,0},{4,2},{6,4},{8,6},{10,8},{12,10},{14,12},{16,14},{18,16},{20... | collective-permute-start | bytes 6152 | tf_op jit(solution)/shard_map/ppermute | solution.py:350
  26.0 0.0 copy-start.7
  26.0 0.1 pad_add_fusion.refs_0_.place_ref
  26.1 0.6 copy-done.7
  26.7 0.1 reshape.19.refs_1_
  26.7 0.0 collective-permute-done.5.refs_3_
  26.7 1.3 %collective-permute-start.1 = (bf16[8,128]{1,0:T(8,128)(2,1)S(1)}, bf16[8,128]{1,0:T(8,128)(2,1)S(1)}, u32[]{:S(2)}, u32[]{:S(2)}) collective-permute-start(bf16[8,128]{1,0:T(8,128)(2,1)S(1)} %get-tuple-element.17.refs_2_), channel_id=1, source_target_pairs={{4,0},{6,2},{8,4},{10,6},{12,8},{14,10},{16,12},{18,14},{20,16},{2... | collective-permute-start | bytes 6152 | tf_op jit(solution)/shard_map/ppermute | solution.py:350
  28.0 0.0 collective-permute-done.6.refs_5_
  28.0 0.0 copy-done.3
  28.0 0.0 copy-start
  28.1 1.0 %copy-done = bf16[8,32,1024]{2,1,0:T(8,128)(2,1)S(1)} copy-done((bf16[8,32,1024]{2,1,0:T(8,128)(2,1)S(1)}, bf16[8,32,1024]{2,1,0:T(8,128)(2,1)}, u32[]{:S(2)}) %copy-start) | copy-done | bytes 524312
  29.1 2.9 %shard_map.79 = (bf16[4,256,256]{2,1,0:T(8,128)(2,1)S(1)}, bf16[4,256,256]{2,1,0:T(8,128)(2,1)S(1)}, bf16[128,1024]{1,0:T(8,128)(2,1)S(1)}, bf16[128,1024]{1,0:T(8,128)(2,1)S(1)}) custom-call(s32[2]{0:T(128)S(1)} %pad_add_fusion.refs_0_.place_ref, s32[2,32]{1,0:T(2,128)S(1)} %reshape.19.refs_1_, bf16[8,128]{1,0:T(8,128)(2,1)S(1)} %get-tuple-element.17.refs_2_, ...), custom_call_target="tpu_custom_call" | custom-call | flops 100000000 | bytes 1000000 | tf_op jit(solution)/shard_map/pallas_call | solution.py:331
  32.0 0.0 copy-start.1
  32.0 2.9 %shard_map.78 = (bf16[4,256,256]{2,1,0:T(8,128)(2,1)S(1)}, bf16[4,256,256]{2,1,0:T(8,128)(2,1)S(1)}, bf16[128,1024]{1,0:T(8,128)(2,1)S(1)}, bf16[128,1024]{1,0:T(8,128)(2,1)S(1)}) custom-call(s32[2]{0:T(128)S(1)} %pad_add_fusion.refs_0_.place_ref, s32[2,32]{1,0:T(2,128)S(1)} %reshape.19.refs_1_, bf16[8,128]{1,0:T(8,128)(2,1)S(1)} %get-tuple-element.17.refs_2_, ...), custom_call_target="tpu_custom_call" | custom-call | flops 100000000 | bytes 1000000 | tf_op jit(solution)/shard_map/pallas_call | solution.py:331
  34.9 0.0 collective-permute-done.refs_3_
  34.9 0.0 collective-permute-done.1.refs_4_
  34.9 0.0 collective-permute-done.2
  34.9 0.0 collective-permute-done.4
  34.9 0.0 copy-done.1
  35.0 7.6 %shard_map.80 = (f32[2,144,128]{2,1,0:T(8,128)S(1)}, f32[2,144,128]{2,1,0:T(8,128)S(1)}) custom-call(s32[2]{0:T(128)S(1)} %pad_add_fusion.refs_0_.place_ref, s32[2,32]{1,0:T(2,128)S(1)} %reshape.19.refs_1_, bf16[8,128]{1,0:T(8,128)(2,1)S(1)} %get-tuple-element.17.refs_2_, bf16[8,128]{1,0:T(8,128)(2,1)S(1)} %collective-permute-done.refs_3_, ...), custom_call_target="tpu_custom_call" | custom-call | flops 100000000 | bytes 1000000 | tf_op jit(solution)/shard_map/pallas_call | solution.py:331
  42.6 1.2 %collective-permute-start.7 = (f32[2,144,128]{2,1,0:T(8,128)S(1)}, f32[2,144,128]{2,1,0:T(8,128)S(1)}, u32[]{:S(2)}, u32[]{:S(2)}) collective-permute-start(f32[2,144,128]{2,1,0:T(8,128)S(1)} %get-tuple-element.31), channel_id=1, source_target_pairs={{0,2},{2,0},{4,6},{6,4},{8,10},{10,8},{12,14},{14,12},{16,18},{18,... | collective-permute-start | bytes 442376 | tf_op jit(solution)/shard_map/ppermute | solution.py:366
  43.8 1.0 %collective-permute-done.7 = f32[2,144,128]{2,1,0:T(8,128)S(1)} collective-permute-done((f32[2,144,128]{2,1,0:T(8,128)S(1)}, f32[2,144,128]{2,1,0:T(8,128)S(1)}, u32[]{:S(2)}, u32[]{:S(2)}) %collective-permute-start.7) | collective-permute-done | bytes 147488 | tf_op jit(solution)/shard_map/ppermute | solution.py:366
  44.8 0.8 %collective-permute-start.8 = (f32[144,128]{1,0:T(8,128)S(1)}, f32[144,128]{1,0:T(8,128)S(1)}, u32[]{:S(2)}, u32[]{:S(2)}) collective-permute-start(f32[144,128]{1,0:T(8,128)S(1)} %slice_bitcast_fusion), channel_id=1, source_target_pairs={{0,1},{1,0},{2,3},{3,2},{4,5},{5,4},{6,7},{7,6},{8,9},{9,8},{10,11... | collective-permute-start | bytes 221192 | tf_op jit(solution)/shard_map/ppermute | solution.py:361
  45.6 3.8 %collective-permute-done.8 = f32[144,128]{1,0:T(8,128)S(1)} collective-permute-done((f32[144,128]{1,0:T(8,128)S(1)}, f32[144,128]{1,0:T(8,128)S(1)}, u32[]{:S(2)}, u32[]{:S(2)}) %collective-permute-start.8) | collective-permute-done | bytes 73760 | tf_op jit(solution)/shard_map/ppermute | solution.py:361
  49.4 3.1 %collective-permute-start.9 = (f32[144,128]{1,0:T(8,128)S(1)}, f32[144,128]{1,0:T(8,128)S(1)}, u32[]{:S(2)}, u32[]{:S(2)}) collective-permute-start(f32[144,128]{1,0:T(8,128)S(1)} %fusion), channel_id=1, source_target_pairs={{0,4},{2,6},{4,0},{6,2},{8,12},{10,14},{12,8},{14,10},{16,20},{18,... | collective-permute-start | bytes 221192 | tf_op jit(solution)/shard_map/ppermute | solution.py:366
  52.5 2.3 %collective-permute-done.9 = f32[144,128]{1,0:T(8,128)S(1)} collective-permute-done((f32[144,128]{1,0:T(8,128)S(1)}, f32[144,128]{1,0:T(8,128)S(1)}, u32[]{:S(2)}, u32[]{:S(2)}) %collective-permute-start.9) | collective-permute-done | bytes 73760 | tf_op jit(solution)/shard_map/ppermute | solution.py:366
  54.8 3.3 %collective-permute-start.10 = (f32[144,128]{1,0:T(8,128)S(1)}, f32[144,128]{1,0:T(8,128)S(1)}, u32[]{:S(2)}, u32[]{:S(2)}) collective-permute-start(f32[144,128]{1,0:T(8,128)S(1)} %add.17), channel_id=1, source_target_pairs={{0,8},{2,10},{4,12},{6,14},{8,0},{10,2},{12,4},{14,6},{16,24},{18,... | collective-permute-start | bytes 221192 | tf_op jit(solution)/shard_map/ppermute | solution.py:366
  58.1 2.3 %collective-permute-done.10 = f32[144,128]{1,0:T(8,128)S(1)} collective-permute-done((f32[144,128]{1,0:T(8,128)S(1)}, f32[144,128]{1,0:T(8,128)S(1)}, u32[]{:S(2)}, u32[]{:S(2)}) %collective-permute-start.10) | collective-permute-done | bytes 73760 | tf_op jit(solution)/shard_map/ppermute | solution.py:366
  60.5 3.5 %collective-permute-start.11 = (f32[144,128]{1,0:T(8,128)S(1)}, f32[144,128]{1,0:T(8,128)S(1)}, u32[]{:S(2)}, u32[]{:S(2)}) collective-permute-start(f32[144,128]{1,0:T(8,128)S(1)} %add.18), channel_id=1, source_target_pairs={{0,16},{2,18},{4,20},{6,22},{8,24},{10,26},{12,28},{14,30},{16,0},... | collective-permute-start | bytes 221192 | tf_op jit(solution)/shard_map/ppermute | solution.py:366
  63.9 2.3 %collective-permute-done.11 = f32[144,128]{1,0:T(8,128)S(1)} collective-permute-done((f32[144,128]{1,0:T(8,128)S(1)}, f32[144,128]{1,0:T(8,128)S(1)}, u32[]{:S(2)}, u32[]{:S(2)}) %collective-permute-start.11) | collective-permute-done | bytes 73760 | tf_op jit(solution)/shard_map/ppermute | solution.py:366
  66.3 0.1 collective-permute-start.12
  66.3 1.3 %collective-permute-done.12.other_ref = f32[144,128]{1,0:T(8,128)S(1)} collective-permute-done((f32[144,128]{1,0:T(8,128)S(1)}, f32[144,128]{1,0:T(8,128)S(1)}, u32[]{:S(2)}, u32[]{:S(2)}) %collective-permute-start.12) | collective-permute-done | bytes 73760 | tf_op jit(solution)/shard_map/ppermute | solution.py:366
  67.6 1.3 %shard_map.81 = (f32[8,20]{1,0:T(8,128)}, f32[32,1024]{1,0:T(8,128)}) custom-call(s32[2]{0:T(128)S(1)} %pad_add_fusion.refs_0_.place_ref, f32[144,128]{1,0:T(8,128)S(1)} %add.19.own_ref, f32[144,128]{1,0:T(8,128)S(1)} %collective-permute-done.12.other_ref), custom_call_target="tpu_custom_call" | custom-call | flops 100000000 | bytes 1000000 | tf_op jit(solution)/shard_map/pallas_call | solution.py:331
  (6 shorter events, 0.1 us)
Async XLA Ops:
  0.6 17.0 %collective-permute-start.3 = (bf16[8,32,1024]{2,1,0:T(8,128)(2,1)}, bf16[8,32,1024]{2,1,0:T(8,128)(2,1)S(1)}, u32[]{:S(2)}, u32[]{:S(2)}) collective-permute-start(bf16[8,32,1024]{2,1,0:T(8,128)(2,1)} %refs_4_.3), channel_id=1, source_target_pairs={{4,0},{6,2},{8,4},{10,6},{12,8},{14,10},{16,12},{18,14},{20,16},{2... | collective-permute-start | bytes 1572872 | tf_op jit(solution)/shard_map/ppermute | solution.py:350
  1.9 26.1 %collective-permute-start.6 = (bf16[8,32,1024]{2,1,0:T(8,128)(2,1)}, bf16[8,32,1024]{2,1,0:T(8,128)(2,1)S(1)}, u32[]{:S(2)}, u32[]{:S(2)}) collective-permute-start(bf16[8,32,1024]{2,1,0:T(8,128)(2,1)} %refs_4_.3), channel_id=1, source_target_pairs={{0,1},{1,0},{2,3},{3,2},{4,5},{5,4},{6,7},{7,6},{8,9},{9,8},{10,11... | collective-permute-start | bytes 1572872 | tf_op jit(solution)/shard_map/ppermute | solution.py:361
  5.0 29.9 %collective-permute-start.2 = (bf16[8,32,1024]{2,1,0:T(8,128)(2,1)}, bf16[8,32,1024]{2,1,0:T(8,128)(2,1)S(1)}, u32[]{:S(2)}, u32[]{:S(2)}) collective-permute-start(bf16[8,32,1024]{2,1,0:T(8,128)(2,1)} %refs_4_.3), channel_id=1, source_target_pairs={{2,0},{6,4},{10,8},{14,12},{18,16},{22,20},{26,24},{30,28},{3,1},{... | collective-permute-start | bytes 1572872 | tf_op jit(solution)/shard_map/ppermute | solution.py:350
  17.6 17.3 %collective-permute-start.4 = (bf16[8,32,1024]{2,1,0:T(8,128)(2,1)S(1)}, bf16[8,32,1024]{2,1,0:T(8,128)(2,1)S(1)}, u32[]{:S(2)}, u32[]{:S(2)}) collective-permute-start(bf16[8,32,1024]{2,1,0:T(8,128)(2,1)S(1)} %collective-permute-done.3), channel_id=1, source_target_pairs={{0,2},{4,6},{8,10},{12,14},{16,18},{20,22},{24,26},{28,30},{1,3},{... | collective-permute-start | bytes 1572872 | tf_op jit(solution)/shard_map/ppermute | solution.py:350
  19.0 0.9 %copy-start.2 = (bf16[256,256]{1,0:T(8,128)(2,1)S(1)}, bf16[256,256]{1,0:T(8,128)(2,1)}, u32[]{:S(2)}) copy-start(bf16[256,256]{1,0:T(8,128)(2,1)} %refs_9_.3) | copy-start | bytes 393220
  19.9 0.9 %copy-start.4 = (bf16[256,256]{1,0:T(8,128)(2,1)S(1)}, bf16[256,256]{1,0:T(8,128)(2,1)}, u32[]{:S(2)}) copy-start(bf16[256,256]{1,0:T(8,128)(2,1)} %occ_ref.1) | copy-start | bytes 393220
  20.8 0.7 copy-start.5
  21.4 0.7 copy-start.6
  22.1 5.9 %copy-start.3 = (bf16[256,256]{1,0:T(8,128)(2,1)S(1)}, bf16[256,256]{1,0:T(8,128)(2,1)}, u32[]{:S(2)}) copy-start(bf16[256,256]{1,0:T(8,128)(2,1)} %refs_9_.3) | copy-start | bytes 393220
  22.9 3.9 %collective-permute-start.5 = (bf16[8,128]{1,0:T(8,128)(2,1)S(1)}, bf16[8,128]{1,0:T(8,128)(2,1)S(1)}, u32[]{:S(2)}, u32[]{:S(2)}) collective-permute-start(bf16[8,128]{1,0:T(8,128)(2,1)S(1)} %get-tuple-element.17.refs_2_), channel_id=1, source_target_pairs={{0,1},{1,0},{2,3},{3,2},{4,5},{5,4},{6,7},{7,6},{8,9},{9,8},{10,11... | collective-permute-start | bytes 6152 | tf_op jit(solution)/shard_map/ppermute | solution.py:361
  24.7 10.2 %collective-permute-start = (bf16[8,128]{1,0:T(8,128)(2,1)S(1)}, bf16[8,128]{1,0:T(8,128)(2,1)S(1)}, u32[]{:S(2)}, u32[]{:S(2)}) collective-permute-start(bf16[8,128]{1,0:T(8,128)(2,1)S(1)} %get-tuple-element.17.refs_2_), channel_id=1, source_target_pairs={{2,0},{4,2},{6,4},{8,6},{10,8},{12,10},{14,12},{16,14},{18,16},{20... | collective-permute-start | bytes 6152 | tf_op jit(solution)/shard_map/ppermute | solution.py:350
  26.0 0.7 copy-start.7
  26.7 8.2 %collective-permute-start.1 = (bf16[8,128]{1,0:T(8,128)(2,1)S(1)}, bf16[8,128]{1,0:T(8,128)(2,1)S(1)}, u32[]{:S(2)}, u32[]{:S(2)}) collective-permute-start(bf16[8,128]{1,0:T(8,128)(2,1)S(1)} %get-tuple-element.17.refs_2_), channel_id=1, source_target_pairs={{4,0},{6,2},{8,4},{10,6},{12,8},{14,10},{16,12},{18,14},{20,16},{2... | collective-permute-start | bytes 6152 | tf_op jit(solution)/shard_map/ppermute | solution.py:350
  28.0 1.0 %copy-start = (bf16[8,32,1024]{2,1,0:T(8,128)(2,1)S(1)}, bf16[8,32,1024]{2,1,0:T(8,128)(2,1)}, u32[]{:S(2)}) copy-start(bf16[8,32,1024]{2,1,0:T(8,128)(2,1)} %refs_4_.3) | copy-start | bytes 1572868
  32.0 3.0 %copy-start.1 = (bf16[8,32,1024]{2,1,0:T(8,128)(2,1)S(1)}, bf16[8,32,1024]{2,1,0:T(8,128)(2,1)}, u32[]{:S(2)}) copy-start(bf16[8,32,1024]{2,1,0:T(8,128)(2,1)} %refs_4_.3) | copy-start | bytes 1572868
  42.6 2.2 %collective-permute-start.7 = (f32[2,144,128]{2,1,0:T(8,128)S(1)}, f32[2,144,128]{2,1,0:T(8,128)S(1)}, u32[]{:S(2)}, u32[]{:S(2)}) collective-permute-start(f32[2,144,128]{2,1,0:T(8,128)S(1)} %get-tuple-element.31), channel_id=1, source_target_pairs={{0,2},{2,0},{4,6},{6,4},{8,10},{10,8},{12,14},{14,12},{16,18},{18,... | collective-permute-start | bytes 442376 | tf_op jit(solution)/shard_map/ppermute | solution.py:366
  44.8 4.6 %collective-permute-start.8 = (f32[144,128]{1,0:T(8,128)S(1)}, f32[144,128]{1,0:T(8,128)S(1)}, u32[]{:S(2)}, u32[]{:S(2)}) collective-permute-start(f32[144,128]{1,0:T(8,128)S(1)} %slice_bitcast_fusion), channel_id=1, source_target_pairs={{0,1},{1,0},{2,3},{3,2},{4,5},{5,4},{6,7},{7,6},{8,9},{9,8},{10,11... | collective-permute-start | bytes 221192 | tf_op jit(solution)/shard_map/ppermute | solution.py:361
  49.4 5.4 %collective-permute-start.9 = (f32[144,128]{1,0:T(8,128)S(1)}, f32[144,128]{1,0:T(8,128)S(1)}, u32[]{:S(2)}, u32[]{:S(2)}) collective-permute-start(f32[144,128]{1,0:T(8,128)S(1)} %fusion), channel_id=1, source_target_pairs={{0,4},{2,6},{4,0},{6,2},{8,12},{10,14},{12,8},{14,10},{16,20},{18,... | collective-permute-start | bytes 221192 | tf_op jit(solution)/shard_map/ppermute | solution.py:366
  54.8 5.6 %collective-permute-start.10 = (f32[144,128]{1,0:T(8,128)S(1)}, f32[144,128]{1,0:T(8,128)S(1)}, u32[]{:S(2)}, u32[]{:S(2)}) collective-permute-start(f32[144,128]{1,0:T(8,128)S(1)} %add.17), channel_id=1, source_target_pairs={{0,8},{2,10},{4,12},{6,14},{8,0},{10,2},{12,4},{14,6},{16,24},{18,... | collective-permute-start | bytes 221192 | tf_op jit(solution)/shard_map/ppermute | solution.py:366
  60.5 5.8 %collective-permute-start.11 = (f32[144,128]{1,0:T(8,128)S(1)}, f32[144,128]{1,0:T(8,128)S(1)}, u32[]{:S(2)}, u32[]{:S(2)}) collective-permute-start(f32[144,128]{1,0:T(8,128)S(1)} %add.18), channel_id=1, source_target_pairs={{0,16},{2,18},{4,20},{6,22},{8,24},{10,26},{12,28},{14,30},{16,0},... | collective-permute-start | bytes 221192 | tf_op jit(solution)/shard_map/ppermute | solution.py:366
  66.3 1.3 %collective-permute-start.12 = (f32[144,128]{1,0:T(8,128)S(1)}, f32[144,128]{1,0:T(8,128)S(1)}, u32[]{:S(2)}, u32[]{:S(2)}) collective-permute-start(f32[144,128]{1,0:T(8,128)S(1)} %add.19.own_ref), channel_id=1, source_target_pairs={{0,2},{2,0},{4,6},{6,4},{8,10},{10,8},{12,14},{14,12},{16,18},{18,... | collective-permute-start | bytes 221192 | tf_op jit(solution)/shard_map/ppermute | solution.py:366

commit v3 on v2

v3 whole, which is shorter than its diff:
```python
import math

import jax
import jax.numpy as jnp
from jax import lax
from jax.experimental import pallas as pl
from jax.experimental.pallas import tpu as pltpu
from jax.sharding import PartitionSpec as P


OA = 32
NAT = 8
REACH = 2
BLK = 8
NORB = OA * NAT
PAIR = OA * OA
LANE = 128
RQ = LANE // OA
NQ = OA // RQ
LIVE_AT = 64
CHUNKS = (4, 4)
BF = jnp.bfloat16
F4 = jnp.float32


def iota(shape, dim):
    return lax.broadcasted_iota(jnp.int32, shape, dim)


def mm(a, b):
    return lax.dot_general(a, b, (((1,), (0,)), ((), ())), preferred_element_type=F4)


def mm_nt(a, b):
    return lax.dot_general(a, b, (((1,), (1,)), ((), ())), preferred_element_type=F4)


def mm_tn(a, b):
    return lax.dot_general(a, b, (((0,), (0,)), ((), ())), preferred_element_type=F4)


def onehot(cond):
    return cond.astype(F4).astype(BF)


def div(x, n):
    if n & (n - 1) == 0:
        return lax.shift_right_logical(x, jnp.full_like(x, n.bit_length() - 1))
    return x // n


def mod(x, n):
    if n & (n - 1) == 0:
        return x & (n - 1)
    return x % n


def mm_split(a, b):
    count = a.shape[0]
    high = a.astype(BF)
    rest = a - high.astype(F4)
    middle = rest.astype(BF)
    low = (rest - middle.astype(F4)).astype(BF)
    out = mm(jnp.concatenate([high.astype(F4), middle.astype(F4), low.astype(F4)], axis=0).astype(BF), b)
    return out[:count] + out[count : 2 * count] + out[2 * count :]


def slot_onehot(pair_row):
    count = pair_row.shape[1]
    slot = iota((NAT * NAT, count), 0)
    second = mod(div(slot, NAT), 2) * RQ + div(slot, 2 * NAT)
    return mod(slot, NAT) * NAT + second == pair_row


def pair_row(pairs_ref, place_ref, step, own_count):
    count = pairs_ref.shape[1] // own_count
    at = mod(place_ref[1] + step, count)
    row = jnp.zeros((1, own_count), jnp.int32)
    for s in range(count):
        row = jnp.where(at == s, pairs_ref[0:1, s * own_count : (s + 1) * own_count], row)
    return row


def swap_blocks(parts):
    lane = iota(parts[0].shape, 1)
    low = lane < LANE // 2
    even = mod(lane, LANE // 2) < OA
    a, b, c, d = parts
    a, c = jnp.where(low, a, pltpu.roll(c, LANE // 2, 1)), jnp.where(low, pltpu.roll(a, LANE // 2, 1), c)
    b, d = jnp.where(low, b, pltpu.roll(d, LANE // 2, 1)), jnp.where(low, pltpu.roll(b, LANE // 2, 1), d)
    a, b = jnp.where(even, a, pltpu.roll(b, OA, 1)), jnp.where(even, pltpu.roll(a, LANE - OA, 1), b)
    c, d = jnp.where(even, c, pltpu.roll(d, OA, 1)), jnp.where(even, pltpu.roll(c, LANE - OA, 1), d)
    return a, b, c, d


def to_matrix(tiles):
    parts = [
        jnp.concatenate(
            [tiles[i * 2 * NAT : (i + 1) * 2 * NAT, q * LANE : (q + 1) * LANE] for q in range(NQ)],
            axis=0,
        )
        for i in range(RQ)
    ]
    parts = [part.astype(F4) for part in swap_blocks(parts)]
    out = [
        jnp.concatenate(
            [part[(q * 2 + g) * NAT : (q * 2 + g + 1) * NAT] for g in range(2)], axis=1
        )
        for part in parts
        for q in range(NQ)
    ]
    return jnp.concatenate(out, axis=0).astype(BF)


def from_matrix(matrix):
    parts = [
        jnp.concatenate(
            [
                matrix[(i * NQ + q) * NAT : (i * NQ + q + 1) * NAT, g * LANE : (g + 1) * LANE]
                for q in range(NQ)
                for g in range(2)
            ],
            axis=0,
        ).astype(BF)
        for i in range(RQ)
    ]
    return jnp.concatenate(
        [
            jnp.concatenate(
                [part[q * 2 * NAT : (q + 1) * 2 * NAT] for q in range(NQ)], axis=1
            )
            for part in swap_blocks(parts)
        ],
        axis=0,
    )


def tables_kernel(*refs):
    ins, outs = refs[:6], refs[6:-5]
    pairs_ref, vir_ref, meta_ref, both_ref, cols_ref, vir_t_ref = outs[:6]
    parts = outs[6:]
    occ_ref, screened_ref, live_ref, whole_ref, sems = refs[-5:]
    targets = (occ_ref, vir_ref, screened_ref, live_ref, pairs_ref, whole_ref)
    copies = [
        pltpu.make_async_copy(a, b, sems.at[i]) for i, (a, b) in enumerate(zip(ins, targets))
    ]
    for copy in copies:
        copy.start()
    for copy in copies[:-1]:
        copy.wait()
    own_count = live_ref.shape[1]
    meta_ref[...] = jnp.zeros(meta_ref.shape, BF)
    meta_ref[:, : screened_ref.shape[1]] = screened_ref[...]
    meta_ref[:, LIVE_AT : LIVE_AT + own_count] = jnp.broadcast_to(
        live_ref[...].astype(F4), (BLK, own_count)
    ).astype(BF)
    row = iota((NORB, NORB), 0)
    col = iota((NORB, NORB), 1)
    natural = mod(row, NAT) * OA + mod(div(row, NAT), NQ) * RQ + div(row, NAT * NQ)
    order = onehot(natural == col)
    occ = occ_ref[...]
    cols = mm_nt(occ, order).astype(BF)
    both = mm(order, cols)
    cols_ref[...] = cols
    both_ref[:NORB] = both.T.astype(BF)
    both_ref[NORB:] = both.astype(BF)
    vir_t_ref[...] = vir_ref[...].astype(F4).T.astype(BF)
    diagonal = iota((own_count, own_count), 0) == iota((own_count, own_count), 1)
    live = jnp.where(diagonal, live_ref[...].astype(F4), 0.0)
    live = jnp.sum(live, axis=1, keepdims=True).astype(BF)
    copies[-1].wait()
    at = 0
    for ref in parts:
        for p in range(ref.shape[0] // own_count):
            ref[p * own_count : (p + 1) * own_count] = whole_ref[at] * live
            at += 1


def own_kernel(count, own_count, place_ref, pairs_ref, *refs):
    pieces = refs[:count]
    both_ref, cols_ref, vir_ref, vir_t_ref = refs[count : count + 4]
    matrix_ref, right_ref, z_ref, y_ref = refs[count + 4 :]
    group = matrix_ref.shape[0]
    selects = [
        onehot(slot_onehot(pair_row(pairs_ref, place_ref, s, own_count))) for s in range(count)
    ]
    tiles = []
    for p in range(group):
        at = slice(p * own_count, (p + 1) * own_count)
        total = mm(selects[0], pieces[0][at])
        for s in range(1, count):
            total = total + mm(selects[s], pieces[s][at])
        tiles.append(total.astype(BF))
    own_select = slot_onehot(pair_row(pairs_ref, place_ref, 0, own_count)).astype(F4).T.astype(BF)
    matrices = [to_matrix(t) for t in tiles]
    right = mm(jnp.concatenate(matrices, axis=0), cols_ref[...]).astype(BF)
    both = both_ref[...]
    lefts = [mm(both, m).astype(BF) for m in matrices]
    z = mm(jnp.concatenate([left[:NORB] for left in lefts], axis=0), vir_ref[...])
    y = mm(jnp.concatenate([left[NORB:] for left in lefts], axis=0), vir_t_ref[...])
    for value, ref in ((z, z_ref), (y, y_ref)):
        for p in range(group):
            part = from_matrix(value[p * NORB : (p + 1) * NORB])
            ref[p * own_count : (p + 1) * own_count] = mm(own_select, part).astype(BF)
    for p in range(group):
        matrix_ref[p] = matrices[p]
        right_ref[p] = right[p * NORB : (p + 1) * NORB]


def window_kernel(lanes, sigma_scale, chi_scale, place_ref, *refs):
    (pairs_ref, meta0, meta1, meta2, tile1a, tile1b, tile2, cols_ref) = refs[:8]
    keep_ref, send_ref, near_ref, mixed_ref, other_ref = refs[-5:]
    own, tile0 = refs[8 : 8 + 4 * len(CHUNKS)], refs[8 + 4 * len(CHUNKS) : -5]
    matrices = [ref[p] for ref in own[::4] for p in range(ref.shape[0])]
    rights = [ref[p] for ref in own[1::4] for p in range(ref.shape[0])]
    z = jnp.concatenate([ref[...] for ref in own[2::4]], axis=0)
    y = jnp.concatenate([ref[...] for ref in own[3::4]], axis=0)
    own_count = tile2.shape[0] // BLK
    pair_count = pairs_ref.shape[1] // own_count
    rows = BLK * own_count
    block, pair_at = place_ref[0], place_ref[1]
    row = iota((rows, rows), 0)
    col = iota((rows, rows), 1)
    same = (mod(row, own_count) == mod(col, own_count)).astype(F4)
    spread_row, spread_col = iota((LANE, rows), 0), iota((LANE, rows), 1)
    spread = onehot(spread_row == LIVE_AT + mod(spread_col, own_count))
    metas = [m[...] for m in (meta0, meta1, meta2)]
    masks = [same * mm(m, spread)[0:1, :] for m in metas]
    near_ref[...] = tile1a[...] + tile1b[...]
    tiles = [jnp.concatenate([t[...] for t in tile0], axis=0), near_ref, tile2]

    def spread_rows(value):
        return jnp.concatenate(
            [jnp.broadcast_to(value[p : p + 1], (own_count, rows)) for p in range(BLK)], axis=0
        )

    mixed = jnp.zeros((rows, PAIR), F4)
    for t in range(REACH + 1):
        pick = onehot(spread_row == (REACH + t) * BLK + div(spread_col, own_count))
        weight = spread_rows(mm(metas[0], pick)) * masks[t]
        mixed = mixed + mm(weight.astype(BF), tiles[t][...])
    mixed_ref[...] = mixed.astype(BF)
    other = jnp.zeros((rows, PAIR), F4)
    unspread = onehot(iota((BLK, rows), 0) == div(iota((BLK, rows), 1), own_count))
    for t in range(1, REACH + 1):
        pick = onehot(iota((BLK, LANE), 1) == (REACH - t) * BLK + iota((BLK, LANE), 0))
        weight = spread_rows(mm(mm_nt(pick, metas[t]).astype(BF), unspread)) * masks[t]
        other = other + mm(weight.astype(BF), tiles[t][...])
    other_ref[...] = other.astype(BF)
    own_select = onehot(slot_onehot(pair_row(pairs_ref, place_ref, 0, own_count)))

    def chi_part(steps):
        crosses = []
        for t in steps:
            w = abs(t)
            if t < 0:
                crosses.append(mm_nt(tiles[w][...], y))
            else:
                crosses.append(mm_nt(z, tiles[w][...]))
        sums, picks = [], []
        for t, cross in zip(steps, crosses):
            cross = cross * masks[abs(t)]
            sums.append(
                jnp.concatenate(
                    [
                        jnp.sum(cross[p * own_count : (p + 1) * own_count], axis=0, keepdims=True)
                        for p in range(BLK)
                    ],
                    axis=0,
                )
            )
            picks.append(
                onehot(
                    iota((rows, LANE), 1)
                    == (REACH + t) * BLK + div(iota((rows, LANE), 0), own_count)
                )
            )
        return mm_split(jnp.concatenate(sums, axis=1), jnp.concatenate(picks, axis=0))

    parts = [
        mm(own_select, ref[r * own_count : (r + 1) * own_count]).astype(BF)
        for ref in (mixed_ref, other_ref)
        for r in range(BLK)
    ]
    values = [to_matrix(part) for part in parts]
    chi = chi_part((-2, 2)) + chi_part((-1, 1)) + chi_part((0,))
    scaled = mm(jnp.concatenate(values[:BLK], axis=0), cols_ref[...]).astype(BF)
    lefts = [scaled[r * NORB : (r + 1) * NORB] for r in range(BLK)]
    total = mm(jnp.concatenate(lefts, axis=1), jnp.concatenate(matrices, axis=0))
    total = total + mm(jnp.concatenate(rights, axis=1), jnp.concatenate(values[BLK:], axis=0))
    total = total * -sigma_scale
    high = total.astype(BF).astype(F4)
    parts = [from_matrix(high), from_matrix(total - high)]
    parity = block & 1
    half = own_count // 2
    for s in range(pair_count):
        select = onehot(slot_onehot(pair_row(pairs_ref, place_ref, s, own_count)))
        owned = mm_tn(select, parts[0]) + mm_tn(select, parts[1])
        first, second = owned[:half], owned[half:]
        keep = jnp.where(parity == 0, first, second)
        send = jnp.where(parity == 0, second, first)
        for q in range(NQ):
            keep_ref[s, q * half : (q + 1) * half, :] = keep[:, q * LANE : (q + 1) * LANE]
            send_ref[s, q * half : (q + 1) * half, :] = send[:, q * LANE : (q + 1) * LANE]

    chi = chi * chi_scale
    share = (2 * REACH + 1) * BLK // pair_count
    column = iota((LANE, 1), 0)
    target = block + jnp.maximum(REACH - div(column, BLK), 0)
    at_pair = jnp.zeros((LANE, 1), jnp.int32)
    for s in range(1, pair_count):
        at_pair = at_pair + (column >= s * share).astype(jnp.int32)
    place = mod(at_pair - pair_at + pair_count, pair_count) + (
        ((target ^ block) & 1) * pair_count
    )
    spot = place * lanes + div(target, 2) * share + column - at_pair * share
    spread = onehot(iota((LANE, 2 * pair_count * lanes), 1) == spot)
    placed = mm_split(chi, spread)
    for s in range(pair_count):
        for i in range(lanes // LANE):
            at = slice(NQ * half + i * BLK, NQ * half + (i + 1) * BLK)
            begin = s * lanes + i * LANE
            keep_ref[s, at, :] = placed[:, begin : begin + LANE]
            begin += pair_count * lanes
            send_ref[s, at, :] = placed[:, begin : begin + LANE]


def last_kernel(place_ref, own_ref, other_ref, chi_ref, energy_ref):
    half = energy_ref.shape[0] // 2
    share = chi_ref.shape[1]
    parity = place_ref[0] & 1
    own, other = own_ref[...], other_ref[...]
    first = jnp.where(parity == 0, own, other)
    second = jnp.where(parity == 0, other, own)
    for q in range(NQ):
        at = slice(q * LANE, (q + 1) * LANE)
        energy_ref[:half, at] = first[q * half : (q + 1) * half]
        energy_ref[half:, at] = second[q * half : (q + 1) * half]
    start = (place_ref[0] >> 1) * share
    total = None
    for i in range((own.shape[0] - NQ * half) // BLK):
        chi = own[NQ * half + i * BLK : NQ * half + (i + 1) * BLK]
        pick = onehot(iota((LANE, LANE), 0) + i * LANE == start + iota((LANE, LANE), 1))
        part = mm_split(chi, pick)
        total = part if total is None else total + part
    chi_ref[...] = total[:, :share]


def call(body, outs, *args, scratch=(), ins=None, flops=10**8):
    full = pl.BlockSpec(memory_space=pltpu.VMEM)
    ins = ins or full
    if ins is not full:
        args = [pltpu.with_memory_space_constraint(a, pltpu.HBM) for a in args]
    return pl.pallas_call(
        body,
        out_shape=outs,
        in_specs=[pl.BlockSpec(memory_space=pltpu.SMEM) if a.ndim == 1 else ins for a in args],
        out_specs=jax.tree.map(lambda o: full, outs),
        scratch_shapes=scratch,
        cost_estimate=pl.CostEstimate(flops=flops, bytes_accessed=10**6, transcendentals=0),
        compiler_params=pltpu.CompilerParams(vmem_limit_bytes=24 << 20),
    )(*args)


def per_device(three_center, tile_live, pair_atoms, green_occ, green_vir, screened):
    block_rows, own_count = three_center.shape[:2]
    aux_count, pair_count = lax.axis_size("aux"), lax.axis_size("pair")
    block, pair_at = lax.axis_index("aux"), lax.axis_index("pair")
    rows = block_rows * own_count
    window = screened.shape[1]
    shape = jax.ShapeDtypeStruct

    def shifted(value, steps, parity=None):
        return lax.ppermute(
            value,
            "aux",
            [
                (s, s + steps)
                for s in range(aux_count)
                if 0 <= s + steps < aux_count and parity in (None, s % 2)
            ],
        )

    def turned(value, steps):
        return lax.ppermute(
            value, "pair", [(s, (s - steps) % pair_count) for s in range(pair_count)]
        )

    def flipped(value, mask):
        return lax.ppermute(value, "aux", [(s, s ^ mask) for s in range(aux_count)])

    far = shifted(three_center, -2)
    near_even = shifted(three_center, -1, 1)
    square = shape((NORB, NORB), BF)
    pairs, vir, meta, both, cols, vir_t, *parts = call(
        tables_kernel,
        [
            shape((1, pair_count * own_count), jnp.int32),
            square,
            shape((block_rows, LANE), BF),
            shape((2 * NORB, NORB), BF),
            square,
            square,
        ]
        + [shape((c * own_count, PAIR), BF) for c in CHUNKS],
        green_occ,
        green_vir,
        screened,
        tile_live,
        pair_atoms.reshape(1, pair_count * own_count),
        three_center,
        scratch=[
            pltpu.VMEM((NORB, NORB), BF),
            pltpu.VMEM(screened.shape, BF),
            pltpu.VMEM(tile_live.shape, jnp.int32),
            pltpu.VMEM(three_center.shape, BF),
            pltpu.SemaphoreType.DMA((6,)),
        ],
        ins=pl.BlockSpec(memory_space=pltpu.HBM),
    )
    pieces = []
    for part in parts:
        pieces.append([part] + [turned(part, s) for s in range(1, pair_count)])
    meta_near = shifted(meta, -1)
    meta_far = shifted(meta, -2)
    near_odd = shifted(far, 1, 0)
    place = jnp.stack([block, pair_at]).astype(jnp.int32)
    own = []
    for c, count in enumerate(CHUNKS):
        own += call(
            lambda *refs: own_kernel(pair_count, own_count, *refs),
            [
                shape((count, NORB, NORB), BF),
                shape((count, NORB, NORB), BF),
                shape((count * own_count, PAIR), BF),
                shape((count * own_count, PAIR), BF),
            ],
            place,
            pairs,
            *pieces[c],
            both,
            cols,
            vir,
            vir_t,
        )

    lanes = -(-(aux_count // 2) * (window // pair_count) // LANE) * LANE
    message = shape((pair_count, own_count // 2 * NQ + lanes // LANE * BLK, LANE), F4)
    aux_total = block_rows * aux_count
    keep, send = call(
        lambda *refs: window_kernel(
            lanes, 1.0 / math.sqrt(aux_total * NAT * OA * NAT), 1.0 / (OA * NAT), *refs
        ),
        [message, message],
        place,
        pairs,
        meta,
        meta_near,
        meta_far,
        near_even.reshape(rows, PAIR),
        near_odd.reshape(rows, PAIR),
        far.reshape(rows, PAIR),
        cols,
        *own,
        *parts,
        scratch=[pltpu.VMEM((rows, PAIR), BF)] * 3,
    )
    total = keep + flipped(send, 1)
    owned = total[0]
    for s in range(1, pair_count):
        owned = owned + turned(total[s], -s)
    masks = [1 << i for i in range(1, (aux_count - 1).bit_length())]
    for even, odd in zip(masks, masks[1:] + masks[:1]):
        owned = owned + lax.ppermute(
            owned, "aux", [(s, s ^ (odd if s % 2 else even)) for s in range(aux_count)]
        )
    polarizability, self_energy = call(
        last_kernel,
        [
            shape((block_rows, window // pair_count), F4),
            shape((own_count, PAIR), F4),
        ],
        place,
        owned,
        flipped(owned, 1),
    )
    return polarizability, self_energy


def solution(mesh):
    placed = (P("aux", "pair", None), P("aux", "pair"), P(), P(), P(), P("aux", None))
    return jax.shard_map(
        per_device,
        mesh=mesh,
        in_specs=placed,
        out_specs=(P("aux", "pair"), P("pair", None)),
        check_vma=False,
    )
```

time: 69.2 us -> 67.6 us (0.977)
  waiting for transfers between devices: 24.4 us -> 32.4 us
  local copies, waits for them, and re-layouts: 4.85 us -> 0.01 us
  starting transfers between devices: 23.2 us -> 20.5 us
  Pallas kernels: 15.4 us -> 13.5 us
    ppermute x5 -> x2, starting transfers between devices: 11.1 us -> 0.14 us  [flipped(): return lax.ppermute(value, 'aux', [(s, s ^ mask) for s in range(aux_count)])]
    ppermute x0 -> x3, starting transfers between devices: none -> 9.97 us  [per_device(): lax.ppermute(owned, 'aux', [(s, s ^ (odd if s % 2 else even)) for s in ra...]
    ppermute x0 -> x3, waiting for transfers between devices: none -> 7 us  [per_device(): lax.ppermute(owned, 'aux', [(s, s ^ (odd if s % 2 else even)) for s in ra...]
    ppermute x5 -> x2, waiting for transfers between devices: 9.26 us -> 2.61 us  [flipped(): return lax.ppermute(value, 'aux', [(s, s ^ mask) for s in range(aux_count)])]
    unnamed x16 -> x0, local copies, waits for them, and re-layouts: 4.76 us -> none
    ppermute x3, waiting for transfers between devices: 3.77 us -> 8.38 us  [turned(): lax.ppermute(value, 'pair', [(s, (s - steps) % pair_count) for s in range...]
    ppermute x5, waiting for transfers between devices: 11.4 us -> 14.4 us  [shifted(): lax.ppermute(value, 'aux', [(s, s + steps) for s in range(aux_count) if 0...]
    pallas_call x5, Pallas kernels: 15.4 us -> 13.5 us  [call(): pl.pallas_call(body, out_shape=outs, in_specs=[pl.BlockSpec(memory_space=...]
  transfers between devices with their start and end apart: 13 -> 13, of which waited for: 7 -> 8; matrix products, arithmetic and copies ran while one was open for 0% -> 0% of each run, Pallas kernels for 10% -> 10%
where the time goes in v3:
time: 67.6 us; the launch traced here: 67.3 us
  waiting for transfers between devices  32.4 us (48%)
  starting transfers between devices  20.5 us (30%)
  Pallas kernels  13.5 us (20%)
  between operations  0.79 us (1%)
    ppermute x5, waiting for transfers between devices, shifted(): lax.ppermute(value, 'aux', [(s, s + steps) for s in range(aux_count) if 0...  14.4 us
    pallas_call x5, Pallas kernels, call(): pl.pallas_call(body, out_shape=outs, in_specs=[pl.BlockSpec(memory_space=...  13.5 us
    ppermute x3, starting transfers between devices, per_device(): lax.ppermute(owned, 'aux', [(s, s ^ (odd if s % 2 else even)) for s in ra...  9.97 us
    ppermute x3, waiting for transfers between devices, turned(): lax.ppermute(value, 'pair', [(s, (s - steps) % pair_count) for s in range...  8.38 us
    ppermute x3, waiting for transfers between devices, per_device(): lax.ppermute(owned, 'aux', [(s, s ^ (odd if s % 2 else even)) for s in ra...  7 us
    ppermute x5, starting transfers between devices, shifted(): lax.ppermute(value, 'aux', [(s, s + steps) for s in range(aux_count) if 0...  6.46 us
    ppermute x3, starting transfers between devices, turned(): lax.ppermute(value, 'pair', [(s, (s - steps) % pair_count) for s in range...  3.91 us
    ppermute x2, waiting for transfers between devices, flipped(): return lax.ppermute(value, 'aux', [(s, s ^ mask) for s in range(aux_count)])  2.61 us
  transfers between devices with their start and end apart: 13, of which 8 were waited for; matrix products, arithmetic and copies ran while one was open for 0% of the time, Pallas kernels for 10%

profile of v3, /device:TPU:0, one launch (start us, length us, event | category | flops | bytes accessed | tf_op | source)
XLA Modules:
  0.0 67.3 jit_solution(5480100027474231875)
XLA Ops:
  0.6 1.3 %collective-permute-start.3 = (bf16[8,32,1024]{2,1,0:T(8,128)(2,1)}, bf16[8,32,1024]{2,1,0:T(8,128)(2,1)S(1)}, u32[]{:S(2)}, u32[]{:S(2)}) collective-permute-start(bf16[8,32,1024]{2,1,0:T(8,128)(2,1)} %refs_5_.1), channel_id=1, source_target_pairs={{4,0},{6,2},{8,4},{10,6},{12,8},{14,10},{16,12},{18,14},{20,16},{2... | collective-permute-start | bytes 1572872 | tf_op jit(solution)/shard_map/ppermute | solution.py:374
  1.9 1.3 %collective-permute-start.2 = (bf16[8,32,1024]{2,1,0:T(8,128)(2,1)}, bf16[8,32,1024]{2,1,0:T(8,128)(2,1)S(1)}, u32[]{:S(2)}, u32[]{:S(2)}) collective-permute-start(bf16[8,32,1024]{2,1,0:T(8,128)(2,1)} %refs_5_.1), channel_id=1, source_target_pairs={{2,0},{6,4},{10,8},{14,12},{18,16},{22,20},{26,24},{30,28},{3,1},{... | collective-permute-start | bytes 1572872 | tf_op jit(solution)/shard_map/ppermute | solution.py:374
  3.2 14.4 %collective-permute-done.3 = bf16[8,32,1024]{2,1,0:T(8,128)(2,1)S(1)} collective-permute-done((bf16[8,32,1024]{2,1,0:T(8,128)(2,1)}, bf16[8,32,1024]{2,1,0:T(8,128)(2,1)S(1)}, u32[]{:S(2)}, u32[]{:S(2)}) %collective-permute-start.3) | collective-permute-done | bytes 524320 | tf_op jit(solution)/shard_map/ppermute | solution.py:374
  17.6 1.3 %collective-permute-start.4 = (bf16[8,32,1024]{2,1,0:T(8,128)(2,1)S(1)}, bf16[8,32,1024]{2,1,0:T(8,128)(2,1)S(1)}, u32[]{:S(2)}, u32[]{:S(2)}) collective-permute-start(bf16[8,32,1024]{2,1,0:T(8,128)(2,1)S(1)} %collective-permute-done.3), channel_id=1, source_target_pairs={{0,2},{4,6},{8,10},{12,14},{16,18},{20,22},{24,26},{28,30},{1,3},{... | collective-permute-start | bytes 1572872 | tf_op jit(solution)/shard_map/ppermute | solution.py:374
  19.0 1.6 %shard_map.77 = (s32[1,64]{1,0:T(1,128)S(1)}, bf16[256,256]{1,0:T(8,128)(2,1)S(1)}, bf16[8,128]{1,0:T(8,128)(2,1)S(1)}, bf16[512,256]{1,0:T(8,128)(2,1)S(1)}, bf...) custom-call(bf16[256,256]{1,0:T(8,128)(2,1)} %refs_0_.1, ...), custom_call_target="tpu_custom_call" | custom-call | flops 100000000 | bytes 1000000 | tf_op jit(solution)/shard_map/pallas_call | solution.py:354
  20.6 1.8 %collective-permute-start.6 = (bf16[128,1024]{1,0:T(8,128)(2,1)S(1)}, bf16[128,1024]{1,0:T(8,128)(2,1)S(1)}, u32[]{:S(2)}, u32[]{:S(2)}) collective-permute-start(bf16[128,1024]{1,0:T(8,128)(2,1)S(1)} %get-tuple-element.31.refs_2_.refs_18_), channel_id=1, source_target_pairs={{0,1},{1,0},{2,3},{3,2},{4,5},{5,4},{6,7},{7,6},{8,9},{9,8},{10,11... | collective-permute-start | bytes 786440 | tf_op jit(solution)/shard_map/ppermute | solution.py:385
  22.4 0.3 collective-permute-start.5
  22.7 1.3 %collective-permute-start = (bf16[8,128]{1,0:T(8,128)(2,1)S(1)}, bf16[8,128]{1,0:T(8,128)(2,1)S(1)}, u32[]{:S(2)}, u32[]{:S(2)}) collective-permute-start(bf16[8,128]{1,0:T(8,128)(2,1)S(1)} %get-tuple-element.21.refs_2_), channel_id=1, source_target_pairs={{2,0},{4,2},{6,4},{8,6},{10,8},{12,10},{14,12},{16,14},{18,16},{20... | collective-permute-start | bytes 6152 | tf_op jit(solution)/shard_map/ppermute | solution.py:374
  23.9 0.1 pad_add_fusion.refs_0_.place_ref
  24.0 5.8 %collective-permute-done.6.refs_3_ = bf16[128,1024]{1,0:T(8,128)(2,1)S(1)} collective-permute-done((bf16[128,1024]{1,0:T(8,128)(2,1)S(1)}, bf16[128,1024]{1,0:T(8,128)(2,1)S(1)}, u32[]{:S(2)}, u32[]{:S(2)}) %collective-permute-start.6) | collective-permute-done | bytes 262176 | tf_op jit(solution)/shard_map/ppermute | solution.py:385
  29.8 1.3 %collective-permute-start.1 = (bf16[8,128]{1,0:T(8,128)(2,1)S(1)}, bf16[8,128]{1,0:T(8,128)(2,1)S(1)}, u32[]{:S(2)}, u32[]{:S(2)}) collective-permute-start(bf16[8,128]{1,0:T(8,128)(2,1)S(1)} %get-tuple-element.21.refs_2_), channel_id=1, source_target_pairs={{4,0},{6,2},{8,4},{10,6},{12,8},{14,10},{16,12},{18,14},{20,16},{2... | collective-permute-start | bytes 6152 | tf_op jit(solution)/shard_map/ppermute | solution.py:374
  31.1 2.6 %shard_map.79 = (bf16[4,256,256]{2,1,0:T(8,128)(2,1)S(1)}, bf16[4,256,256]{2,1,0:T(8,128)(2,1)S(1)}, bf16[128,1024]{1,0:T(8,128)(2,1)S(1)}, bf16[128,1024]{1,0:T(8,128)(2,1)S(1)}) custom-call(s32[2]{0:T(128)S(1)} %pad_add_fusion.refs_0_.place_ref, s32[1,64]{1,0:T(1,128)S(1)} %get-tuple-element.20.refs_1_, ...), custom_call_target="tpu_custom_call" | custom-call | flops 100000000 | bytes 1000000 | tf_op jit(solution)/shard_map/pallas_call | solution.py:354
  33.7 0.0 collective-permute-done.5.refs_3_
  33.7 2.6 %shard_map.78 = (bf16[4,256,256]{2,1,0:T(8,128)(2,1)S(1)}, bf16[4,256,256]{2,1,0:T(8,128)(2,1)S(1)}, bf16[128,1024]{1,0:T(8,128)(2,1)S(1)}, bf16[128,1024]{1,0:T(8,128)(2,1)S(1)}) custom-call(s32[2]{0:T(128)S(1)} %pad_add_fusion.refs_0_.place_ref, s32[1,64]{1,0:T(1,128)S(1)} %get-tuple-element.20.refs_1_, ...), custom_call_target="tpu_custom_call" | custom-call | flops 100000000 | bytes 1000000 | tf_op jit(solution)/shard_map/pallas_call | solution.py:354
  36.3 0.0 collective-permute-done.refs_3_
  36.3 0.0 collective-permute-done.1.refs_4_
  36.4 0.0 collective-permute-done.2
  36.4 0.0 collective-permute-done.4
  36.4 5.4 %shard_map.80 = (f32[2,144,128]{2,1,0:T(8,128)S(1)}, f32[2,144,128]{2,1,0:T(8,128)S(1)}) custom-call(s32[2]{0:T(128)S(1)} %pad_add_fusion.refs_0_.place_ref, s32[1,64]{1,0:T(1,128)S(1)} %get-tuple-element.20.refs_1_, bf16[8,128]{1,0:T(8,128)(2,1)S(1)} %get-tuple-element.21.refs_2_, bf16[8,128]{1,0:T(8,128)(2,1)S(1)} %collective-permute-done.refs_3_, ...), custom_call_target="tpu_custom_call" | custom-call | flops 100000000 | bytes 1000000 | tf_op jit(solution)/shard_map/pallas_call | solution.py:354
  41.8 0.1 collective-permute-start.7
  41.9 1.4 %collective-permute-done.7 = f32[2,144,128]{2,1,0:T(8,128)S(1)} collective-permute-done((f32[2,144,128]{2,1,0:T(8,128)S(1)}, f32[2,144,128]{2,1,0:T(8,128)S(1)}, u32[]{:S(2)}, u32[]{:S(2)}) %collective-permute-start.7) | collective-permute-done | bytes 147488 | tf_op jit(solution)/shard_map/ppermute | solution.py:390
  43.3 1.8 %collective-permute-start.8 = (f32[144,128]{1,0:T(8,128)S(1)}, f32[144,128]{1,0:T(8,128)S(1)}, u32[]{:S(2)}, u32[]{:S(2)}) collective-permute-start(f32[144,128]{1,0:T(8,128)S(1)} %slice_bitcast_fusion), channel_id=1, source_target_pairs={{0,1},{1,0},{2,3},{3,2},{4,5},{5,4},{6,7},{7,6},{8,9},{9,8},{10,11... | collective-permute-start | bytes 221192 | tf_op jit(solution)/shard_map/ppermute | solution.py:385
  45.1 2.6 %collective-permute-done.8 = f32[144,128]{1,0:T(8,128)S(1)} collective-permute-done((f32[144,128]{1,0:T(8,128)S(1)}, f32[144,128]{1,0:T(8,128)S(1)}, u32[]{:S(2)}, u32[]{:S(2)}) %collective-permute-start.8) | collective-permute-done | bytes 73760 | tf_op jit(solution)/shard_map/ppermute | solution.py:385
  47.7 3.3 %collective-permute-start.9 = (f32[144,128]{1,0:T(8,128)S(1)}, f32[144,128]{1,0:T(8,128)S(1)}, u32[]{:S(2)}, u32[]{:S(2)}) collective-permute-start(f32[144,128]{1,0:T(8,128)S(1)} %fusion), channel_id=1, source_target_pairs={{0,4},{2,10},{4,0},{6,14},{8,12},{10,2},{12,8},{14,6},{16,20},{18,... | collective-permute-start | bytes 221192 | tf_op jit(solution)/shard_map/ppermute | solution.py:474
  51.1 2.3 %collective-permute-done.9 = f32[144,128]{1,0:T(8,128)S(1)} collective-permute-done((f32[144,128]{1,0:T(8,128)S(1)}, f32[144,128]{1,0:T(8,128)S(1)}, u32[]{:S(2)}, u32[]{:S(2)}) %collective-permute-start.9) | collective-permute-done | bytes 73760 | tf_op jit(solution)/shard_map/ppermute | solution.py:474
  53.4 3.5 %collective-permute-start.10 = (f32[144,128]{1,0:T(8,128)S(1)}, f32[144,128]{1,0:T(8,128)S(1)}, u32[]{:S(2)}, u32[]{:S(2)}) collective-permute-start(f32[144,128]{1,0:T(8,128)S(1)} %add.17), channel_id=1, source_target_pairs={{0,8},{2,18},{4,12},{6,22},{8,0},{10,26},{12,4},{14,30},{16,24},{1... | collective-permute-start | bytes 221192 | tf_op jit(solution)/shard_map/ppermute | solution.py:474
  56.9 2.3 %collective-permute-done.10 = f32[144,128]{1,0:T(8,128)S(1)} collective-permute-done((f32[144,128]{1,0:T(8,128)S(1)}, f32[144,128]{1,0:T(8,128)S(1)}, u32[]{:S(2)}, u32[]{:S(2)}) %collective-permute-start.10) | collective-permute-done | bytes 73760 | tf_op jit(solution)/shard_map/ppermute | solution.py:474
  59.3 3.1 %collective-permute-start.11 = (f32[144,128]{1,0:T(8,128)S(1)}, f32[144,128]{1,0:T(8,128)S(1)}, u32[]{:S(2)}, u32[]{:S(2)}) collective-permute-start(f32[144,128]{1,0:T(8,128)S(1)} %add.18), channel_id=1, source_target_pairs={{0,16},{2,6},{4,20},{6,2},{8,24},{10,14},{12,28},{14,10},{16,0},{1... | collective-permute-start | bytes 221192 | tf_op jit(solution)/shard_map/ppermute | solution.py:474
  62.4 2.3 %collective-permute-done.11 = f32[144,128]{1,0:T(8,128)S(1)} collective-permute-done((f32[144,128]{1,0:T(8,128)S(1)}, f32[144,128]{1,0:T(8,128)S(1)}, u32[]{:S(2)}, u32[]{:S(2)}) %collective-permute-start.11) | collective-permute-done | bytes 73760 | tf_op jit(solution)/shard_map/ppermute | solution.py:474
  64.7 0.1 collective-permute-start.12
  64.8 1.3 %collective-permute-done.12.other_ref = f32[144,128]{1,0:T(8,128)S(1)} collective-permute-done((f32[144,128]{1,0:T(8,128)S(1)}, f32[144,128]{1,0:T(8,128)S(1)}, u32[]{:S(2)}, u32[]{:S(2)}) %collective-permute-start.12) | collective-permute-done | bytes 73760 | tf_op jit(solution)/shard_map/ppermute | solution.py:390
  66.1 1.3 %shard_map.81 = (f32[8,20]{1,0:T(8,128)}, f32[32,1024]{1,0:T(8,128)}) custom-call(s32[2]{0:T(128)S(1)} %pad_add_fusion.refs_0_.place_ref, f32[144,128]{1,0:T(8,128)S(1)} %add.19.own_ref, f32[144,128]{1,0:T(8,128)S(1)} %collective-permute-done.12.other_ref), custom_call_target="tpu_custom_call" | custom-call | flops 100000000 | bytes 1000000 | tf_op jit(solution)/shard_map/pallas_call | solution.py:354
  (6 shorter events, 0.1 us)
Async XLA Ops:
  0.6 17.0 %collective-permute-start.3 = (bf16[8,32,1024]{2,1,0:T(8,128)(2,1)}, bf16[8,32,1024]{2,1,0:T(8,128)(2,1)S(1)}, u32[]{:S(2)}, u32[]{:S(2)}) collective-permute-start(bf16[8,32,1024]{2,1,0:T(8,128)(2,1)} %refs_5_.1), channel_id=1, source_target_pairs={{4,0},{6,2},{8,4},{10,6},{12,8},{14,10},{16,12},{18,14},{20,16},{2... | collective-permute-start | bytes 1572872 | tf_op jit(solution)/shard_map/ppermute | solution.py:374
  1.9 34.4 %collective-permute-start.2 = (bf16[8,32,1024]{2,1,0:T(8,128)(2,1)}, bf16[8,32,1024]{2,1,0:T(8,128)(2,1)S(1)}, u32[]{:S(2)}, u32[]{:S(2)}) collective-permute-start(bf16[8,32,1024]{2,1,0:T(8,128)(2,1)} %refs_5_.1), channel_id=1, source_target_pairs={{2,0},{6,4},{10,8},{14,12},{18,16},{22,20},{26,24},{30,28},{3,1},{... | collective-permute-start | bytes 1572872 | tf_op jit(solution)/shard_map/ppermute | solution.py:374
  17.6 18.7 %collective-permute-start.4 = (bf16[8,32,1024]{2,1,0:T(8,128)(2,1)S(1)}, bf16[8,32,1024]{2,1,0:T(8,128)(2,1)S(1)}, u32[]{:S(2)}, u32[]{:S(2)}) collective-permute-start(bf16[8,32,1024]{2,1,0:T(8,128)(2,1)S(1)} %collective-permute-done.3), channel_id=1, source_target_pairs={{0,2},{4,6},{8,10},{12,14},{16,18},{20,22},{24,26},{28,30},{1,3},{... | collective-permute-start | bytes 1572872 | tf_op jit(solution)/shard_map/ppermute | solution.py:374
  20.6 9.2 %collective-permute-start.6 = (bf16[128,1024]{1,0:T(8,128)(2,1)S(1)}, bf16[128,1024]{1,0:T(8,128)(2,1)S(1)}, u32[]{:S(2)}, u32[]{:S(2)}) collective-permute-start(bf16[128,1024]{1,0:T(8,128)(2,1)S(1)} %get-tuple-element.31.refs_2_.refs_18_), channel_id=1, source_target_pairs={{0,1},{1,0},{2,3},{3,2},{4,5},{5,4},{6,7},{7,6},{8,9},{9,8},{10,11... | collective-permute-start | bytes 786440 | tf_op jit(solution)/shard_map/ppermute | solution.py:385
  22.4 11.3 %collective-permute-start.5 = (bf16[128,1024]{1,0:T(8,128)(2,1)S(1)}, bf16[128,1024]{1,0:T(8,128)(2,1)S(1)}, u32[]{:S(2)}, u32[]{:S(2)}) collective-permute-start(bf16[128,1024]{1,0:T(8,128)(2,1)S(1)} %get-tuple-element.23.refs_2_.refs_17_), channel_id=1, source_target_pairs={{0,1},{1,0},{2,3},{3,2},{4,5},{5,4},{6,7},{7,6},{8,9},{9,8},{10,11... | collective-permute-start | bytes 786440 | tf_op jit(solution)/shard_map/ppermute | solution.py:385
  22.7 13.7 %collective-permute-start = (bf16[8,128]{1,0:T(8,128)(2,1)S(1)}, bf16[8,128]{1,0:T(8,128)(2,1)S(1)}, u32[]{:S(2)}, u32[]{:S(2)}) collective-permute-start(bf16[8,128]{1,0:T(8,128)(2,1)S(1)} %get-tuple-element.21.refs_2_), channel_id=1, source_target_pairs={{2,0},{4,2},{6,4},{8,6},{10,8},{12,10},{14,12},{16,14},{18,16},{20... | collective-permute-start | bytes 6152 | tf_op jit(solution)/shard_map/ppermute | solution.py:374
  29.8 6.5 %collective-permute-start.1 = (bf16[8,128]{1,0:T(8,128)(2,1)S(1)}, bf16[8,128]{1,0:T(8,128)(2,1)S(1)}, u32[]{:S(2)}, u32[]{:S(2)}) collective-permute-start(bf16[8,128]{1,0:T(8,128)(2,1)S(1)} %get-tuple-element.21.refs_2_), channel_id=1, source_target_pairs={{4,0},{6,2},{8,4},{10,6},{12,8},{14,10},{16,12},{18,14},{20,16},{2... | collective-permute-start | bytes 6152 | tf_op jit(solution)/shard_map/ppermute | solution.py:374
  41.8 1.4 %collective-permute-start.7 = (f32[2,144,128]{2,1,0:T(8,128)S(1)}, f32[2,144,128]{2,1,0:T(8,128)S(1)}, u32[]{:S(2)}, u32[]{:S(2)}) collective-permute-start(f32[2,144,128]{2,1,0:T(8,128)S(1)} %get-tuple-element.37), channel_id=1, source_target_pairs={{0,2},{2,0},{4,6},{6,4},{8,10},{10,8},{12,14},{14,12},{16,18},{18,... | collective-permute-start | bytes 442376 | tf_op jit(solution)/shard_map/ppermute | solution.py:390
  43.3 4.4 %collective-permute-start.8 = (f32[144,128]{1,0:T(8,128)S(1)}, f32[144,128]{1,0:T(8,128)S(1)}, u32[]{:S(2)}, u32[]{:S(2)}) collective-permute-start(f32[144,128]{1,0:T(8,128)S(1)} %slice_bitcast_fusion), channel_id=1, source_target_pairs={{0,1},{1,0},{2,3},{3,2},{4,5},{5,4},{6,7},{7,6},{8,9},{9,8},{10,11... | collective-permute-start | bytes 221192 | tf_op jit(solution)/shard_map/ppermute | solution.py:385
  47.7 5.7 %collective-permute-start.9 = (f32[144,128]{1,0:T(8,128)S(1)}, f32[144,128]{1,0:T(8,128)S(1)}, u32[]{:S(2)}, u32[]{:S(2)}) collective-permute-start(f32[144,128]{1,0:T(8,128)S(1)} %fusion), channel_id=1, source_target_pairs={{0,4},{2,10},{4,0},{6,14},{8,12},{10,2},{12,8},{14,6},{16,20},{18,... | collective-permute-start | bytes 221192 | tf_op jit(solution)/shard_map/ppermute | solution.py:474
  53.4 5.8 %collective-permute-start.10 = (f32[144,128]{1,0:T(8,128)S(1)}, f32[144,128]{1,0:T(8,128)S(1)}, u32[]{:S(2)}, u32[]{:S(2)}) collective-permute-start(f32[144,128]{1,0:T(8,128)S(1)} %add.17), channel_id=1, source_target_pairs={{0,8},{2,18},{4,12},{6,22},{8,0},{10,26},{12,4},{14,30},{16,24},{1... | collective-permute-start | bytes 221192 | tf_op jit(solution)/shard_map/ppermute | solution.py:474
  59.3 5.5 %collective-permute-start.11 = (f32[144,128]{1,0:T(8,128)S(1)}, f32[144,128]{1,0:T(8,128)S(1)}, u32[]{:S(2)}, u32[]{:S(2)}) collective-permute-start(f32[144,128]{1,0:T(8,128)S(1)} %add.18), channel_id=1, source_target_pairs={{0,16},{2,6},{4,20},{6,2},{8,24},{10,14},{12,28},{14,10},{16,0},{1... | collective-permute-start | bytes 221192 | tf_op jit(solution)/shard_map/ppermute | solution.py:474
  64.7 1.3 %collective-permute-start.12 = (f32[144,128]{1,0:T(8,128)S(1)}, f32[144,128]{1,0:T(8,128)S(1)}, u32[]{:S(2)}, u32[]{:S(2)}) collective-permute-start(f32[144,128]{1,0:T(8,128)S(1)} %add.19.own_ref), channel_id=1, source_target_pairs={{0,2},{2,0},{4,6},{6,4},{8,10},{10,8},{12,14},{14,12},{16,18},{18,... | collective-permute-start | bytes 221192 | tf_op jit(solution)/shard_map/ppermute | solution.py:390

commit v4 on v3

--- a/solution.py
+++ b/solution.py
@@ -35,10 +35,6 @@
     return lax.dot_general(a, b, (((1,), (1,)), ((), ())), preferred_element_type=F4)
 
 
-def mm_tn(a, b):
-    return lax.dot_general(a, b, (((0,), (0,)), ((), ())), preferred_element_type=F4)
-
-
 def onehot(cond):
     return cond.astype(F4).astype(BF)
 
@@ -86,8 +82,10 @@
     low = lane < LANE // 2
     even = mod(lane, LANE // 2) < OA
     a, b, c, d = parts
-    a, c = jnp.where(low, a, pltpu.roll(c, LANE // 2, 1)), jnp.where(low, pltpu.roll(a, LANE // 2, 1), c)
-    b, d = jnp.where(low, b, pltpu.roll(d, LANE // 2, 1)), jnp.where(low, pltpu.roll(b, LANE // 2, 1), d)
+    moved = pltpu.roll(jnp.where(low, c, a), LANE // 2, 1)
+    a, c = jnp.where(low, a, moved), jnp.where(low, moved, c)
+    moved = pltpu.roll(jnp.where(low, d, b), LANE // 2, 1)
+    b, d = jnp.where(low, b, moved), jnp.where(low, moved, d)
     a, b = jnp.where(even, a, pltpu.roll(b, OA, 1)), jnp.where(even, pltpu.roll(a, LANE - OA, 1), b)
     c, d = jnp.where(even, c, pltpu.roll(d, OA, 1)), jnp.where(even, pltpu.roll(c, LANE - OA, 1), d)
     return a, b, c, d
@@ -193,18 +191,26 @@
         tiles.append(total.astype(BF))
     own_select = slot_onehot(pair_row(pairs_ref, place_ref, 0, own_count)).astype(F4).T.astype(BF)
     matrices = [to_matrix(t) for t in tiles]
+    both = both_ref[...]
+
+    def transformed(rows, side):
+        lefts = [mm(both[rows], m).astype(BF) for m in matrices]
+        value = mm(jnp.concatenate(lefts, axis=0), side)
+        return [value[p * NORB : (p + 1) * NORB] for p in range(group)]
+
+    def selected(value, ref):
+        for p in range(group):
+            part = from_matrix(value[p])
+            ref[p * own_count : (p + 1) * own_count] = mm(own_select, part).astype(BF)
+
+    z = transformed(slice(0, NORB), vir_ref[...])
+    y = transformed(slice(NORB, 2 * NORB), vir_t_ref[...])
+    selected(z, z_ref)
     right = mm(jnp.concatenate(matrices, axis=0), cols_ref[...]).astype(BF)
-    both = both_ref[...]
-    lefts = [mm(both, m).astype(BF) for m in matrices]
-    z = mm(jnp.concatenate([left[:NORB] for left in lefts], axis=0), vir_ref[...])
-    y = mm(jnp.concatenate([left[NORB:] for left in lefts], axis=0), vir_t_ref[...])
-    for value, ref in ((z, z_ref), (y, y_ref)):
-        for p in range(group):
-            part = from_matrix(value[p * NORB : (p + 1) * NORB])
-            ref[p * own_count : (p + 1) * own_count] = mm(own_select, part).astype(BF)
     for p in range(group):
         matrix_ref[p] = matrices[p]
         right_ref[p] = right[p * NORB : (p + 1) * NORB]
+    selected(y, y_ref)
 
 
 def window_kernel(lanes, sigma_scale, chi_scale, place_ref, *refs):
@@ -247,7 +253,13 @@
         weight = spread_rows(mm(mm_nt(pick, metas[t]).astype(BF), unspread)) * masks[t]
         other = other + mm(weight.astype(BF), tiles[t][...])
     other_ref[...] = other.astype(BF)
-    own_select = onehot(slot_onehot(pair_row(pairs_ref, place_ref, 0, own_count)))
+    selects = [
+        onehot(slot_onehot(pair_row(pairs_ref, place_ref, s, own_count)))
+        for s in range(pair_count)
+    ]
+    own_select = selects[0]
+    both_parts = jnp.concatenate(selects, axis=1).astype(F4).T.astype(BF)
+    both_parts = jnp.concatenate([both_parts, both_parts], axis=1)
 
     def chi_part(steps):
         crosses = []
@@ -290,12 +302,12 @@
     total = total + mm(jnp.concatenate(rights, axis=1), jnp.concatenate(values[BLK:], axis=0))
     total = total * -sigma_scale
     high = total.astype(BF).astype(F4)
-    parts = [from_matrix(high), from_matrix(total - high)]
-    parity = block & 1
+    parts = jnp.concatenate([from_matrix(high), from_matrix(total - high)], axis=0)
+    owned_all = mm(both_parts, parts)
+    parity = place_ref[2]
     half = own_count // 2
     for s in range(pair_count):
-        select = onehot(slot_onehot(pair_row(pairs_ref, place_ref, s, own_count)))
-        owned = mm_tn(select, parts[0]) + mm_tn(select, parts[1])
+        owned = owned_all[s * own_count : (s + 1) * own_count]
         first, second = owned[:half], owned[half:]
         keep = jnp.where(parity == 0, first, second)
         send = jnp.where(parity == 0, second, first)
@@ -311,7 +323,7 @@
     for s in range(1, pair_count):
         at_pair = at_pair + (column >= s * share).astype(jnp.int32)
     place = mod(at_pair - pair_at + pair_count, pair_count) + (
-        ((target ^ block) & 1) * pair_count
+        ((target & 1) ^ place_ref[2]) * pair_count
     )
     spot = place * lanes + div(target, 2) * share + column - at_pair * share
     spread = onehot(iota((LANE, 2 * pair_count * lanes), 1) == spot)
@@ -328,7 +340,7 @@
 def last_kernel(place_ref, own_ref, other_ref, chi_ref, energy_ref):
     half = energy_ref.shape[0] // 2
     share = chi_ref.shape[1]
-    parity = place_ref[0] & 1
+    parity = place_ref[2]
     own, other = own_ref[...], other_ref[...]
     first = jnp.where(parity == 0, own, other)
     second = jnp.where(parity == 0, other, own)
@@ -339,7 +351,8 @@
     start = (place_ref[0] >> 1) * share
     total = None
     for i in range((own.shape[0] - NQ * half) // BLK):
-        chi = own[NQ * half + i * BLK : NQ * half + (i + 1) * BLK]
+        at = slice(NQ * half + i * BLK, NQ * half + (i + 1) * BLK)
+        chi = jnp.where((place_ref[0] & 1) == parity, own[at], other[at])
         pick = onehot(iota((LANE, LANE), 0) + i * LANE == start + iota((LANE, LANE), 1))
         part = mm_split(chi, pick)
         total = part if total is None else total + part
@@ -424,7 +437,22 @@
     meta_near = shifted(meta, -1)
     meta_far = shifted(meta, -2)
     near_odd = shifted(far, 1, 0)
-    place = jnp.stack([block, pair_at]).astype(jnp.int32)
+    turn = pair_count == 2
+    half_at = (lax.population_count(block) + (pair_at if turn else 0)) & 1
+    place = jnp.stack([block, pair_at, half_at]).astype(jnp.int32)
+
+    def joint(value, target):
+        return lax.ppermute(
+            value,
+            ("aux", "pair"),
+            [
+                (s * pair_count + p, t * pair_count + q)
+                for s in range(aux_count)
+                for p in range(pair_count)
+                for t, q in [target(s, p)]
+            ],
+        )
+
     own = []
     for c, count in enumerate(CHUNKS):
         own += call(
@@ -467,12 +495,16 @@
     )
     total = keep + flipped(send, 1)
     owned = total[0]
-    for s in range(1, pair_count):
-        owned = owned + turned(total[s], -s)
-    masks = [1 << i for i in range(1, (aux_count - 1).bit_length())]
-    for even, odd in zip(masks, masks[1:] + masks[:1]):
-        owned = owned + lax.ppermute(
-            owned, "aux", [(s, s ^ (odd if s % 2 else even)) for s in range(aux_count)]
+    if turn:
+        owned = owned + joint(total[1].astype(BF), lambda s, p: (s ^ 1, p ^ 1)).astype(F4)
+    else:
+        for s in range(1, pair_count):
+            owned = owned + turned(total[s].astype(BF), -s).astype(F4)
+    masks = [1 << i | 1 for i in range(1, (aux_count - 1).bit_length())]
+    for masks_here in zip(masks, masks[1:] + masks[:1]):
+        owned = owned + joint(
+            owned,
+            lambda s, p: (s ^ masks_here[(s.bit_count() + (p if turn else 0)) % 2], p),
         )
     polarizability, self_energy = call(
         last_kernel,

time: 67.6 us -> 65.1 us (0.963)
  waiting for transfers between devices: 32.4 us -> 31.3 us
  starting transfers between devices: 20.5 us -> 19.6 us
    ppermute x3 -> x2, waiting for transfers between devices: 8.38 us -> 6 us  [turned(): lax.ppermute(value, 'pair', [(s, (s - steps) % pair_count) for s in range...]
    ppermute x3 -> x2, starting transfers between devices: 3.91 us -> 2.09 us  [turned(): lax.ppermute(value, 'pair', [(s, (s - steps) % pair_count) for s in range...]
    ppermute x3 -> x4, waiting for transfers between devices: 7 us -> 8.27 us  [joint(): lax.ppermute(value, ('aux', 'pair'), [(s * pair_count + p, t * pair_count...]
    ppermute x3 -> x4, starting transfers between devices: 9.97 us -> 10.9 us  [joint(): lax.ppermute(value, ('aux', 'pair'), [(s * pair_count + p, t * pair_count...]
  transfers between devices with their start and end apart: 13 -> 13, of which waited for: 8 -> 9; matrix products, arithmetic and copies ran while one was open for 0% -> 0% of each run, Pallas kernels for 10% -> 10%
where the time goes in v4:
time: 65.1 us; the launch traced here: 64.8 us
  waiting for transfers between devices  31.3 us (48%)
  starting transfers between devices  19.6 us (30%)
  Pallas kernels  13 us (20%)
  between operations  0.78 us (1%)
    ppermute x5, waiting for transfers between devices, shifted(): lax.ppermute(value, 'aux', [(s, s + steps) for s in range(aux_count) if 0...  14.4 us
    pallas_call x5, Pallas kernels, call(): pl.pallas_call(body, out_shape=outs, in_specs=[pl.BlockSpec(memory_space=...  13 us
    ppermute x4, starting transfers between devices, joint(): lax.ppermute(value, ('aux', 'pair'), [(s * pair_count + p, t * pair_count...  10.9 us
    ppermute x4, waiting for transfers between devices, joint(): lax.ppermute(value, ('aux', 'pair'), [(s * pair_count + p, t * pair_count...  8.27 us
    ppermute x5, starting transfers between devices, shifted(): lax.ppermute(value, 'aux', [(s, s + steps) for s in range(aux_count) if 0...  6.46 us
    ppermute x2, waiting for transfers between devices, turned(): lax.ppermute(value, 'pair', [(s, (s - steps) % pair_count) for s in range...  6 us
    ppermute x2, waiting for transfers between devices, flipped(): return lax.ppermute(value, 'aux', [(s, s ^ mask) for s in range(aux_count)])  2.61 us
    ppermute x2, starting transfers between devices, turned(): lax.ppermute(value, 'pair', [(s, (s - steps) % pair_count) for s in range...  2.09 us
  transfers between devices with their start and end apart: 13, of which 9 were waited for; matrix products, arithmetic and copies ran while one was open for 0% of the time, Pallas kernels for 10%

profile of v4, /device:TPU:0, one launch (start us, length us, event | category | flops | bytes accessed | tf_op | source)
XLA Modules:
  0.0 64.8 jit_solution(1300070049865853334)
XLA Ops:
  0.6 1.3 %collective-permute-start.3 = (bf16[8,32,1024]{2,1,0:T(8,128)(2,1)}, bf16[8,32,1024]{2,1,0:T(8,128)(2,1)S(1)}, u32[]{:S(2)}, u32[]{:S(2)}) collective-permute-start(bf16[8,32,1024]{2,1,0:T(8,128)(2,1)} %refs_5_.1), channel_id=1, source_target_pairs={{4,0},{6,2},{8,4},{10,6},{12,8},{14,10},{16,12},{18,14},{20,16},{2... | collective-permute-start | bytes 1572872 | tf_op jit(solution)/shard_map/ppermute | solution.py:387
  1.9 1.3 %collective-permute-start.2 = (bf16[8,32,1024]{2,1,0:T(8,128)(2,1)}, bf16[8,32,1024]{2,1,0:T(8,128)(2,1)S(1)}, u32[]{:S(2)}, u32[]{:S(2)}) collective-permute-start(bf16[8,32,1024]{2,1,0:T(8,128)(2,1)} %refs_5_.1), channel_id=1, source_target_pairs={{2,0},{6,4},{10,8},{14,12},{18,16},{22,20},{26,24},{30,28},{3,1},{... | collective-permute-start | bytes 1572872 | tf_op jit(solution)/shard_map/ppermute | solution.py:387
  3.2 14.4 %collective-permute-done.3 = bf16[8,32,1024]{2,1,0:T(8,128)(2,1)S(1)} collective-permute-done((bf16[8,32,1024]{2,1,0:T(8,128)(2,1)}, bf16[8,32,1024]{2,1,0:T(8,128)(2,1)S(1)}, u32[]{:S(2)}, u32[]{:S(2)}) %collective-permute-start.3) | collective-permute-done | bytes 524320 | tf_op jit(solution)/shard_map/ppermute | solution.py:387
  17.6 1.3 %collective-permute-start.4 = (bf16[8,32,1024]{2,1,0:T(8,128)(2,1)S(1)}, bf16[8,32,1024]{2,1,0:T(8,128)(2,1)S(1)}, u32[]{:S(2)}, u32[]{:S(2)}) collective-permute-start(bf16[8,32,1024]{2,1,0:T(8,128)(2,1)S(1)} %collective-permute-done.3), channel_id=1, source_target_pairs={{0,2},{4,6},{8,10},{12,14},{16,18},{20,22},{24,26},{28,30},{1,3},{... | collective-permute-start | bytes 1572872 | tf_op jit(solution)/shard_map/ppermute | solution.py:387
  19.0 1.6 %shard_map.77 = (s32[1,64]{1,0:T(1,128)S(1)}, bf16[256,256]{1,0:T(8,128)(2,1)S(1)}, bf16[8,128]{1,0:T(8,128)(2,1)S(1)}, bf16[512,256]{1,0:T(8,128)(2,1)S(1)}, bf...) custom-call(bf16[256,256]{1,0:T(8,128)(2,1)} %refs_0_.1, ...), custom_call_target="tpu_custom_call" | custom-call | flops 100000000 | bytes 1000000 | tf_op jit(solution)/shard_map/pallas_call | solution.py:367
  20.6 1.8 %collective-permute-start.6 = (bf16[128,1024]{1,0:T(8,128)(2,1)S(1)}, bf16[128,1024]{1,0:T(8,128)(2,1)S(1)}, u32[]{:S(2)}, u32[]{:S(2)}) collective-permute-start(bf16[128,1024]{1,0:T(8,128)(2,1)S(1)} %get-tuple-element.31.refs_2_.refs_18_), channel_id=1, source_target_pairs={{0,1},{1,0},{2,3},{3,2},{4,5},{5,4},{6,7},{7,6},{8,9},{9,8},{10,11... | collective-permute-start | bytes 786440 | tf_op jit(solution)/shard_map/ppermute | solution.py:398
  22.4 0.3 collective-permute-start.5
  22.7 1.3 %collective-permute-start = (bf16[8,128]{1,0:T(8,128)(2,1)S(1)}, bf16[8,128]{1,0:T(8,128)(2,1)S(1)}, u32[]{:S(2)}, u32[]{:S(2)}) collective-permute-start(bf16[8,128]{1,0:T(8,128)(2,1)S(1)} %get-tuple-element.21.refs_2_), channel_id=1, source_target_pairs={{2,0},{4,2},{6,4},{8,6},{10,8},{12,10},{14,12},{16,14},{18,16},{20... | collective-permute-start | bytes 6152 | tf_op jit(solution)/shard_map/ppermute | solution.py:387
  24.0 0.1 pad_add_fusion.refs_0_.place_ref
  24.0 5.8 %collective-permute-done.6.refs_3_ = bf16[128,1024]{1,0:T(8,128)(2,1)S(1)} collective-permute-done((bf16[128,1024]{1,0:T(8,128)(2,1)S(1)}, bf16[128,1024]{1,0:T(8,128)(2,1)S(1)}, u32[]{:S(2)}, u32[]{:S(2)}) %collective-permute-start.6) | collective-permute-done | bytes 262176 | tf_op jit(solution)/shard_map/ppermute | solution.py:398
  29.8 1.3 %collective-permute-start.1 = (bf16[8,128]{1,0:T(8,128)(2,1)S(1)}, bf16[8,128]{1,0:T(8,128)(2,1)S(1)}, u32[]{:S(2)}, u32[]{:S(2)}) collective-permute-start(bf16[8,128]{1,0:T(8,128)(2,1)S(1)} %get-tuple-element.21.refs_2_), channel_id=1, source_target_pairs={{4,0},{6,2},{8,4},{10,6},{12,8},{14,10},{16,12},{18,14},{20,16},{2... | collective-permute-start | bytes 6152 | tf_op jit(solution)/shard_map/ppermute | solution.py:387
  31.1 2.4 %shard_map.79 = (bf16[4,256,256]{2,1,0:T(8,128)(2,1)S(1)}, bf16[4,256,256]{2,1,0:T(8,128)(2,1)S(1)}, bf16[128,1024]{1,0:T(8,128)(2,1)S(1)}, bf16[128,1024]{1,0:T(8,128)(2,1)S(1)}) custom-call(s32[3]{0:T(128)S(1)} %pad_add_fusion.refs_0_.place_ref, s32[1,64]{1,0:T(1,128)S(1)} %get-tuple-element.20.refs_1_, ...), custom_call_target="tpu_custom_call" | custom-call | flops 100000000 | bytes 1000000 | tf_op jit(solution)/shard_map/pallas_call | solution.py:367
  33.5 0.2 collective-permute-done.5.refs_3_
  33.7 2.4 %shard_map.78 = (bf16[4,256,256]{2,1,0:T(8,128)(2,1)S(1)}, bf16[4,256,256]{2,1,0:T(8,128)(2,1)S(1)}, bf16[128,1024]{1,0:T(8,128)(2,1)S(1)}, bf16[128,1024]{1,0:T(8,128)(2,1)S(1)}) custom-call(s32[3]{0:T(128)S(1)} %pad_add_fusion.refs_0_.place_ref, s32[1,64]{1,0:T(1,128)S(1)} %get-tuple-element.20.refs_1_, ...), custom_call_target="tpu_custom_call" | custom-call | flops 100000000 | bytes 1000000 | tf_op jit(solution)/shard_map/pallas_call | solution.py:367
  36.1 0.0 collective-permute-done.refs_3_
  36.1 0.0 collective-permute-done.1.refs_4_
  36.1 0.0 collective-permute-done.2
  36.1 0.0 collective-permute-done.4
  36.1 5.4 %shard_map.80 = (f32[2,144,128]{2,1,0:T(8,128)S(1)}, f32[2,144,128]{2,1,0:T(8,128)S(1)}) custom-call(s32[3]{0:T(128)S(1)} %pad_add_fusion.refs_0_.place_ref, s32[1,64]{1,0:T(1,128)S(1)} %get-tuple-element.20.refs_1_, bf16[8,128]{1,0:T(8,128)(2,1)S(1)} %get-tuple-element.21.refs_2_, bf16[8,128]{1,0:T(8,128)(2,1)S(1)} %collective-permute-done.refs_3_, ...), custom_call_target="tpu_custom_call" | custom-call | flops 100000000 | bytes 1000000 | tf_op jit(solution)/shard_map/pallas_call | solution.py:367
  41.5 0.1 collective-permute-start.7
  41.6 1.4 %collective-permute-done.7 = f32[2,144,128]{2,1,0:T(8,128)S(1)} collective-permute-done((f32[2,144,128]{2,1,0:T(8,128)S(1)}, f32[2,144,128]{2,1,0:T(8,128)S(1)}, u32[]{:S(2)}, u32[]{:S(2)}) %collective-permute-start.7) | collective-permute-done | bytes 147488 | tf_op jit(solution)/shard_map/ppermute | solution.py:403
  43.0 1.4 %collective-permute-start.8 = (bf16[144,128]{1,0:T(8,128)(2,1)S(1)}, bf16[144,128]{1,0:T(8,128)(2,1)S(1)}, u32[]{:S(2)}, u32[]{:S(2)}) collective-permute-start(bf16[144,128]{1,0:T(8,128)(2,1)S(1)} %fusion.1), channel_id=1, source_target_pairs={{0,3},{1,2},{2,1},{3,0},{4,7},{5,6},{6,5},{7,4},{8,11},{9,10},{10,... | collective-permute-start | bytes 110600 | tf_op jit(solution)/shard_map/ppermute | solution.py:445
  44.3 2.2 %collective-permute-done.8 = bf16[144,128]{1,0:T(8,128)(2,1)S(1)} collective-permute-done((bf16[144,128]{1,0:T(8,128)(2,1)S(1)}, bf16[144,128]{1,0:T(8,128)(2,1)S(1)}, u32[]{:S(2)}, u32[]{:S(2)}) %collective-permute-start.8) | collective-permute-done | bytes 36896 | tf_op jit(solution)/shard_map/ppermute | solution.py:445
  46.5 2.9 %collective-permute-start.9 = (f32[144,128]{1,0:T(8,128)S(1)}, f32[144,128]{1,0:T(8,128)S(1)}, u32[]{:S(2)}, u32[]{:S(2)}) collective-permute-start(f32[144,128]{1,0:T(8,128)S(1)} %fusion), channel_id=1, source_target_pairs={{0,6},{1,11},{2,8},{3,5},{4,14},{5,3},{6,0},{7,13},{8,2},{9,15},{1... | collective-permute-start | bytes 221192 | tf_op jit(solution)/shard_map/ppermute | solution.py:445
  49.4 2.0 %collective-permute-done.9 = f32[144,128]{1,0:T(8,128)S(1)} collective-permute-done((f32[144,128]{1,0:T(8,128)S(1)}, f32[144,128]{1,0:T(8,128)S(1)}, u32[]{:S(2)}, u32[]{:S(2)}) %collective-permute-start.9) | collective-permute-done | bytes 73760 | tf_op jit(solution)/shard_map/ppermute | solution.py:445
  51.4 3.2 %collective-permute-start.10 = (f32[144,128]{1,0:T(8,128)S(1)}, f32[144,128]{1,0:T(8,128)S(1)}, u32[]{:S(2)}, u32[]{:S(2)}) collective-permute-start(f32[144,128]{1,0:T(8,128)S(1)} %add.21), channel_id=1, source_target_pairs={{0,10},{1,19},{2,16},{3,9},{4,22},{5,15},{6,12},{7,21},{8,26},{9,3... | collective-permute-start | bytes 221192 | tf_op jit(solution)/shard_map/ppermute | solution.py:445
  54.7 2.0 %collective-permute-done.10 = f32[144,128]{1,0:T(8,128)S(1)} collective-permute-done((f32[144,128]{1,0:T(8,128)S(1)}, f32[144,128]{1,0:T(8,128)S(1)}, u32[]{:S(2)}, u32[]{:S(2)}) %collective-permute-start.10) | collective-permute-done | bytes 73760 | tf_op jit(solution)/shard_map/ppermute | solution.py:445
  56.7 3.5 %collective-permute-start.11 = (f32[144,128]{1,0:T(8,128)S(1)}, f32[144,128]{1,0:T(8,128)S(1)}, u32[]{:S(2)}, u32[]{:S(2)}) collective-permute-start(f32[144,128]{1,0:T(8,128)S(1)} %add.22), channel_id=1, source_target_pairs={{0,18},{1,7},{2,4},{3,17},{4,2},{5,23},{6,20},{7,1},{8,14},{9,27},... | collective-permute-start | bytes 221192 | tf_op jit(solution)/shard_map/ppermute | solution.py:445
  60.2 2.0 %collective-permute-done.11 = f32[144,128]{1,0:T(8,128)S(1)} collective-permute-done((f32[144,128]{1,0:T(8,128)S(1)}, f32[144,128]{1,0:T(8,128)S(1)}, u32[]{:S(2)}, u32[]{:S(2)}) %collective-permute-start.11) | collective-permute-done | bytes 73760 | tf_op jit(solution)/shard_map/ppermute | solution.py:445
  62.2 0.1 collective-permute-start.12
  62.3 1.2 %collective-permute-done.12.other_ref = f32[144,128]{1,0:T(8,128)S(1)} collective-permute-done((f32[144,128]{1,0:T(8,128)S(1)}, f32[144,128]{1,0:T(8,128)S(1)}, u32[]{:S(2)}, u32[]{:S(2)}) %collective-permute-start.12) | collective-permute-done | bytes 73760 | tf_op jit(solution)/shard_map/ppermute | solution.py:403
  63.6 1.3 %shard_map.81 = (f32[8,20]{1,0:T(8,128)}, f32[32,1024]{1,0:T(8,128)}) custom-call(s32[3]{0:T(128)S(1)} %pad_add_fusion.refs_0_.place_ref, f32[144,128]{1,0:T(8,128)S(1)} %add.23.own_ref, f32[144,128]{1,0:T(8,128)S(1)} %collective-permute-done.12.other_ref), custom_call_target="tpu_custom_call" | custom-call | flops 100000000 | bytes 1000000 | tf_op jit(solution)/shard_map/pallas_call | solution.py:367
  (6 shorter events, 0.1 us)
Async XLA Ops:
  0.6 17.0 %collective-permute-start.3 = (bf16[8,32,1024]{2,1,0:T(8,128)(2,1)}, bf16[8,32,1024]{2,1,0:T(8,128)(2,1)S(1)}, u32[]{:S(2)}, u32[]{:S(2)}) collective-permute-start(bf16[8,32,1024]{2,1,0:T(8,128)(2,1)} %refs_5_.1), channel_id=1, source_target_pairs={{4,0},{6,2},{8,4},{10,6},{12,8},{14,10},{16,12},{18,14},{20,16},{2... | collective-permute-start | bytes 1572872 | tf_op jit(solution)/shard_map/ppermute | solution.py:387
  1.9 34.1 %collective-permute-start.2 = (bf16[8,32,1024]{2,1,0:T(8,128)(2,1)}, bf16[8,32,1024]{2,1,0:T(8,128)(2,1)S(1)}, u32[]{:S(2)}, u32[]{:S(2)}) collective-permute-start(bf16[8,32,1024]{2,1,0:T(8,128)(2,1)} %refs_5_.1), channel_id=1, source_target_pairs={{2,0},{6,4},{10,8},{14,12},{18,16},{22,20},{26,24},{30,28},{3,1},{... | collective-permute-start | bytes 1572872 | tf_op jit(solution)/shard_map/ppermute | solution.py:387
  17.6 18.5 %collective-permute-start.4 = (bf16[8,32,1024]{2,1,0:T(8,128)(2,1)S(1)}, bf16[8,32,1024]{2,1,0:T(8,128)(2,1)S(1)}, u32[]{:S(2)}, u32[]{:S(2)}) collective-permute-start(bf16[8,32,1024]{2,1,0:T(8,128)(2,1)S(1)} %collective-permute-done.3), channel_id=1, source_target_pairs={{0,2},{4,6},{8,10},{12,14},{16,18},{20,22},{24,26},{28,30},{1,3},{... | collective-permute-start | bytes 1572872 | tf_op jit(solution)/shard_map/ppermute | solution.py:387
  20.6 9.2 %collective-permute-start.6 = (bf16[128,1024]{1,0:T(8,128)(2,1)S(1)}, bf16[128,1024]{1,0:T(8,128)(2,1)S(1)}, u32[]{:S(2)}, u32[]{:S(2)}) collective-permute-start(bf16[128,1024]{1,0:T(8,128)(2,1)S(1)} %get-tuple-element.31.refs_2_.refs_18_), channel_id=1, source_target_pairs={{0,1},{1,0},{2,3},{3,2},{4,5},{5,4},{6,7},{7,6},{8,9},{9,8},{10,11... | collective-permute-start | bytes 786440 | tf_op jit(solution)/shard_map/ppermute | solution.py:398
  22.4 11.3 %collective-permute-start.5 = (bf16[128,1024]{1,0:T(8,128)(2,1)S(1)}, bf16[128,1024]{1,0:T(8,128)(2,1)S(1)}, u32[]{:S(2)}, u32[]{:S(2)}) collective-permute-start(bf16[128,1024]{1,0:T(8,128)(2,1)S(1)} %get-tuple-element.23.refs_2_.refs_17_), channel_id=1, source_target_pairs={{0,1},{1,0},{2,3},{3,2},{4,5},{5,4},{6,7},{7,6},{8,9},{9,8},{10,11... | collective-permute-start | bytes 786440 | tf_op jit(solution)/shard_map/ppermute | solution.py:398
  22.7 13.4 %collective-permute-start = (bf16[8,128]{1,0:T(8,128)(2,1)S(1)}, bf16[8,128]{1,0:T(8,128)(2,1)S(1)}, u32[]{:S(2)}, u32[]{:S(2)}) collective-permute-start(bf16[8,128]{1,0:T(8,128)(2,1)S(1)} %get-tuple-element.21.refs_2_), channel_id=1, source_target_pairs={{2,0},{4,2},{6,4},{8,6},{10,8},{12,10},{14,12},{16,14},{18,16},{20... | collective-permute-start | bytes 6152 | tf_op jit(solution)/shard_map/ppermute | solution.py:387
  29.8 6.3 %collective-permute-start.1 = (bf16[8,128]{1,0:T(8,128)(2,1)S(1)}, bf16[8,128]{1,0:T(8,128)(2,1)S(1)}, u32[]{:S(2)}, u32[]{:S(2)}) collective-permute-start(bf16[8,128]{1,0:T(8,128)(2,1)S(1)} %get-tuple-element.21.refs_2_), channel_id=1, source_target_pairs={{4,0},{6,2},{8,4},{10,6},{12,8},{14,10},{16,12},{18,14},{20,16},{2... | collective-permute-start | bytes 6152 | tf_op jit(solution)/shard_map/ppermute | solution.py:387
  41.5 1.4 %collective-permute-start.7 = (f32[2,144,128]{2,1,0:T(8,128)S(1)}, f32[2,144,128]{2,1,0:T(8,128)S(1)}, u32[]{:S(2)}, u32[]{:S(2)}) collective-permute-start(f32[2,144,128]{2,1,0:T(8,128)S(1)} %get-tuple-element.37), channel_id=1, source_target_pairs={{0,2},{2,0},{4,6},{6,4},{8,10},{10,8},{12,14},{14,12},{16,18},{18,... | collective-permute-start | bytes 442376 | tf_op jit(solution)/shard_map/ppermute | solution.py:403
  43.0 3.5 %collective-permute-start.8 = (bf16[144,128]{1,0:T(8,128)(2,1)S(1)}, bf16[144,128]{1,0:T(8,128)(2,1)S(1)}, u32[]{:S(2)}, u32[]{:S(2)}) collective-permute-start(bf16[144,128]{1,0:T(8,128)(2,1)S(1)} %fusion.1), channel_id=1, source_target_pairs={{0,3},{1,2},{2,1},{3,0},{4,7},{5,6},{6,5},{7,4},{8,11},{9,10},{10,... | collective-permute-start | bytes 110600 | tf_op jit(solution)/shard_map/ppermute | solution.py:445
  46.5 4.9 %collective-permute-start.9 = (f32[144,128]{1,0:T(8,128)S(1)}, f32[144,128]{1,0:T(8,128)S(1)}, u32[]{:S(2)}, u32[]{:S(2)}) collective-permute-start(f32[144,128]{1,0:T(8,128)S(1)} %fusion), channel_id=1, source_target_pairs={{0,6},{1,11},{2,8},{3,5},{4,14},{5,3},{6,0},{7,13},{8,2},{9,15},{1... | collective-permute-start | bytes 221192 | tf_op jit(solution)/shard_map/ppermute | solution.py:445
  51.4 5.3 %collective-permute-start.10 = (f32[144,128]{1,0:T(8,128)S(1)}, f32[144,128]{1,0:T(8,128)S(1)}, u32[]{:S(2)}, u32[]{:S(2)}) collective-permute-start(f32[144,128]{1,0:T(8,128)S(1)} %add.21), channel_id=1, source_target_pairs={{0,10},{1,19},{2,16},{3,9},{4,22},{5,15},{6,12},{7,21},{8,26},{9,3... | collective-permute-start | bytes 221192 | tf_op jit(solution)/shard_map/ppermute | solution.py:445
  56.7 5.5 %collective-permute-start.11 = (f32[144,128]{1,0:T(8,128)S(1)}, f32[144,128]{1,0:T(8,128)S(1)}, u32[]{:S(2)}, u32[]{:S(2)}) collective-permute-start(f32[144,128]{1,0:T(8,128)S(1)} %add.22), channel_id=1, source_target_pairs={{0,18},{1,7},{2,4},{3,17},{4,2},{5,23},{6,20},{7,1},{8,14},{9,27},... | collective-permute-start | bytes 221192 | tf_op jit(solution)/shard_map/ppermute | solution.py:445
  62.2 1.3 %collective-permute-start.12 = (f32[144,128]{1,0:T(8,128)S(1)}, f32[144,128]{1,0:T(8,128)S(1)}, u32[]{:S(2)}, u32[]{:S(2)}) collective-permute-start(f32[144,128]{1,0:T(8,128)S(1)} %add.23.own_ref), channel_id=1, source_target_pairs={{0,2},{2,0},{4,6},{6,4},{8,10},{10,8},{12,14},{14,12},{16,18},{18,... | collective-permute-start | bytes 221192 | tf_op jit(solution)/shard_map/ppermute | solution.py:403

commit v5 on v4

--- a/solution.py
+++ b/solution.py
@@ -133,17 +133,36 @@
     )
 
 
+def load(ins, targets, sems):
+    copies = [
+        pltpu.make_async_copy(a, b, sems.at[i]) for i, (a, b) in enumerate(zip(ins, targets))
+    ]
+    for copy in copies:
+        copy.start()
+    return copies
+
+
+def mask_rows(ref, live_row, whole_ref):
+    own_count = live_row.shape[1]
+    diagonal = iota((own_count, own_count), 0) == iota((own_count, own_count), 1)
+    live = jnp.sum(jnp.where(diagonal, live_row.astype(F4), 0.0), axis=1, keepdims=True).astype(BF)
+    for p in range(whole_ref.shape[0]):
+        ref[p * own_count : (p + 1) * own_count] = whole_ref[p] * live
+
+
+def pack_kernel(live_hbm, whole_hbm, part_ref, live_ref, whole_ref, sems):
+    copies = load((live_hbm, whole_hbm.at[: CHUNKS[0]]), (live_ref, whole_ref), sems)
+    for copy in copies:
+        copy.wait()
+    mask_rows(part_ref, live_ref[...], whole_ref)
+
+
 def tables_kernel(*refs):
     ins, outs = refs[:6], refs[6:-5]
-    pairs_ref, vir_ref, meta_ref, both_ref, cols_ref, vir_t_ref = outs[:6]
-    parts = outs[6:]
+    pairs_ref, vir_ref, meta_ref, both_ref, cols_ref, vir_t_ref, part_ref = outs
     occ_ref, screened_ref, live_ref, whole_ref, sems = refs[-5:]
     targets = (occ_ref, vir_ref, screened_ref, live_ref, pairs_ref, whole_ref)
-    copies = [
-        pltpu.make_async_copy(a, b, sems.at[i]) for i, (a, b) in enumerate(zip(ins, targets))
-    ]
-    for copy in copies:
-        copy.start()
+    copies = load(ins[:-1] + (ins[-1].at[CHUNKS[0] :],), targets, sems)
     for copy in copies[:-1]:
         copy.wait()
     own_count = live_ref.shape[1]
@@ -163,15 +182,8 @@
     both_ref[:NORB] = both.T.astype(BF)
     both_ref[NORB:] = both.astype(BF)
     vir_t_ref[...] = vir_ref[...].astype(F4).T.astype(BF)
-    diagonal = iota((own_count, own_count), 0) == iota((own_count, own_count), 1)
-    live = jnp.where(diagonal, live_ref[...].astype(F4), 0.0)
-    live = jnp.sum(live, axis=1, keepdims=True).astype(BF)
     copies[-1].wait()
-    at = 0
-    for ref in parts:
-        for p in range(ref.shape[0] // own_count):
-            ref[p * own_count : (p + 1) * own_count] = whole_ref[at] * live
-            at += 1
+    mask_rows(part_ref, live_ref[...], whole_ref)
 
 
 def own_kernel(count, own_count, place_ref, pairs_ref, *refs):
@@ -214,9 +226,9 @@
 
 
 def window_kernel(lanes, sigma_scale, chi_scale, place_ref, *refs):
-    (pairs_ref, meta0, meta1, meta2, tile1a, tile1b, tile2, cols_ref) = refs[:8]
+    (pairs_ref, meta0, meta1a, meta1b, meta2, tile1a, tile1b, tile2, cols_ref) = refs[:9]
     keep_ref, send_ref, near_ref, mixed_ref, other_ref = refs[-5:]
-    own, tile0 = refs[8 : 8 + 4 * len(CHUNKS)], refs[8 + 4 * len(CHUNKS) : -5]
+    own, tile0 = refs[9 : 9 + 4 * len(CHUNKS)], refs[9 + 4 * len(CHUNKS) : -5]
     matrices = [ref[p] for ref in own[::4] for p in range(ref.shape[0])]
     rights = [ref[p] for ref in own[1::4] for p in range(ref.shape[0])]
     z = jnp.concatenate([ref[...] for ref in own[2::4]], axis=0)
@@ -230,9 +242,9 @@
     same = (mod(row, own_count) == mod(col, own_count)).astype(F4)
     spread_row, spread_col = iota((LANE, rows), 0), iota((LANE, rows), 1)
     spread = onehot(spread_row == LIVE_AT + mod(spread_col, own_count))
-    metas = [m[...] for m in (meta0, meta1, meta2)]
+    metas = [meta0[...], jnp.where((block & 1) == 0, meta1a[...], meta1b[...]), meta2[...]]
     masks = [same * mm(m, spread)[0:1, :] for m in metas]
-    near_ref[...] = tile1a[...] + tile1b[...]
+    near_ref[...] = jnp.where((block & 1) == 0, tile1a[...], tile1b[...])
     tiles = [jnp.concatenate([t[...] for t in tile0], axis=0), near_ref, tile2]
 
     def spread_rows(value):
@@ -403,9 +415,29 @@
         return lax.ppermute(value, "aux", [(s, s ^ mask) for s in range(aux_count)])
 
     far = shifted(three_center, -2)
-    near_even = shifted(three_center, -1, 1)
+    near_even = flipped(three_center, 1)
     square = shape((NORB, NORB), BF)
-    pairs, vir, meta, both, cols, vir_t, *parts = call(
+
+    def part_of(c):
+        return shape((CHUNKS[c] * own_count, PAIR), BF)
+
+    def whole_of(c):
+        return pltpu.VMEM((CHUNKS[c], own_count, PAIR), BF)
+
+    hbm = pl.BlockSpec(memory_space=pltpu.HBM)
+    first_part = call(
+        pack_kernel,
+        [part_of(0)],
+        tile_live,
+        three_center,
+        scratch=[
+            pltpu.VMEM(tile_live.shape, jnp.int32),
+            whole_of(0),
+            pltpu.SemaphoreType.DMA((2,)),
+        ],
+        ins=hbm,
+    )[0]
+    pairs, vir, meta, both, cols, vir_t, second_part = call(
         tables_kernel,
         [
             shape((1, pair_count * own_count), jnp.int32),
@@ -414,8 +446,8 @@
             shape((2 * NORB, NORB), BF),
             square,
             square,
-        ]
-        + [shape((c * own_count, PAIR), BF) for c in CHUNKS],
+            part_of(1),
+        ],
         green_occ,
         green_vir,
         screened,
@@ -426,17 +458,19 @@
             pltpu.VMEM((NORB, NORB), BF),
             pltpu.VMEM(screened.shape, BF),
             pltpu.VMEM(tile_live.shape, jnp.int32),
-            pltpu.VMEM(three_center.shape, BF),
+            whole_of(1),
             pltpu.SemaphoreType.DMA((6,)),
         ],
-        ins=pl.BlockSpec(memory_space=pltpu.HBM),
+        ins=hbm,
     )
+    parts = [first_part, second_part]
     pieces = []
     for part in parts:
         pieces.append([part] + [turned(part, s) for s in range(1, pair_count)])
-    meta_near = shifted(meta, -1)
+    meta_even = flipped(meta, 1)
     meta_far = shifted(meta, -2)
-    near_odd = shifted(far, 1, 0)
+    near_odd = flipped(far, 1)
+    meta_odd = flipped(meta_far, 1)
     turn = pair_count == 2
     half_at = (lax.population_count(block) + (pair_at if turn else 0)) & 1
     place = jnp.stack([block, pair_at, half_at]).astype(jnp.int32)
@@ -483,7 +517,8 @@
         place,
         pairs,
         meta,
-        meta_near,
+        meta_even,
+        meta_odd,
         meta_far,
         near_even.reshape(rows, PAIR),
         near_odd.reshape(rows, PAIR),

time: 65.1 us -> 63.3 us (0.972)
  starting transfers between devices: 19.6 us -> 14.3 us
  waiting for transfers between devices: 31.3 us -> 33.2 us
  Pallas kernels: 13 us -> 14.2 us
    ppermute x5 -> x2, waiting for transfers between devices: 14.4 us -> 19.9 us  [shifted(): lax.ppermute(value, 'aux', [(s, s + steps) for s in range(aux_count) if 0...]
    ppermute x5 -> x2, starting transfers between devices: 6.46 us -> 2.57 us  [shifted(): lax.ppermute(value, 'aux', [(s, s + steps) for s in range(aux_count) if 0...]
    ppermute x2, waiting for transfers between devices: 6 us -> 2.22 us  [turned(): lax.ppermute(value, 'pair', [(s, (s - steps) % pair_count) for s in range...]
    ppermute x4, starting transfers between devices: 10.9 us -> 8.13 us  [joint(): lax.ppermute(value, ('aux', 'pair'), [(s * pair_count + p, t * pair_count...]
    ppermute x2 -> x6, starting transfers between devices: 0.15 us -> 1.48 us  [flipped(): return lax.ppermute(value, 'aux', [(s, s ^ mask) for s in range(aux_count)])]
    pallas_call x5 -> x6, Pallas kernels: 13 us -> 14.2 us  [call(): pl.pallas_call(body, out_shape=outs, in_specs=[pl.BlockSpec(memory_space=...]
    ppermute x2 -> x6, waiting for transfers between devices: 2.61 us -> 2.36 us  [flipped(): return lax.ppermute(value, 'aux', [(s, s ^ mask) for s in range(aux_count)])]
  transfers between devices with their start and end apart: 13 -> 14, of which waited for: 9 -> 9; matrix products, arithmetic and copies ran while one was open for 0% -> 0% of each run, Pallas kernels for 10% -> 12%
where the time goes in v5:
time: 63.3 us; the launch traced here: 62.6 us
  waiting for transfers between devices  33.2 us (52%)
  starting transfers between devices  14.3 us (23%)
  Pallas kernels  14.2 us (22%)
  between operations  0.76 us (1%)
    ppermute x2, waiting for transfers between devices, shifted(): lax.ppermute(value, 'aux', [(s, s + steps) for s in range(aux_count) if 0...  19.9 us
    pallas_call x6, Pallas kernels, call(): pl.pallas_call(body, out_shape=outs, in_specs=[pl.BlockSpec(memory_space=...  14.2 us
    ppermute x4, waiting for transfers between devices, joint(): lax.ppermute(value, ('aux', 'pair'), [(s * pair_count + p, t * pair_count...  8.8 us
    ppermute x4, starting transfers between devices, joint(): lax.ppermute(value, ('aux', 'pair'), [(s * pair_count + p, t * pair_count...  8.13 us
    ppermute x2, starting transfers between devices, shifted(): lax.ppermute(value, 'aux', [(s, s + steps) for s in range(aux_count) if 0...  2.57 us
    ppermute x6, waiting for transfers between devices, flipped(): return lax.ppermute(value, 'aux', [(s, s ^ mask) for s in range(aux_count)])  2.36 us
    ppermute x2, waiting for transfers between devices, turned(): lax.ppermute(value, 'pair', [(s, (s - steps) % pair_count) for s in range...  2.22 us
    ppermute x2, starting transfers between devices, turned(): lax.ppermute(value, 'pair', [(s, (s - steps) % pair_count) for s in range...  2.16 us
  transfers between devices with their start and end apart: 14, of which 9 were waited for; matrix products, arithmetic and copies ran while one was open for 0% of the time, Pallas kernels for 12%

profile of v5, /device:TPU:0, one launch (start us, length us, event | category | flops | bytes accessed | tf_op | source)
XLA Modules:
  0.0 62.6 jit_solution(16470455908987459527)
XLA Ops:
  0.6 1.3 %collective-permute-start.4 = (bf16[8,32,1024]{2,1,0:T(8,128)(2,1)}, bf16[8,32,1024]{2,1,0:T(8,128)(2,1)S(1)}, u32[]{:S(2)}, u32[]{:S(2)}) collective-permute-start(bf16[8,32,1024]{2,1,0:T(8,128)(2,1)} %whole_hbm.1), channel_id=1, source_target_pairs={{4,0},{6,2},{8,4},{10,6},{12,8},{14,10},{16,12},{18,14},{20,16},{2... | collective-permute-start | bytes 1572872 | tf_op jit(solution)/shard_map/ppermute | solution.py:399
  1.9 0.6 collective-permute-start.3
  2.5 15.1 %collective-permute-done.4 = bf16[8,32,1024]{2,1,0:T(8,128)(2,1)S(1)} collective-permute-done((bf16[8,32,1024]{2,1,0:T(8,128)(2,1)}, bf16[8,32,1024]{2,1,0:T(8,128)(2,1)S(1)}, u32[]{:S(2)}, u32[]{:S(2)}) %collective-permute-start.4) | collective-permute-done | bytes 524320 | tf_op jit(solution)/shard_map/ppermute | solution.py:399
  17.6 0.0 collective-permute-start.5
  17.6 1.7 %shard_map.77 = (s32[1,64]{1,0:T(1,128)S(1)}, bf16[256,256]{1,0:T(8,128)(2,1)S(1)}, bf16[8,128]{1,0:T(8,128)(2,1)S(1)}, bf16[512,256]{1,0:T(8,128)(2,1)S(1)}, bf...) custom-call(bf16[256,256]{1,0:T(8,128)(2,1)} %refs_0_.1, ...), custom_call_target="tpu_custom_call" | custom-call | flops 100000000 | bytes 1000000 | tf_op jit(solution)/shard_map/pallas_call | solution.py:379
  19.3 1.8 %collective-permute-start.7 = (bf16[128,1024]{1,0:T(8,128)(2,1)S(1)}, bf16[128,1024]{1,0:T(8,128)(2,1)S(1)}, u32[]{:S(2)}, u32[]{:S(2)}) collective-permute-start(bf16[128,1024]{1,0:T(8,128)(2,1)S(1)} %get-tuple-element.29.refs_2_.refs_19_), channel_id=1, source_target_pairs={{0,1},{1,0},{2,3},{3,2},{4,5},{5,4},{6,7},{7,6},{8,9},{9,8},{10,11... | collective-permute-start | bytes 786440 | tf_op jit(solution)/shard_map/ppermute | solution.py:410
  21.1 1.1 %shard_map.78.refs_2_.refs_18_ = bf16[128,1024]{1,0:T(8,128)(2,1)S(1)} custom-call(s32[1,32]{1,0:T(1,128)} %live_hbm.1, bf16[8,32,1024]{2,1,0:T(8,128)(2,1)} %whole_hbm.1), custom_call_target="tpu_custom_call" | custom-call | flops 100000000 | bytes 1000000 | tf_op jit(solution)/shard_map/pallas_call | solution.py:379
  22.2 0.3 collective-permute-start.6
  22.6 1.3 %collective-permute-start.1 = (bf16[8,128]{1,0:T(8,128)(2,1)S(1)}, bf16[8,128]{1,0:T(8,128)(2,1)S(1)}, u32[]{:S(2)}, u32[]{:S(2)}) collective-permute-start(bf16[8,128]{1,0:T(8,128)(2,1)S(1)} %get-tuple-element.20.refs_2_), channel_id=1, source_target_pairs={{4,0},{6,2},{8,4},{10,6},{12,8},{14,10},{16,12},{18,14},{20,16},{2... | collective-permute-start | bytes 6152 | tf_op jit(solution)/shard_map/ppermute | solution.py:399
  23.9 0.1 pad_add_fusion.refs_0_.place_ref
  23.9 4.7 %collective-permute-done.1.refs_5_ = bf16[8,128]{1,0:T(8,128)(2,1)S(1)} collective-permute-done((bf16[8,128]{1,0:T(8,128)(2,1)S(1)}, bf16[8,128]{1,0:T(8,128)(2,1)S(1)}, u32[]{:S(2)}, u32[]{:S(2)}) %collective-permute-start.1) | collective-permute-done | bytes 2080 | tf_op jit(solution)/shard_map/ppermute | solution.py:399
  28.6 0.0 collective-permute-start
  28.7 0.0 collective-permute-done.7.refs_3_
  28.7 0.5 collective-permute-start.2
  29.2 2.4 %shard_map.80 = (bf16[4,256,256]{2,1,0:T(8,128)(2,1)S(1)}, bf16[4,256,256]{2,1,0:T(8,128)(2,1)S(1)}, bf16[128,1024]{1,0:T(8,128)(2,1)S(1)}, bf16[128,1024]{1,0:T(8,128)(2,1)S(1)}) custom-call(s32[3]{0:T(128)S(1)} %pad_add_fusion.refs_0_.place_ref, s32[1,64]{1,0:T(1,128)S(1)} %get-tuple-element.19.refs_1_, ...), custom_call_target="tpu_custom_call" | custom-call | flops 100000000 | bytes 1000000 | tf_op jit(solution)/shard_map/pallas_call | solution.py:379
  31.5 2.2 %collective-permute-done.6.refs_3_ = bf16[128,1024]{1,0:T(8,128)(2,1)S(1)} collective-permute-done((bf16[128,1024]{1,0:T(8,128)(2,1)S(1)}, bf16[128,1024]{1,0:T(8,128)(2,1)S(1)}, u32[]{:S(2)}, u32[]{:S(2)}) %collective-permute-start.6) | collective-permute-done | bytes 262176 | tf_op jit(solution)/shard_map/ppermute | solution.py:410
  33.7 2.4 %shard_map.79 = (bf16[4,256,256]{2,1,0:T(8,128)(2,1)S(1)}, bf16[4,256,256]{2,1,0:T(8,128)(2,1)S(1)}, bf16[128,1024]{1,0:T(8,128)(2,1)S(1)}, bf16[128,1024]{1,0:T(8,128)(2,1)S(1)}) custom-call(s32[3]{0:T(128)S(1)} %pad_add_fusion.refs_0_.place_ref, s32[1,64]{1,0:T(1,128)S(1)} %get-tuple-element.19.refs_1_, bf16[128,1024]{1,0:T(8,128)(2,1)S(1)} %shard_map.78.refs_2_.refs_18_, ...), custom_call_target="tpu_custom_call" | custom-call | flops 100000000 | bytes 1000000 | tf_op jit(solution)/shard_map/pallas_call | solution.py:379
  36.1 0.0 collective-permute-done.refs_3_
  36.1 0.0 collective-permute-done.2.refs_4_
  36.1 0.0 collective-permute-done.3
  36.1 0.0 collective-permute-done.5
  36.2 5.4 %shard_map.81 = (f32[2,144,128]{2,1,0:T(8,128)S(1)}, f32[2,144,128]{2,1,0:T(8,128)S(1)}) custom-call(s32[3]{0:T(128)S(1)} %pad_add_fusion.refs_0_.place_ref, s32[1,64]{1,0:T(1,128)S(1)} %get-tuple-element.19.refs_1_, bf16[8,128]{1,0:T(8,128)(2,1)S(1)} %get-tuple-element.20.refs_2_, bf16[8,128]{1,0:T(8,128)(2,1)S(1)} %collective-permute-done.refs_3_, ...), custom_call_target="tpu_custom_call" | custom-call | flops 100000000 | bytes 1000000 | tf_op jit(solution)/shard_map/pallas_call | solution.py:379
  41.6 0.1 collective-permute-start.8
  41.6 1.4 %collective-permute-done.8 = f32[2,144,128]{2,1,0:T(8,128)S(1)} collective-permute-done((f32[2,144,128]{2,1,0:T(8,128)S(1)}, f32[2,144,128]{2,1,0:T(8,128)S(1)}, u32[]{:S(2)}, u32[]{:S(2)}) %collective-permute-start.8) | collective-permute-done | bytes 147488 | tf_op jit(solution)/shard_map/ppermute | solution.py:415
  43.0 1.5 %collective-permute-start.9 = (bf16[144,128]{1,0:T(8,128)(2,1)S(1)}, bf16[144,128]{1,0:T(8,128)(2,1)S(1)}, u32[]{:S(2)}, u32[]{:S(2)}) collective-permute-start(bf16[144,128]{1,0:T(8,128)(2,1)S(1)} %fusion.1), channel_id=1, source_target_pairs={{0,3},{1,2},{2,1},{3,0},{4,7},{5,6},{6,5},{7,4},{8,11},{9,10},{10,... | collective-permute-start | bytes 110600 | tf_op jit(solution)/shard_map/ppermute | solution.py:479
  44.6 2.0 %collective-permute-done.9 = bf16[144,128]{1,0:T(8,128)(2,1)S(1)} collective-permute-done((bf16[144,128]{1,0:T(8,128)(2,1)S(1)}, bf16[144,128]{1,0:T(8,128)(2,1)S(1)}, u32[]{:S(2)}, u32[]{:S(2)}) %collective-permute-start.9) | collective-permute-done | bytes 36896 | tf_op jit(solution)/shard_map/ppermute | solution.py:479
  46.6 2.4 %collective-permute-start.10 = (f32[144,128]{1,0:T(8,128)S(1)}, f32[144,128]{1,0:T(8,128)S(1)}, u32[]{:S(2)}, u32[]{:S(2)}) collective-permute-start(f32[144,128]{1,0:T(8,128)S(1)} %fusion), channel_id=1, source_target_pairs={{0,6},{1,11},{2,8},{3,5},{4,14},{5,3},{6,0},{7,13},{8,2},{9,15},{1... | collective-permute-start | bytes 221192 | tf_op jit(solution)/shard_map/ppermute | solution.py:479
  49.0 2.0 %collective-permute-done.10 = f32[144,128]{1,0:T(8,128)S(1)} collective-permute-done((f32[144,128]{1,0:T(8,128)S(1)}, f32[144,128]{1,0:T(8,128)S(1)}, u32[]{:S(2)}, u32[]{:S(2)}) %collective-permute-start.10) | collective-permute-done | bytes 73760 | tf_op jit(solution)/shard_map/ppermute | solution.py:479
  51.0 1.6 %collective-permute-start.11 = (f32[144,128]{1,0:T(8,128)S(1)}, f32[144,128]{1,0:T(8,128)S(1)}, u32[]{:S(2)}, u32[]{:S(2)}) collective-permute-start(f32[144,128]{1,0:T(8,128)S(1)} %add.21), channel_id=1, source_target_pairs={{0,10},{1,19},{2,16},{3,9},{4,22},{5,15},{6,12},{7,21},{8,26},{9,3... | collective-permute-start | bytes 221192 | tf_op jit(solution)/shard_map/ppermute | solution.py:479
  52.7 2.6 %collective-permute-done.11 = f32[144,128]{1,0:T(8,128)S(1)} collective-permute-done((f32[144,128]{1,0:T(8,128)S(1)}, f32[144,128]{1,0:T(8,128)S(1)}, u32[]{:S(2)}, u32[]{:S(2)}) %collective-permute-start.11) | collective-permute-done | bytes 73760 | tf_op jit(solution)/shard_map/ppermute | solution.py:479
  55.3 2.6 %collective-permute-start.12 = (f32[144,128]{1,0:T(8,128)S(1)}, f32[144,128]{1,0:T(8,128)S(1)}, u32[]{:S(2)}, u32[]{:S(2)}) collective-permute-start(f32[144,128]{1,0:T(8,128)S(1)} %add.22), channel_id=1, source_target_pairs={{0,18},{1,7},{2,4},{3,17},{4,2},{5,23},{6,20},{7,1},{8,14},{9,27},... | collective-permute-start | bytes 221192 | tf_op jit(solution)/shard_map/ppermute | solution.py:479
  57.8 2.2 %collective-permute-done.12 = f32[144,128]{1,0:T(8,128)S(1)} collective-permute-done((f32[144,128]{1,0:T(8,128)S(1)}, f32[144,128]{1,0:T(8,128)S(1)}, u32[]{:S(2)}, u32[]{:S(2)}) %collective-permute-start.12) | collective-permute-done | bytes 73760 | tf_op jit(solution)/shard_map/ppermute | solution.py:479
  60.0 0.3 collective-permute-start.13
  60.4 1.0 %collective-permute-done.13.other_ref = f32[144,128]{1,0:T(8,128)S(1)} collective-permute-done((f32[144,128]{1,0:T(8,128)S(1)}, f32[144,128]{1,0:T(8,128)S(1)}, u32[]{:S(2)}, u32[]{:S(2)}) %collective-permute-start.13) | collective-permute-done | bytes 73760 | tf_op jit(solution)/shard_map/ppermute | solution.py:415
  61.3 1.3 %shard_map.82 = (f32[8,20]{1,0:T(8,128)}, f32[32,1024]{1,0:T(8,128)}) custom-call(s32[3]{0:T(128)S(1)} %pad_add_fusion.refs_0_.place_ref, f32[144,128]{1,0:T(8,128)S(1)} %add.23.own_ref, f32[144,128]{1,0:T(8,128)S(1)} %collective-permute-done.13.other_ref), custom_call_target="tpu_custom_call" | custom-call | flops 100000000 | bytes 1000000 | tf_op jit(solution)/shard_map/pallas_call | solution.py:379
  (6 shorter events, 0.1 us)
Async XLA Ops:
  0.6 17.0 %collective-permute-start.4 = (bf16[8,32,1024]{2,1,0:T(8,128)(2,1)}, bf16[8,32,1024]{2,1,0:T(8,128)(2,1)S(1)}, u32[]{:S(2)}, u32[]{:S(2)}) collective-permute-start(bf16[8,32,1024]{2,1,0:T(8,128)(2,1)} %whole_hbm.1), channel_id=1, source_target_pairs={{4,0},{6,2},{8,4},{10,6},{12,8},{14,10},{16,12},{18,14},{20,16},{2... | collective-permute-start | bytes 1572872 | tf_op jit(solution)/shard_map/ppermute | solution.py:399
  1.9 34.2 %collective-permute-start.3 = (bf16[8,32,1024]{2,1,0:T(8,128)(2,1)}, bf16[8,32,1024]{2,1,0:T(8,128)(2,1)S(1)}, u32[]{:S(2)}, u32[]{:S(2)}) collective-permute-start(bf16[8,32,1024]{2,1,0:T(8,128)(2,1)} %whole_hbm.1), channel_id=1, source_target_pairs={{0,2},{2,0},{4,6},{6,4},{8,10},{10,8},{12,14},{14,12},{16,18},{18,... | collective-permute-start | bytes 1572872 | tf_op jit(solution)/shard_map/ppermute | solution.py:415
  17.6 18.5 %collective-permute-start.5 = (bf16[8,32,1024]{2,1,0:T(8,128)(2,1)S(1)}, bf16[8,32,1024]{2,1,0:T(8,128)(2,1)S(1)}, u32[]{:S(2)}, u32[]{:S(2)}) collective-permute-start(bf16[8,32,1024]{2,1,0:T(8,128)(2,1)S(1)} %collective-permute-done.4), channel_id=1, source_target_pairs={{0,2},{2,0},{4,6},{6,4},{8,10},{10,8},{12,14},{14,12},{16,18},{18,... | collective-permute-start | bytes 1572872 | tf_op jit(solution)/shard_map/ppermute | solution.py:415
  19.3 9.3 %collective-permute-start.7 = (bf16[128,1024]{1,0:T(8,128)(2,1)S(1)}, bf16[128,1024]{1,0:T(8,128)(2,1)S(1)}, u32[]{:S(2)}, u32[]{:S(2)}) collective-permute-start(bf16[128,1024]{1,0:T(8,128)(2,1)S(1)} %get-tuple-element.29.refs_2_.refs_19_), channel_id=1, source_target_pairs={{0,1},{1,0},{2,3},{3,2},{4,5},{5,4},{6,7},{7,6},{8,9},{9,8},{10,11... | collective-permute-start | bytes 786440 | tf_op jit(solution)/shard_map/ppermute | solution.py:410
  22.2 11.5 %collective-permute-start.6 = (bf16[128,1024]{1,0:T(8,128)(2,1)S(1)}, bf16[128,1024]{1,0:T(8,128)(2,1)S(1)}, u32[]{:S(2)}, u32[]{:S(2)}) collective-permute-start(bf16[128,1024]{1,0:T(8,128)(2,1)S(1)} %shard_map.78.refs_2_.refs_18_), channel_id=1, source_target_pairs={{0,1},{1,0},{2,3},{3,2},{4,5},{5,4},{6,7},{7,6},{8,9},{9,8},{10,11... | collective-permute-start | bytes 786440 | tf_op jit(solution)/shard_map/ppermute | solution.py:410
  22.6 6.1 %collective-permute-start.1 = (bf16[8,128]{1,0:T(8,128)(2,1)S(1)}, bf16[8,128]{1,0:T(8,128)(2,1)S(1)}, u32[]{:S(2)}, u32[]{:S(2)}) collective-permute-start(bf16[8,128]{1,0:T(8,128)(2,1)S(1)} %get-tuple-element.20.refs_2_), channel_id=1, source_target_pairs={{4,0},{6,2},{8,4},{10,6},{12,8},{14,10},{16,12},{18,14},{20,16},{2... | collective-permute-start | bytes 6152 | tf_op jit(solution)/shard_map/ppermute | solution.py:399
  28.6 7.5 %collective-permute-start = (bf16[8,128]{1,0:T(8,128)(2,1)S(1)}, bf16[8,128]{1,0:T(8,128)(2,1)S(1)}, u32[]{:S(2)}, u32[]{:S(2)}) collective-permute-start(bf16[8,128]{1,0:T(8,128)(2,1)S(1)} %get-tuple-element.20.refs_2_), channel_id=1, source_target_pairs={{0,2},{2,0},{4,6},{6,4},{8,10},{10,8},{12,14},{14,12},{16,18},{18,... | collective-permute-start | bytes 6152 | tf_op jit(solution)/shard_map/ppermute | solution.py:415
  28.7 7.5 %collective-permute-start.2 = (bf16[8,128]{1,0:T(8,128)(2,1)S(1)}, bf16[8,128]{1,0:T(8,128)(2,1)S(1)}, u32[]{:S(2)}, u32[]{:S(2)}) collective-permute-start(bf16[8,128]{1,0:T(8,128)(2,1)S(1)} %collective-permute-done.1.refs_5_), channel_id=1, source_target_pairs={{0,2},{2,0},{4,6},{6,4},{8,10},{10,8},{12,14},{14,12},{16,18},{18,... | collective-permute-start | bytes 6152 | tf_op jit(solution)/shard_map/ppermute | solution.py:415
  41.6 1.4 %collective-permute-start.8 = (f32[2,144,128]{2,1,0:T(8,128)S(1)}, f32[2,144,128]{2,1,0:T(8,128)S(1)}, u32[]{:S(2)}, u32[]{:S(2)}) collective-permute-start(f32[2,144,128]{2,1,0:T(8,128)S(1)} %get-tuple-element.35), channel_id=1, source_target_pairs={{0,2},{2,0},{4,6},{6,4},{8,10},{10,8},{12,14},{14,12},{16,18},{18,... | collective-permute-start | bytes 442376 | tf_op jit(solution)/shard_map/ppermute | solution.py:415
  43.0 3.5 %collective-permute-start.9 = (bf16[144,128]{1,0:T(8,128)(2,1)S(1)}, bf16[144,128]{1,0:T(8,128)(2,1)S(1)}, u32[]{:S(2)}, u32[]{:S(2)}) collective-permute-start(bf16[144,128]{1,0:T(8,128)(2,1)S(1)} %fusion.1), channel_id=1, source_target_pairs={{0,3},{1,2},{2,1},{3,0},{4,7},{5,6},{6,5},{7,4},{8,11},{9,10},{10,... | collective-permute-start | bytes 110600 | tf_op jit(solution)/shard_map/ppermute | solution.py:479
  46.6 4.5 %collective-permute-start.10 = (f32[144,128]{1,0:T(8,128)S(1)}, f32[144,128]{1,0:T(8,128)S(1)}, u32[]{:S(2)}, u32[]{:S(2)}) collective-permute-start(f32[144,128]{1,0:T(8,128)S(1)} %fusion), channel_id=1, source_target_pairs={{0,6},{1,11},{2,8},{3,5},{4,14},{5,3},{6,0},{7,13},{8,2},{9,15},{1... | collective-permute-start | bytes 221192 | tf_op jit(solution)/shard_map/ppermute | solution.py:479
  51.0 4.2 %collective-permute-start.11 = (f32[144,128]{1,0:T(8,128)S(1)}, f32[144,128]{1,0:T(8,128)S(1)}, u32[]{:S(2)}, u32[]{:S(2)}) collective-permute-start(f32[144,128]{1,0:T(8,128)S(1)} %add.21), channel_id=1, source_target_pairs={{0,10},{1,19},{2,16},{3,9},{4,22},{5,15},{6,12},{7,21},{8,26},{9,3... | collective-permute-start | bytes 221192 | tf_op jit(solution)/shard_map/ppermute | solution.py:479
  55.3 4.7 %collective-permute-start.12 = (f32[144,128]{1,0:T(8,128)S(1)}, f32[144,128]{1,0:T(8,128)S(1)}, u32[]{:S(2)}, u32[]{:S(2)}) collective-permute-start(f32[144,128]{1,0:T(8,128)S(1)} %add.22), channel_id=1, source_target_pairs={{0,18},{1,7},{2,4},{3,17},{4,2},{5,23},{6,20},{7,1},{8,14},{9,27},... | collective-permute-start | bytes 221192 | tf_op jit(solution)/shard_map/ppermute | solution.py:479
  60.0 1.3 %collective-permute-start.13 = (f32[144,128]{1,0:T(8,128)S(1)}, f32[144,128]{1,0:T(8,128)S(1)}, u32[]{:S(2)}, u32[]{:S(2)}) collective-permute-start(f32[144,128]{1,0:T(8,128)S(1)} %add.23.own_ref), channel_id=1, source_target_pairs={{0,2},{2,0},{4,6},{6,4},{8,10},{10,8},{12,14},{14,12},{16,18},{18,... | collective-permute-start | bytes 221192 | tf_op jit(solution)/shard_map/ppermute | solution.py:415

commit v6 on v5

--- a/solution.py
+++ b/solution.py
@@ -18,7 +18,7 @@
 RQ = LANE // OA
 NQ = OA // RQ
 LIVE_AT = 64
-CHUNKS = (4, 4)
+CHUNKS = (5, 3)
 BF = jnp.bfloat16
 F4 = jnp.float32
 
@@ -225,10 +225,35 @@
     selected(y, y_ref)
 
 
+def spread_rows(value, own_count):
+    return jnp.concatenate(
+        [jnp.broadcast_to(value[p : p + 1], (own_count, value.shape[1])) for p in range(BLK)],
+        axis=0,
+    )
+
+
+def early_kernel(meta_ref, *refs):
+    parts, (base_ref, weight_ref) = refs[:-2], refs[-2:]
+    rows = base_ref.shape[0]
+    own_count = rows // BLK
+    row, col = iota((rows, rows), 0), iota((rows, rows), 1)
+    same = (mod(row, own_count) == mod(col, own_count)).astype(F4)
+    spread_row, spread_col = iota((LANE, rows), 0), iota((LANE, rows), 1)
+    meta = meta_ref[...]
+    for t in range(REACH + 1):
+        pick = onehot(spread_row == (REACH + t) * BLK + div(spread_col, own_count))
+        weight = (spread_rows(mm(meta, pick), own_count) * same).astype(BF)
+        if t:
+            weight_ref[(t - 1) * rows : t * rows] = weight
+        else:
+            base_ref[...] = mm(weight, jnp.concatenate([p[...] for p in parts], axis=0))
+
+
 def window_kernel(lanes, sigma_scale, chi_scale, place_ref, *refs):
-    (pairs_ref, meta0, meta1a, meta1b, meta2, tile1a, tile1b, tile2, cols_ref) = refs[:9]
+    (pairs_ref, meta1a, meta1b, meta2, tile1a, tile1b, tile2, cols_ref) = refs[:8]
+    base_ref, weight_ref = refs[8:10]
     keep_ref, send_ref, near_ref, mixed_ref, other_ref = refs[-5:]
-    own, tile0 = refs[9 : 9 + 4 * len(CHUNKS)], refs[9 + 4 * len(CHUNKS) : -5]
+    own, tile0 = refs[10 : 10 + 4 * len(CHUNKS)], refs[10 + 4 * len(CHUNKS) : -5]
     matrices = [ref[p] for ref in own[::4] for p in range(ref.shape[0])]
     rights = [ref[p] for ref in own[1::4] for p in range(ref.shape[0])]
     z = jnp.concatenate([ref[...] for ref in own[2::4]], axis=0)
@@ -237,32 +262,24 @@
     pair_count = pairs_ref.shape[1] // own_count
     rows = BLK * own_count
     block, pair_at = place_ref[0], place_ref[1]
-    row = iota((rows, rows), 0)
-    col = iota((rows, rows), 1)
+    metas = [None, jnp.where((block & 1) == 0, meta1a[...], meta1b[...]), meta2[...]]
+    spread = onehot(iota((LANE, rows), 0) == LIVE_AT + mod(iota((LANE, rows), 1), own_count))
+    lives = [None] + [mm(m, spread)[0:1, :] for m in metas[1:]]
+    row, col = iota((rows, rows), 0), iota((rows, rows), 1)
     same = (mod(row, own_count) == mod(col, own_count)).astype(F4)
-    spread_row, spread_col = iota((LANE, rows), 0), iota((LANE, rows), 1)
-    spread = onehot(spread_row == LIVE_AT + mod(spread_col, own_count))
-    metas = [meta0[...], jnp.where((block & 1) == 0, meta1a[...], meta1b[...]), meta2[...]]
-    masks = [same * mm(m, spread)[0:1, :] for m in metas]
+    masks = [same] + [same * live for live in lives[1:]]
     near_ref[...] = jnp.where((block & 1) == 0, tile1a[...], tile1b[...])
     tiles = [jnp.concatenate([t[...] for t in tile0], axis=0), near_ref, tile2]
-
-    def spread_rows(value):
-        return jnp.concatenate(
-            [jnp.broadcast_to(value[p : p + 1], (own_count, rows)) for p in range(BLK)], axis=0
-        )
-
-    mixed = jnp.zeros((rows, PAIR), F4)
-    for t in range(REACH + 1):
-        pick = onehot(spread_row == (REACH + t) * BLK + div(spread_col, own_count))
-        weight = spread_rows(mm(metas[0], pick)) * masks[t]
+    mixed = base_ref[...]
+    for t in range(1, REACH + 1):
+        weight = weight_ref[(t - 1) * rows : t * rows].astype(F4) * lives[t]
         mixed = mixed + mm(weight.astype(BF), tiles[t][...])
     mixed_ref[...] = mixed.astype(BF)
     other = jnp.zeros((rows, PAIR), F4)
     unspread = onehot(iota((BLK, rows), 0) == div(iota((BLK, rows), 1), own_count))
     for t in range(1, REACH + 1):
         pick = onehot(iota((BLK, LANE), 1) == (REACH - t) * BLK + iota((BLK, LANE), 0))
-        weight = spread_rows(mm(mm_nt(pick, metas[t]).astype(BF), unspread)) * masks[t]
+        weight = spread_rows(mm(mm_nt(pick, metas[t]).astype(BF), unspread), own_count) * masks[t]
         other = other + mm(weight.astype(BF), tiles[t][...])
     other_ref[...] = other.astype(BF)
     selects = [
@@ -469,6 +486,15 @@
         pieces.append([part] + [turned(part, s) for s in range(1, pair_count)])
     meta_even = flipped(meta, 1)
     meta_far = shifted(meta, -2)
+    early = call(
+        early_kernel,
+        [
+            shape((rows, PAIR), F4),
+            shape((REACH * rows, rows), BF),
+        ],
+        meta,
+        *parts,
+    )
     near_odd = flipped(far, 1)
     meta_odd = flipped(meta_far, 1)
     turn = pair_count == 2
@@ -516,7 +542,6 @@
         [message, message],
         place,
         pairs,
-        meta,
         meta_even,
         meta_odd,
         meta_far,
@@ -524,6 +549,7 @@
         near_odd.reshape(rows, PAIR),
         far.reshape(rows, PAIR),
         cols,
+        *early,
         *own,
         *parts,
         scratch=[pltpu.VMEM((rows, PAIR), BF)] * 3,

time: 63.3 us -> 64.5 us (1.019)
  waiting for transfers between devices: 33.2 us -> 34.3 us
    ppermute x2, waiting for transfers between devices: 2.22 us -> 4.5 us  [turned(): lax.ppermute(value, 'pair', [(s, (s - steps) % pair_count) for s in range...]
    pallas_call x6 -> x7, Pallas kernels: 14.2 us -> 14 us  [call(): pl.pallas_call(body, out_shape=outs, in_specs=[pl.BlockSpec(memory_space=...]
where the time goes in v6:
time: 64.5 us; the launch traced here: 64 us
  waiting for transfers between devices  34.3 us (53%)
  starting transfers between devices  14.8 us (23%)
  Pallas kernels  14 us (22%)
  between operations  0.77 us (1%)
    ppermute x2, waiting for transfers between devices, shifted(): lax.ppermute(value, 'aux', [(s, s + steps) for s in range(aux_count) if 0...  19.4 us
    pallas_call x7, Pallas kernels, call(): pl.pallas_call(body, out_shape=outs, in_specs=[pl.BlockSpec(memory_space=...  14 us
    ppermute x4, waiting for transfers between devices, joint(): lax.ppermute(value, ('aux', 'pair'), [(s * pair_count + p, t * pair_count...  8.48 us
    ppermute x4, starting transfers between devices, joint(): lax.ppermute(value, ('aux', 'pair'), [(s * pair_count + p, t * pair_count...  8.37 us
    ppermute x2, waiting for transfers between devices, turned(): lax.ppermute(value, 'pair', [(s, (s - steps) % pair_count) for s in range...  4.5 us
    ppermute x2, starting transfers between devices, shifted(): lax.ppermute(value, 'aux', [(s, s + steps) for s in range(aux_count) if 0...  2.57 us
    ppermute x2, starting transfers between devices, turned(): lax.ppermute(value, 'pair', [(s, (s - steps) % pair_count) for s in range...  2.16 us
    ppermute x6, waiting for transfers between devices, flipped(): return lax.ppermute(value, 'aux', [(s, s ^ mask) for s in range(aux_count)])  1.93 us
  transfers between devices with their start and end apart: 14, of which 9 were waited for; matrix products, arithmetic and copies ran while one was open for 0% of the time, Pallas kernels for 12%

profile of v6, /device:TPU:0, one launch (start us, length us, event | category | flops | bytes accessed | tf_op | source)
XLA Modules:
  0.0 64.0 jit_solution(5472314828658367623)
XLA Ops:
  0.6 1.3 %collective-permute-start.4 = (bf16[8,32,1024]{2,1,0:T(8,128)(2,1)}, bf16[8,32,1024]{2,1,0:T(8,128)(2,1)S(1)}, u32[]{:S(2)}, u32[]{:S(2)}) collective-permute-start(bf16[8,32,1024]{2,1,0:T(8,128)(2,1)} %whole_hbm.1), channel_id=1, source_target_pairs={{4,0},{6,2},{8,4},{10,6},{12,8},{14,10},{16,12},{18,14},{20,16},{2... | collective-permute-start | bytes 1572872 | tf_op jit(solution)/shard_map/ppermute | solution.py:416
  1.9 0.6 collective-permute-start.3
  2.5 15.1 %collective-permute-done.4 = bf16[8,32,1024]{2,1,0:T(8,128)(2,1)S(1)} collective-permute-done((bf16[8,32,1024]{2,1,0:T(8,128)(2,1)}, bf16[8,32,1024]{2,1,0:T(8,128)(2,1)S(1)}, u32[]{:S(2)}, u32[]{:S(2)}) %collective-permute-start.4) | collective-permute-done | bytes 524320 | tf_op jit(solution)/shard_map/ppermute | solution.py:416
  17.6 0.0 collective-permute-start.5
  17.6 1.1 %shard_map.78.refs_0_.refs_2_.refs_19_ = bf16[160,1024]{1,0:T(8,128)(2,1)S(1)} custom-call(s32[1,32]{1,0:T(1,128)} %live_hbm.1, bf16[8,32,1024]{2,1,0:T(8,128)(2,1)} %whole_hbm.1), custom_call_target="tpu_custom_call" | custom-call | flops 100000000 | bytes 1000000 | tf_op jit(solution)/shard_map/pallas_call | solution.py:396
  18.8 1.8 %collective-permute-start.6 = (bf16[160,1024]{1,0:T(8,128)(2,1)S(1)}, bf16[160,1024]{1,0:T(8,128)(2,1)S(1)}, u32[]{:S(2)}, u32[]{:S(2)}) collective-permute-start(bf16[160,1024]{1,0:T(8,128)(2,1)S(1)} %shard_map.78.refs_0_.refs_2_.refs_19_), channel_id=1, source_target_pairs={{0,1},{1,0},{2,3},{3,2},{4,5},{5,4},{6,7},{7,6},{8,9},{9,8},{10,11... | collective-permute-start | bytes 983048 | tf_op jit(solution)/shard_map/ppermute | solution.py:427
  20.6 1.7 %shard_map.77 = (s32[1,64]{1,0:T(1,128)S(1)}, bf16[256,256]{1,0:T(8,128)(2,1)S(1)}, bf16[8,128]{1,0:T(8,128)(2,1)S(1)}, bf16[512,256]{1,0:T(8,128)(2,1)S(1)}, bf...) custom-call(bf16[256,256]{1,0:T(8,128)(2,1)} %refs_0_.1, ...), custom_call_target="tpu_custom_call" | custom-call | flops 100000000 | bytes 1000000 | tf_op jit(solution)/shard_map/pallas_call | solution.py:396
  22.3 0.3 collective-permute-start.7
  22.6 1.3 %collective-permute-start.1 = (bf16[8,128]{1,0:T(8,128)(2,1)S(1)}, bf16[8,128]{1,0:T(8,128)(2,1)S(1)}, u32[]{:S(2)}, u32[]{:S(2)}) collective-permute-start(bf16[8,128]{1,0:T(8,128)(2,1)S(1)} %get-tuple-element.22.meta_ref), channel_id=1, source_target_pairs={{4,0},{6,2},{8,4},{10,6},{12,8},{14,10},{16,12},{18,14},{20,16},{2... | collective-permute-start | bytes 6152 | tf_op jit(solution)/shard_map/ppermute | solution.py:416
  23.9 0.1 pad_add_fusion.refs_0_.place_ref
  24.0 0.4 shard_map.79
  24.4 4.3 %collective-permute-done.1.refs_4_ = bf16[8,128]{1,0:T(8,128)(2,1)S(1)} collective-permute-done((bf16[8,128]{1,0:T(8,128)(2,1)S(1)}, bf16[8,128]{1,0:T(8,128)(2,1)S(1)}, u32[]{:S(2)}, u32[]{:S(2)}) %collective-permute-start.1) | collective-permute-done | bytes 2080 | tf_op jit(solution)/shard_map/ppermute | solution.py:416
  28.7 0.0 collective-permute-start
  28.7 4.5 %collective-permute-done.7.refs_3_ = bf16[96,1024]{1,0:T(8,128)(2,1)S(1)} collective-permute-done((bf16[96,1024]{1,0:T(8,128)(2,1)S(1)}, bf16[96,1024]{1,0:T(8,128)(2,1)S(1)}, u32[]{:S(2)}, u32[]{:S(2)}) %collective-permute-start.7) | collective-permute-done | bytes 196640 | tf_op jit(solution)/shard_map/ppermute | solution.py:427
  33.2 0.0 collective-permute-start.2
  33.2 2.1 %shard_map.81 = (bf16[3,256,256]{2,1,0:T(8,128)(2,1)S(1)}, bf16[3,256,256]{2,1,0:T(8,128)(2,1)S(1)}, bf16[96,1024]{1,0:T(8,128)(2,1)S(1)}, bf16[96,1024]{1,0:T(8,128)(2,1)S(1)}) custom-call(s32[3]{0:T(128)S(1)} %pad_add_fusion.refs_0_.place_ref, s32[1,64]{1,0:T(1,128)S(1)} %get-tuple-element.21.refs_1_, ...), custom_call_target="tpu_custom_call" | custom-call | flops 100000000 | bytes 1000000 | tf_op jit(solution)/shard_map/pallas_call | solution.py:396
  35.3 0.0 collective-permute-done.6.refs_3_
  35.3 2.5 %shard_map.80 = (bf16[5,256,256]{2,1,0:T(8,128)(2,1)S(1)}, bf16[5,256,256]{2,1,0:T(8,128)(2,1)S(1)}, bf16[160,1024]{1,0:T(8,128)(2,1)S(1)}, bf16[160,1024]{1,0:T(8,128)(2,1)S(1)}) custom-call(s32[3]{0:T(128)S(1)} %pad_add_fusion.refs_0_.place_ref, s32[1,64]{1,0:T(1,128)S(1)} %get-tuple-element.21.refs_1_, ...), custom_call_target="tpu_custom_call" | custom-call | flops 100000000 | bytes 1000000 | tf_op jit(solution)/shard_map/pallas_call | solution.py:396
  37.8 0.0 collective-permute-done.refs_2_
  37.8 0.0 collective-permute-done.2.refs_3_
  37.8 0.0 collective-permute-done.3
  37.9 0.0 collective-permute-done.5
  37.9 4.8 %shard_map.82 = (f32[2,144,128]{2,1,0:T(8,128)S(1)}, f32[2,144,128]{2,1,0:T(8,128)S(1)}) custom-call(s32[3]{0:T(128)S(1)} %pad_add_fusion.refs_0_.place_ref, s32[1,64]{1,0:T(1,128)S(1)} %get-tuple-element.21.refs_1_, bf16[8,128]{1,0:T(8,128)(2,1)S(1)} %collective-permute-done.refs_2_, bf16[8,128]{1,0:T(8,128)(2,1)S(1)} %collective-permute-done.2.refs_3_, ...), custom_call_target="tpu_custom_call" | custom-call | flops 100000000 | bytes 1000000 | tf_op jit(solution)/shard_map/pallas_call | solution.py:396
  42.7 0.6 collective-permute-start.8
  43.3 1.0 %collective-permute-done.8 = f32[2,144,128]{2,1,0:T(8,128)S(1)} collective-permute-done((f32[2,144,128]{2,1,0:T(8,128)S(1)}, f32[2,144,128]{2,1,0:T(8,128)S(1)}, u32[]{:S(2)}, u32[]{:S(2)}) %collective-permute-start.8) | collective-permute-done | bytes 147488 | tf_op jit(solution)/shard_map/ppermute | solution.py:432
  44.3 1.8 %collective-permute-start.9 = (bf16[144,128]{1,0:T(8,128)(2,1)S(1)}, bf16[144,128]{1,0:T(8,128)(2,1)S(1)}, u32[]{:S(2)}, u32[]{:S(2)}) collective-permute-start(bf16[144,128]{1,0:T(8,128)(2,1)S(1)} %fusion.1), channel_id=1, source_target_pairs={{0,3},{1,2},{2,1},{3,0},{4,7},{5,6},{6,5},{7,4},{8,11},{9,10},{10,... | collective-permute-start | bytes 110600 | tf_op jit(solution)/shard_map/ppermute | solution.py:505
  46.1 1.7 %collective-permute-done.9 = bf16[144,128]{1,0:T(8,128)(2,1)S(1)} collective-permute-done((bf16[144,128]{1,0:T(8,128)(2,1)S(1)}, bf16[144,128]{1,0:T(8,128)(2,1)S(1)}, u32[]{:S(2)}, u32[]{:S(2)}) %collective-permute-start.9) | collective-permute-done | bytes 36896 | tf_op jit(solution)/shard_map/ppermute | solution.py:505
  47.8 2.6 %collective-permute-start.10 = (f32[144,128]{1,0:T(8,128)S(1)}, f32[144,128]{1,0:T(8,128)S(1)}, u32[]{:S(2)}, u32[]{:S(2)}) collective-permute-start(f32[144,128]{1,0:T(8,128)S(1)} %fusion), channel_id=1, source_target_pairs={{0,6},{1,11},{2,8},{3,5},{4,14},{5,3},{6,0},{7,13},{8,2},{9,15},{1... | collective-permute-start | bytes 221192 | tf_op jit(solution)/shard_map/ppermute | solution.py:505
  50.5 2.0 %collective-permute-done.10 = f32[144,128]{1,0:T(8,128)S(1)} collective-permute-done((f32[144,128]{1,0:T(8,128)S(1)}, f32[144,128]{1,0:T(8,128)S(1)}, u32[]{:S(2)}, u32[]{:S(2)}) %collective-permute-start.10) | collective-permute-done | bytes 73760 | tf_op jit(solution)/shard_map/ppermute | solution.py:505
  52.5 1.4 %collective-permute-start.11 = (f32[144,128]{1,0:T(8,128)S(1)}, f32[144,128]{1,0:T(8,128)S(1)}, u32[]{:S(2)}, u32[]{:S(2)}) collective-permute-start(f32[144,128]{1,0:T(8,128)S(1)} %add.21), channel_id=1, source_target_pairs={{0,10},{1,19},{2,16},{3,9},{4,22},{5,15},{6,12},{7,21},{8,26},{9,3... | collective-permute-start | bytes 221192 | tf_op jit(solution)/shard_map/ppermute | solution.py:505
  53.9 2.6 %collective-permute-done.11 = f32[144,128]{1,0:T(8,128)S(1)} collective-permute-done((f32[144,128]{1,0:T(8,128)S(1)}, f32[144,128]{1,0:T(8,128)S(1)}, u32[]{:S(2)}, u32[]{:S(2)}) %collective-permute-start.11) | collective-permute-done | bytes 73760 | tf_op jit(solution)/shard_map/ppermute | solution.py:505
  56.5 2.6 %collective-permute-start.12 = (f32[144,128]{1,0:T(8,128)S(1)}, f32[144,128]{1,0:T(8,128)S(1)}, u32[]{:S(2)}, u32[]{:S(2)}) collective-permute-start(f32[144,128]{1,0:T(8,128)S(1)} %add.22), channel_id=1, source_target_pairs={{0,18},{1,7},{2,4},{3,17},{4,2},{5,23},{6,20},{7,1},{8,14},{9,27},... | collective-permute-start | bytes 221192 | tf_op jit(solution)/shard_map/ppermute | solution.py:505
  59.1 2.2 %collective-permute-done.12 = f32[144,128]{1,0:T(8,128)S(1)} collective-permute-done((f32[144,128]{1,0:T(8,128)S(1)}, f32[144,128]{1,0:T(8,128)S(1)}, u32[]{:S(2)}, u32[]{:S(2)}) %collective-permute-start.12) | collective-permute-done | bytes 73760 | tf_op jit(solution)/shard_map/ppermute | solution.py:505
  61.3 0.5 collective-permute-start.13
  61.8 0.9 %collective-permute-done.13.other_ref = f32[144,128]{1,0:T(8,128)S(1)} collective-permute-done((f32[144,128]{1,0:T(8,128)S(1)}, f32[144,128]{1,0:T(8,128)S(1)}, u32[]{:S(2)}, u32[]{:S(2)}) %collective-permute-start.13) | collective-permute-done | bytes 73760 | tf_op jit(solution)/shard_map/ppermute | solution.py:432
  62.7 1.3 %shard_map.83 = (f32[8,20]{1,0:T(8,128)}, f32[32,1024]{1,0:T(8,128)}) custom-call(s32[3]{0:T(128)S(1)} %pad_add_fusion.refs_0_.place_ref, f32[144,128]{1,0:T(8,128)S(1)} %add.23.own_ref, f32[144,128]{1,0:T(8,128)S(1)} %collective-permute-done.13.other_ref), custom_call_target="tpu_custom_call" | custom-call | flops 100000000 | bytes 1000000 | tf_op jit(solution)/shard_map/pallas_call | solution.py:396
  (6 shorter events, 0.1 us)
Async XLA Ops:
  0.6 17.0 %collective-permute-start.4 = (bf16[8,32,1024]{2,1,0:T(8,128)(2,1)}, bf16[8,32,1024]{2,1,0:T(8,128)(2,1)S(1)}, u32[]{:S(2)}, u32[]{:S(2)}) collective-permute-start(bf16[8,32,1024]{2,1,0:T(8,128)(2,1)} %whole_hbm.1), channel_id=1, source_target_pairs={{4,0},{6,2},{8,4},{10,6},{12,8},{14,10},{16,12},{18,14},{20,16},{2... | collective-permute-start | bytes 1572872 | tf_op jit(solution)/shard_map/ppermute | solution.py:416
  1.9 35.9 %collective-permute-start.3 = (bf16[8,32,1024]{2,1,0:T(8,128)(2,1)}, bf16[8,32,1024]{2,1,0:T(8,128)(2,1)S(1)}, u32[]{:S(2)}, u32[]{:S(2)}) collective-permute-start(bf16[8,32,1024]{2,1,0:T(8,128)(2,1)} %whole_hbm.1), channel_id=1, source_target_pairs={{0,2},{2,0},{4,6},{6,4},{8,10},{10,8},{12,14},{14,12},{16,18},{18,... | collective-permute-start | bytes 1572872 | tf_op jit(solution)/shard_map/ppermute | solution.py:432
  17.6 20.2 %collective-permute-start.5 = (bf16[8,32,1024]{2,1,0:T(8,128)(2,1)S(1)}, bf16[8,32,1024]{2,1,0:T(8,128)(2,1)S(1)}, u32[]{:S(2)}, u32[]{:S(2)}) collective-permute-start(bf16[8,32,1024]{2,1,0:T(8,128)(2,1)S(1)} %collective-permute-done.4), channel_id=1, source_target_pairs={{0,2},{2,0},{4,6},{6,4},{8,10},{10,8},{12,14},{14,12},{16,18},{18,... | collective-permute-start | bytes 1572872 | tf_op jit(solution)/shard_map/ppermute | solution.py:432
  18.8 16.6 %collective-permute-start.6 = (bf16[160,1024]{1,0:T(8,128)(2,1)S(1)}, bf16[160,1024]{1,0:T(8,128)(2,1)S(1)}, u32[]{:S(2)}, u32[]{:S(2)}) collective-permute-start(bf16[160,1024]{1,0:T(8,128)(2,1)S(1)} %shard_map.78.refs_0_.refs_2_.refs_19_), channel_id=1, source_target_pairs={{0,1},{1,0},{2,3},{3,2},{4,5},{5,4},{6,7},{7,6},{8,9},{9,8},{10,11... | collective-permute-start | bytes 983048 | tf_op jit(solution)/shard_map/ppermute | solution.py:427
  22.3 10.9 %collective-permute-start.7 = (bf16[96,1024]{1,0:T(8,128)(2,1)S(1)}, bf16[96,1024]{1,0:T(8,128)(2,1)S(1)}, u32[]{:S(2)}, u32[]{:S(2)}) collective-permute-start(bf16[96,1024]{1,0:T(8,128)(2,1)S(1)} %get-tuple-element.24.refs_1_.refs_2_.refs_20_), channel_id=1, source_target_pairs={{0,1},{1,0},{2,3},{3,2},{4,5},{5,4},{6,7},{7,6},{8,9},{9,8},{10,11... | collective-permute-start | bytes 589832 | tf_op jit(solution)/shard_map/ppermute | solution.py:427
  22.6 6.1 %collective-permute-start.1 = (bf16[8,128]{1,0:T(8,128)(2,1)S(1)}, bf16[8,128]{1,0:T(8,128)(2,1)S(1)}, u32[]{:S(2)}, u32[]{:S(2)}) collective-permute-start(bf16[8,128]{1,0:T(8,128)(2,1)S(1)} %get-tuple-element.22.meta_ref), channel_id=1, source_target_pairs={{4,0},{6,2},{8,4},{10,6},{12,8},{14,10},{16,12},{18,14},{20,16},{2... | collective-permute-start | bytes 6152 | tf_op jit(solution)/shard_map/ppermute | solution.py:416
  28.7 9.2 %collective-permute-start = (bf16[8,128]{1,0:T(8,128)(2,1)S(1)}, bf16[8,128]{1,0:T(8,128)(2,1)S(1)}, u32[]{:S(2)}, u32[]{:S(2)}) collective-permute-start(bf16[8,128]{1,0:T(8,128)(2,1)S(1)} %get-tuple-element.22.meta_ref), channel_id=1, source_target_pairs={{0,2},{2,0},{4,6},{6,4},{8,10},{10,8},{12,14},{14,12},{16,18},{18,... | collective-permute-start | bytes 6152 | tf_op jit(solution)/shard_map/ppermute | solution.py:432
  33.2 4.7 %collective-permute-start.2 = (bf16[8,128]{1,0:T(8,128)(2,1)S(1)}, bf16[8,128]{1,0:T(8,128)(2,1)S(1)}, u32[]{:S(2)}, u32[]{:S(2)}) collective-permute-start(bf16[8,128]{1,0:T(8,128)(2,1)S(1)} %collective-permute-done.1.refs_4_), channel_id=1, source_target_pairs={{0,2},{2,0},{4,6},{6,4},{8,10},{10,8},{12,14},{14,12},{16,18},{18,... | collective-permute-start | bytes 6152 | tf_op jit(solution)/shard_map/ppermute | solution.py:432
  42.7 1.6 %collective-permute-start.8 = (f32[2,144,128]{2,1,0:T(8,128)S(1)}, f32[2,144,128]{2,1,0:T(8,128)S(1)}, u32[]{:S(2)}, u32[]{:S(2)}) collective-permute-start(f32[2,144,128]{2,1,0:T(8,128)S(1)} %get-tuple-element.39), channel_id=1, source_target_pairs={{0,2},{2,0},{4,6},{6,4},{8,10},{10,8},{12,14},{14,12},{16,18},{18,... | collective-permute-start | bytes 442376 | tf_op jit(solution)/shard_map/ppermute | solution.py:432
  44.3 3.4 %collective-permute-start.9 = (bf16[144,128]{1,0:T(8,128)(2,1)S(1)}, bf16[144,128]{1,0:T(8,128)(2,1)S(1)}, u32[]{:S(2)}, u32[]{:S(2)}) collective-permute-start(bf16[144,128]{1,0:T(8,128)(2,1)S(1)} %fusion.1), channel_id=1, source_target_pairs={{0,3},{1,2},{2,1},{3,0},{4,7},{5,6},{6,5},{7,4},{8,11},{9,10},{10,... | collective-permute-start | bytes 110600 | tf_op jit(solution)/shard_map/ppermute | solution.py:505
  47.8 4.7 %collective-permute-start.10 = (f32[144,128]{1,0:T(8,128)S(1)}, f32[144,128]{1,0:T(8,128)S(1)}, u32[]{:S(2)}, u32[]{:S(2)}) collective-permute-start(f32[144,128]{1,0:T(8,128)S(1)} %fusion), channel_id=1, source_target_pairs={{0,6},{1,11},{2,8},{3,5},{4,14},{5,3},{6,0},{7,13},{8,2},{9,15},{1... | collective-permute-start | bytes 221192 | tf_op jit(solution)/shard_map/ppermute | solution.py:505
  52.5 4.0 %collective-permute-start.11 = (f32[144,128]{1,0:T(8,128)S(1)}, f32[144,128]{1,0:T(8,128)S(1)}, u32[]{:S(2)}, u32[]{:S(2)}) collective-permute-start(f32[144,128]{1,0:T(8,128)S(1)} %add.21), channel_id=1, source_target_pairs={{0,10},{1,19},{2,16},{3,9},{4,22},{5,15},{6,12},{7,21},{8,26},{9,3... | collective-permute-start | bytes 221192 | tf_op jit(solution)/shard_map/ppermute | solution.py:505
  56.5 4.7 %collective-permute-start.12 = (f32[144,128]{1,0:T(8,128)S(1)}, f32[144,128]{1,0:T(8,128)S(1)}, u32[]{:S(2)}, u32[]{:S(2)}) collective-permute-start(f32[144,128]{1,0:T(8,128)S(1)} %add.22), channel_id=1, source_target_pairs={{0,18},{1,7},{2,4},{3,17},{4,2},{5,23},{6,20},{7,1},{8,14},{9,27},... | collective-permute-start | bytes 221192 | tf_op jit(solution)/shard_map/ppermute | solution.py:505
  61.3 1.4 %collective-permute-start.13 = (f32[144,128]{1,0:T(8,128)S(1)}, f32[144,128]{1,0:T(8,128)S(1)}, u32[]{:S(2)}, u32[]{:S(2)}) collective-permute-start(f32[144,128]{1,0:T(8,128)S(1)} %add.23.own_ref), channel_id=1, source_target_pairs={{0,2},{2,0},{4,6},{6,4},{8,10},{10,8},{12,14},{14,12},{16,18},{18,... | collective-permute-start | bytes 221192 | tf_op jit(solution)/shard_map/ppermute | solution.py:432
